TPU v7x, 32 devices: a whole 2x2x4 slice. The times are simulated.
32 devices in a mesh: data: 32 (over z, y, x, core).
Axes of the slice: x: 2, y: 2, z: 4, core: 2. Of those that a mesh axis runs over, the one named last changes fastest.
Arguments:
- x_act: bfloat16 [256, 196, 768], P('data')
- y_tgt: bfloat16 [256, 196, 768], P('data')
- w_in: float32 [2, 768, 3072], replicated
- w_out: float32 [2, 3072, 768], replicated
Outputs:
- output 1: float32 [2, 768, 3072], replicated
- output 2: float32 [2, 3072, 768], replicated
- output 3: float32 [], replicated
All inputs are finite; a program needn't handle non-finite values.
Results may differ from a plain program's by a relative error of at most 0.001.
Values are sent between devices in bfloat16 or wider.
A program may use at most 1 GiB of HBM per device.

v0:
```python
import math
import jax
import jax.numpy as jnp
from jax import lax
from jax.sharding import PartitionSpec as P

RHO_FRAC = 0.1
LEARN_RATE = 1.0
MICRO_STEPS = 2


def gelu_tanh(z_val):
    return jax.nn.gelu(z_val, approximate=True)


def layer_forward(h_act, wi_cast, wo_cast):
    z_pre = jnp.einsum("bsd,df->bsf", h_act, wi_cast, preferred_element_type=jnp.float32).astype(jnp.bfloat16)
    gelu_out = gelu_tanh(z_pre.astype(jnp.float32)).astype(jnp.bfloat16)
    u_out = jnp.einsum("bsf,fd->bsd", gelu_out, wo_cast, preferred_element_type=jnp.float32)
    return (h_act.astype(jnp.float32) + u_out).astype(jnp.bfloat16), z_pre


def micro_grads(x_mb, y_mb, wi_list, wo_list):
    n_layers = len(wi_list)
    h_list = [x_mb]
    z_list = []
    for layer_idx in range(n_layers):
        h_next, z_pre = layer_forward(h_list[-1], wi_list[layer_idx], wo_list[layer_idx])
        h_list.append(h_next)
        z_list.append(z_pre)
    out_err = h_list[-1].astype(jnp.float32) - y_mb.astype(jnp.float32)
    sq_sum = jnp.sum(out_err * out_err)
    back_grad = out_err.astype(jnp.bfloat16)
    sums_in = [None] * n_layers
    sums_out = [None] * n_layers
    for layer_idx in reversed(range(n_layers)):
        gelu_out, gelu_vjp = jax.vjp(gelu_tanh, z_list[layer_idx].astype(jnp.float32))
        sums_out[layer_idx] = jnp.einsum("bsf,bsd->fd", gelu_out.astype(jnp.bfloat16), back_grad, preferred_element_type=jnp.float32)
        d_act = jnp.einsum("bsd,fd->bsf", back_grad, wo_list[layer_idx], preferred_element_type=jnp.float32)
        d_pre = gelu_vjp(d_act)[0].astype(jnp.bfloat16)
        sums_in[layer_idx] = jnp.einsum("bsd,bsf->df", h_list[layer_idx], d_pre, preferred_element_type=jnp.float32)
        if layer_idx > 0:
            back_in = jnp.einsum("bsf,df->bsd", d_pre, wi_list[layer_idx], preferred_element_type=jnp.float32)
            back_grad = (back_grad.astype(jnp.float32) + back_in).astype(jnp.bfloat16)
    return sums_in, sums_out, sq_sum


def grad_pass(x_loc, y_loc, wi_list, wo_list):
    mb_rows = x_loc.shape[0] // MICRO_STEPS
    sums_in, sums_out, sq_sum = micro_grads(x_loc[:mb_rows], y_loc[:mb_rows], wi_list, wo_list)
    for micro_idx in range(1, MICRO_STEPS):
        row_lo = micro_idx * mb_rows
        more_in, more_out, more_sq = micro_grads(x_loc[row_lo:row_lo + mb_rows], y_loc[row_lo:row_lo + mb_rows], wi_list, wo_list)
        sums_in = [left_sum + right_sum for left_sum, right_sum in zip(sums_in, more_in)]
        sums_out = [left_sum + right_sum for left_sum, right_sum in zip(sums_out, more_out)]
        sq_sum = sq_sum + more_sq
    return sums_in, sums_out, sq_sum


def solution(mesh):
    n_dev = mesh.shape["data"]

    def local_step(x_loc, y_loc, w_in, w_out):
        n_layers, d_model, d_ff = w_in.shape
        tok_scale = 1.0 / (x_loc.shape[0] * n_dev * x_loc.shape[1] * d_model)
        rho_val = RHO_FRAC * math.sqrt(n_layers * (d_model + d_ff))
        wi_cast = [w_in[layer_idx].astype(jnp.bfloat16) for layer_idx in range(n_layers)]
        wo_cast = [w_out[layer_idx].astype(jnp.bfloat16) for layer_idx in range(n_layers)]
        sums_in, sums_out, _ = grad_pass(x_loc, y_loc, wi_cast, wo_cast)
        grad_in = [lax.psum(part_sum, "data") * tok_scale for part_sum in sums_in]
        grad_out = [lax.psum(part_sum, "data") * tok_scale for part_sum in sums_out]
        sq_norm = sum(jnp.sum(grad_mat * grad_mat) for grad_mat in grad_in + grad_out)
        perturb_coef = rho_val / jnp.sqrt(sq_norm)
        pi_cast = [(w_in[layer_idx] + perturb_coef * grad_in[layer_idx]).astype(jnp.bfloat16) for layer_idx in range(n_layers)]
        po_cast = [(w_out[layer_idx] + perturb_coef * grad_out[layer_idx]).astype(jnp.bfloat16) for layer_idx in range(n_layers)]
        second_in, second_out, second_sq = grad_pass(x_loc, y_loc, pi_cast, po_cast)
        total_in = [lax.psum(part_sum, "data") for part_sum in second_in]
        total_out = [lax.psum(part_sum, "data") for part_sum in second_out]
        total_sq = lax.psum(second_sq, "data")
        new_in = jnp.stack([w_in[layer_idx] - LEARN_RATE * (total_in[layer_idx] * tok_scale) for layer_idx in range(n_layers)])
        new_out = jnp.stack([w_out[layer_idx] - LEARN_RATE * (total_out[layer_idx] * tok_scale) for layer_idx in range(n_layers)])
        pert_loss = 0.5 * (total_sq * tok_scale)
        return new_in, new_out, pert_loss

    return jax.shard_map(local_step, mesh=mesh, in_specs=(P("data"), P("data"), P(), P()), out_specs=(P(), P(), P()), check_vma=False)
```

profile of v0, /device:TPU:0, one launch (start us, length us, event | category | flops | bytes accessed | tf_op | source)
XLA Modules:
  0.0 1646.6 jit_solution(7179093713131952973)
XLA Ops:
  11.6 5.2 fusion.188
  16.8 9.3 fusion.113
  26.2 5.9 copy-done
  32.0 7.0 convolution_convert_fusion.5
  39.0 9.9 fusion.122
  49.0 7.2 convolution_convert_fusion.4
  56.2 9.3 fusion.124
  66.6 12.1 fusion.34
  78.7 6.9 add_convert_fusion.6
  85.6 10.9 fusion.194
  96.5 9.7 fusion.178
  106.2 9.7 fusion.181
  115.9 17.1 %fusion.102 = f32[3072,768,1]{0,1,2:T(8,128)} fusion(bf16[4,196,3072]{2,1,0:T(8,128)(2,1)} %convolution_convert_fusion.5, bf16[4,196,768]{2,1,0:T(8,128)(2,1)} %copy-done.19, bf16[3072,768,1]{1,0,2:T(8,128)(2,1)} %copy-done.5, bf16[4,196,768]{2,0,1:T(4,128)(2,1)S(1)} %copy-done.10), kind=kOutput, calls=%fused_computation.172 | convolution fusion | flops 7449329664 | bytes 21381120 | tf_op jit(solution)/shard_map/bsd,bsf->df/dot_general | solution.py:41
  133.1 9.6 convolution_convert_fusion.3
  142.8 10.4 fusion.125
  153.2 5.7 convolution_convert_fusion.2
  158.9 9.0 fusion.127
  167.9 12.1 fusion.28
  185.1 10.2 bitcast_add_fusion.6
  195.3 12.5 bitcast_add_fusion.4
  207.9 10.0 bitcast_add_fusion.5
  217.8 17.1 %fusion.81 = f32[768,3072]{1,0:T(8,128)} fusion(f32[3072,768,1]{0,1,2:T(8,128)} %fusion.102, bf16[4,196,3072]{2,1,0:T(8,128)(2,1)} %convolution_convert_fusion.3, bf16[4,196,768]{2,1,0:T(8,128)(2,1)S(1)} %copy-done.16, bf16[3072,768,1]{1,0,2:T(8,128)(2,1)} %copy-done.5, bf16[4,196,768]{2,0,1:T(4,128)(2,1)S(1)} %copy-done.8), kind=kOutput, calls=%fused_computation.129 | convolution fusion | flops 7451688960 | bytes 30818304 | tf_op jit(solution)/shard_map/bsd,bsf->df/dot_general | solution.py:41
  235.0 550.9 %all-reduce.7.cloned.1.call-done = (f32[3072,768]{1,0:T(8,128)}, f32[768,3072]{1,0:T(8,128)}, f32[768,3072]{1,0:T(8,128)}, f32[3072,768]{1,0:T(8,128)}) async-done(((f32[3072,768]{1,0:T(8,128)}, f32[768,3072]{1,0:T(8,128)}, f32[768,3072]{1,0:T(8,128)}, f32[3072,768]{1,0:T(8,128)}), (f32[3072,768]{1,0:T(8,128)}, f32[768,3072]{1,0:T(8,128)}, f32[768,3072]{1,0:T(8,128)}, ...) | async-done | bytes 37748752 | tf_op jit(solution)/shard_map/psum | solution.py:71
  785.9 9.4 multiply_reduce_fusion
  795.3 9.5 multiply_reduce_fusion.2
  807.4 16.4 fusion.114
  823.8 14.2 fusion.116
  838.0 9.7 convolution_convert_fusion.6
  852.2 6.2 fusion.123
  862.8 7.2 multiply_reduce_fusion.5
  870.1 10.3 fusion.25
  880.4 10.3 fusion.175
  895.8 7.6 fusion.195
  903.4 17.0 %fusion.104 = f32[3072,768,1]{0,1,2:T(8,128)} fusion(bf16[3072,4,196]{0,2,1:T(8,128)(2,1)} %copy-done.22, bf16[4,196,768]{2,1,0:T(8,128)(2,1)} %add_convert_fusion.2, bf16[3072,768,1]{1,0,2:T(8,128)(2,1)} %copy-done.1, bf16[4,196,768]{2,0,1:T(4,128)(2,1)S(1)} %copy-done.11), kind=kOutput, calls=%fused_computation.173 | convolution fusion | flops 7449329664 | bytes 21381120 | tf_op jit(solution)/shard_map/bsd,bsf->df/dot_general | solution.py:41
  920.4 12.2 fusion.172
  932.6 10.1 fusion.126
  947.0 7.5 multiply_reduce_fusion.4
  954.4 10.2 fusion.22
  968.7 12.5 bitcast_add_fusion
  981.3 7.8 bitcast_add_fusion.2
  989.0 17.1 %fusion.80 = f32[768,3072]{1,0:T(8,128)} fusion(f32[3072,768,1]{0,1,2:T(8,128)} %fusion.104, bf16[3072,4,196]{0,2,1:T(8,128)(2,1)} %convolution_convert_fusion.6, bf16[4,196,768]{2,1,0:T(8,128)(2,1)S(1)} %add_convert_fusion, bf16[3072,768,1]{1,0,2:T(8,128)(2,1)} %copy-done.1, bf16[4,196,768]{2,0,1:T(4,128)(2,1)S(1)} %copy-done.8), kind=kOutput, calls=%fused_computation.124 | convolution fusion | flops 7451688960 | bytes 30818304 | tf_op jit(solution)/shard_map/bsd,bsf->df/dot_general | solution.py:41
  1006.2 12.7 bitcast_add_fusion.1
  1020.3 41.7 %psum.71 = f32[]{:T(128)} all-reduce(f32[]{:T(128)S(6)} %add.225), channel_id=1, replica_groups=mesh['data'=32] {'data'}, use_global_device_ids=true, to_apply=%region_14.0 | all-reduce | flops 1 | bytes 8 | tf_op jit(solution)/shard_map/psum | solution.py:79
  1062.6 505.6 %all-reduce.5.cloned.1.call-done = (f32[768,3072]{1,0:T(8,128)}, f32[768,3072]{1,0:T(8,128)}, f32[3072,768]{1,0:T(8,128)}, f32[3072,768]{1,0:T(8,128)}) async-done(((f32[768,3072]{1,0:T(8,128)}, f32[768,3072]{1,0:T(8,128)}, f32[3072,768]{1,0:T(8,128)}, f32[3072,768]{1,0:T(8,128)}), (f32[768,3072]{1,0:T(8,128)}, f32[768,3072]{1,0:T(8,128)}, f32[3072,768]{1,0:T(8,128)}, ...) | async-done | bytes 37748752 | tf_op jit(solution)/shard_map/psum | solution.py:77
  1568.2 21.1 %fusion.89 = (f32[1,768,3072]{2,1,0:T(8,128)}, f32[1,768,3072]{2,1,0:T(8,128)}) fusion(f32[768,3072]{1,0:T(8,128)} %get-tuple-element.4, f32[2,768,3072]{2,1,0:T(8,128)} %param.6, f32[768,3072]{1,0:T(8,128)} %get-tuple-element.3), kind=kLoop, calls=%fused_computation.149 | loop fusion | flops 9437184 | bytes 56623104 | tf_op jit(solution)/shard_map/stack | solution.py:80
  1589.3 14.9 pad_maximum_fusion
  1607.7 15.8 fusion.87
  1623.5 14.7 pad_maximum_fusion.1
  (124 shorter events, 36.5 us)
Async XLA Ops:
  7.2 778.7 %all-reduce.7.cloned.1.call-start = ((), (), s32[]{:S(2)}) async-start(), calls=%async_computation.1 | async-start | bytes 75497472 | tf_op jit(solution)/shard_map/psum | solution.py:71
  11.6 121.5 %copy-start.7 = (bf16[4,196,768]{2,0,1:T(4,128)(2,1)}, bf16[4,196,768]{2,0,1:T(4,128)(2,1)S(1)}, u32[]{:S(2)}) copy-start(bf16[4,196,768]{2,0,1:T(4,128)(2,1)S(1)} %get-tuple-element.23) | copy-start | bytes 3612676
  16.8 15.2 copy-start
  26.2 12.9 copy-start.5
  85.6 20.7 %copy-start.19 = (bf16[4,196,768]{2,1,0:T(8,128)(2,1)}, bf16[4,196,768]{2,1,0:T(8,128)(2,1)S(1)}, u32[]{:S(2)}) copy-start(bf16[4,196,768]{2,1,0:T(8,128)(2,1)S(1)} %add_convert_fusion.6) | copy-start | bytes 3612676
  85.6 11.0 copy-start.15
  85.6 10.9 copy-start.21
  85.6 20.6 %slice-start.24 = ((s8[4915200]{0:T(1024)(128)(4,1)}), s8[4194304]{0:T(1024)(128)(4,1)S(1)}, s32[]{:S(2)}) async-start(s8[4915200]{0:T(1024)(128)(4,1)} %bitcast.230), calls=%async_computation.26 | async-start | bytes 8388608
  96.5 9.7 slice-start.25
  106.2 9.7 copy-start.10
  133.1 20.1 %slice-start.5 = ((s8[18874368]{0:T(1024)(128)(4,1)}), s8[4194304]{0:T(1024)(128)(4,1)S(1)}, s32[]{:S(2)}) async-start(s8[18874368]{0:T(1024)(128)(4,1)} %bitcast.216), calls=%async_computation.7 | async-start | bytes 8388608
  133.1 20.1 %slice-start.6 = ((s8[18874368]{0:T(1024)(128)(4,1)}), s8[4194304]{0:T(1024)(128)(4,1)S(1)}, s32[]{:S(2)}) async-start(s8[18874368]{0:T(1024)(128)(4,1)} %bitcast.216), calls=%async_computation.8 | async-start | bytes 8388608
  133.1 25.8 %slice-start.20 = ((s8[4718592]{0:T(1024)(128)(4,1)}), s8[4194304]{0:T(1024)(128)(4,1)S(1)}, s32[]{:S(2)}) async-start(s8[4718592]{0:T(1024)(128)(4,1)} %bitcast.226), calls=%async_computation.22 | async-start | bytes 8388608
  142.7 10.4 slice-start.7
  142.7 10.4 slice-start.8
  142.7 10.4 slice-start.9
  142.7 16.1 slice-start.21
  167.9 12.1 copy-start.17
  185.0 10.3 copy-start.14
  185.0 10.3 copy-start.18
  185.0 22.8 %slice-start.22 = ((s8[4915200]{0:T(1024)(128)(4,1)}), s8[4194304]{0:T(1024)(128)(4,1)S(1)}, s32[]{:S(2)}) async-start(s8[4915200]{0:T(1024)(128)(4,1)} %bitcast.228), calls=%async_computation.24 | async-start | bytes 8388608
  185.1 22.8 %slice-start.26 = ((s8[9437184]{0:T(1024)(128)(4,1)}), s8[4194304]{0:T(1024)(128)(4,1)S(1)}, s32[]{:S(2)}) async-start(s8[9437184]{0:T(1024)(128)(4,1)} %bitcast.232), calls=%async_computation.28 | async-start | bytes 8388608
  195.3 12.5 slice-start.23
  195.3 12.5 slice-start.27
  195.3 12.5 slice-start.28
  195.3 12.5 copy-start.16
  207.9 10.0 copy-start.8
  235.0 1333.2 %all-reduce.5.cloned.1.call-start = ((), (), s32[]{:S(2)}) async-start(), calls=%async_computation | async-start | bytes 75497472 | tf_op jit(solution)/shard_map/psum | solution.py:77
  795.3 28.4 %slice-start.10 = ((s8[9437184]{0:T(1024)(128)(4,1)}), s8[1048576]{0:T(1024)(128)(4,1)S(1)}, s32[]{:S(2)}) async-start(s8[9437184]{0:T(1024)(128)(4,1)} %bitcast.218), calls=%async_computation.12 | async-start | bytes 2097152
  807.3 16.4 slice-start.11
  807.4 16.4 slice-start.12
  823.8 66.9 %copy-start.2 = (bf16[768,3072,1]{1,0,2:T(8,128)(2,1)}, bf16[768,3072,1]{1,0,2:T(8,128)(2,1)S(1)}, u32[]{:S(2)}) copy-start(bf16[768,3072,1]{1,0,2:T(8,128)(2,1)S(1)} %get-tuple-element.17) | copy-start | bytes 14155780
  838.0 14.2 copy-start.1
  838.0 9.8 copy-start.4
  838.0 9.8 copy-start.11
  847.8 15.0 slice-start.16
  852.2 10.6 slice-start.17
  920.4 26.6 %slice-start.18 = ((s8[4718592]{0:T(1024)(128)(4,1)}), s8[4194304]{0:T(1024)(128)(4,1)S(1)}, s32[]{:S(2)}) async-start(s8[4718592]{0:T(1024)(128)(4,1)} %bitcast.224), calls=%async_computation.20 | async-start | bytes 8388608
  932.6 10.1 copy-start.3
  932.6 14.4 slice-start.19
  964.7 16.6 %slice-start.13 = ((s8[9437184]{0:T(1024)(128)(4,1)}), s8[4194304]{0:T(1024)(128)(4,1)S(1)}, s32[]{:S(2)}) async-start(s8[9437184]{0:T(1024)(128)(4,1)} %bitcast.220), calls=%async_computation.15 | async-start | bytes 8388608
  968.7 12.6 slice-start.14
  968.7 12.6 slice-start.15
  1589.2 14.9 slice-start
  1589.2 14.9 slice-start.1
  1589.3 16.6 %slice-start.2 = ((s8[18874368]{0:T(1024)(128)(4,1)}), s8[4194304]{0:T(1024)(128)(4,1)S(1)}, s32[]{:S(2)}) async-start(s8[18874368]{0:T(1024)(128)(4,1)} %bitcast.214), calls=%async_computation.4 | async-start | bytes 8388608
  1589.3 17.8 %slice-start.3 = ((s8[18874368]{0:T(1024)(128)(4,1)}), s8[4194304]{0:T(1024)(128)(4,1)S(1)}, s32[]{:S(2)}) async-start(s8[18874368]{0:T(1024)(128)(4,1)} %bitcast.214), calls=%async_computation.5 | async-start | bytes 8388608
  1589.3 18.4 %slice-start.4 = ((s8[18874368]{0:T(1024)(128)(4,1)}), s8[2097152]{0:T(1024)(128)(4,1)S(1)}, s32[]{:S(2)}) async-start(s8[18874368]{0:T(1024)(128)(4,1)} %bitcast.214), calls=%async_computation.6 | async-start | bytes 4194304
  (6 other events, 30.1 us)
Sparse Core Ops, SparseCore 0:
  235.1 550.7 all-reduce.6
  1019.0 549.1 all-reduce.4
where the time goes:
time: 1650 us
  waiting for transfers between devices  1060 us (64%)
  matrix products  382 us (23%)
  other arithmetic  116 us (7%)
  blocking collectives  41.7 us (3%)
  local copies, waits for them, and re-layouts  29.6 us (2%)
  between operations  20.8 us (1%)
    psum x1, waiting for transfers between devices, local_step(): grad_out = [lax.psum(part_sum, 'data') * tok_scale for part_sum in sums_out]  551 us
    psum x1, waiting for transfers between devices, local_step(): total_in = [lax.psum(part_sum, 'data') for part_sum in second_in]  506 us
    dot_general x8, matrix products, micro_grads(): jnp.einsum('bsd,bsf->df', h_list[layer_idx], d_pre, preferred_element_typ...  105 us
    dot_general x8, matrix products, micro_grads(): jnp.einsum('bsf,bsd->fd', gelu_out.astype(jnp.bfloat16), back_grad, prefe...  89.5 us
    dot_general x8, matrix products, layer_forward(): jnp.einsum('bsf,fd->bsd', gelu_out, wo_cast, preferred_element_type=jnp.f...  69.5 us
    dot_general x8, matrix products, layer_forward(): jnp.einsum('bsd,df->bsf', h_act, wi_cast, preferred_element_type=jnp.floa...  52.3 us
    dot_general x4, matrix products, micro_grads(): jnp.einsum('bsd,fd->bsf', back_grad, wo_list[layer_idx], preferred_elemen...  44.7 us
    psum x1, blocking collectives, local_step(): total_sq = lax.psum(second_sq, 'data')  41.7 us
  transfers between devices with their start and end apart: 2, of which 2 were waited for; matrix products, arithmetic and copies ran while one was open for 0% of the time, Pallas kernels for 0%

commit v1 on v0

v1 whole, which is shorter than its diff:
```python
import math
import functools
import jax
import jax.numpy as jnp
from jax import lax
from jax.experimental import pallas as pl
from jax.experimental.pallas import tpu as pltpu
from jax.sharding import PartitionSpec as P

RHO_FRAC = 0.1
LEARN_RATE = 1.0
TILE_F = 256
MESH = pl.DeviceIdType.MESH
ANY = pl.BlockSpec(memory_space=pl.ANY)
NN = (((1,), (0,)), ((), ()))
NT = (((1,), (1,)), ((), ()))
GELU_C = math.sqrt(2.0 / math.pi)
GELU_K = 0.044715
VMEM_CAP = 67043328
CORE_SLOTS = 14
RS_LAG = (1, 4, 6, 9, 11)
AG_LAG = (13, 15, 17, 20, 22)
VG_LAG = (0, 2, 4, 6, 8)


def dot(lhs, rhs, dims=NN):
    return lax.dot_general(lhs, rhs, dims, preferred_element_type=jnp.float32)


def gelu_parts(z):
    sq = z * z
    th = jnp.tanh(GELU_C * (z + GELU_K * (sq * z)))
    cdf = 0.5 * (1.0 + th)
    return sq, th, cdf


def gelu(z):
    return z * gelu_parts(z)[2]


def gelu_and_grad(z):
    sq, th, cdf = gelu_parts(z)
    slope = cdf + (0.5 * z) * ((1.0 - th * th) * (GELU_C + (3.0 * GELU_K * GELU_C) * sq))
    return z * cdf, slope


def place(axis="data"):
    me = lax.axis_index(axis)
    bits = [lax.rem(lax.div(me, 1 << k), 2) for k in range(5)]
    peers = [me + (1 << k) * (1 - 2 * bits[k]) for k in range(5)]
    return bits, peers


def route(bits, peers, parity, rows):
    _, bx, by, ba, bb = bits
    _, px, py, pa, pb = peers
    b1 = jnp.where(parity == 0, bx, by)
    b3 = jnp.where(parity == 0, by, bx)
    p1 = jnp.where(parity == 0, px, py)
    p3 = jnp.where(parity == 0, py, px)
    keep, send, base = [0], [], 0
    n = rows
    for bit in (b1, ba, b3, bb):
        n //= 2
        keep.append(pl.multiple_of(base + bit * n, 8))
        send.append(pl.multiple_of(base + (1 - bit) * n, 8))
        base = base + bit * n
    return (p1, pa, p3, pb), keep, send


def enter(peers):
    barrier = pltpu.get_barrier_semaphore()
    for peer in peers:
        pl.semaphore_signal(barrier, inc=1, device_id=(peer,), device_id_type=MESH)
    pl.semaphore_wait(barrier, len(peers))


def remote(src, dst, send_sem, recv_sem, peer):
    return pltpu.make_async_remote_copy(src_ref=src, dst_ref=dst, send_sem=send_sem, recv_sem=recv_sem, device_id=(peer,), device_id_type=MESH)


def local(src, dst, sem):
    return pltpu.make_async_copy(src, dst, sem)


def halves(t):
    return [(0, t // 2), (t // 2, t // 2)] if t % 32 == 0 else [(0, t)]


def transpose_into(dst, src, t):
    full = t // 128
    if full:
        @pl.loop(0, full)
        def _(i):
            lo = pl.multiple_of(i * 128, 128)
            dst[:, pl.ds(lo, 128)] = src[pl.ds(lo, 128), :].T
    if t % 128:
        dst[:, full * 128:t] = src[full * 128:t, :].T


def fwd_unit(h_ref, vin_ref, vout_ref, acc_ref, z_ref, t):
    for lo, n in halves(t):
        z = dot(h_ref[lo:lo + n, :], vin_ref[...]).astype(jnp.bfloat16)
        z_ref[lo:lo + n, :] = z
        a = gelu(z.astype(jnp.float32)).astype(jnp.bfloat16)
        acc_ref[lo:lo + n, :] += dot(a, vout_ref[...], NT)


def fwd_close(h_ref, acc_ref, t):
    for lo, n in halves(t):
        h_ref[lo:lo + n, :] = acc_ref[lo:lo + n, :].astype(jnp.bfloat16)


def fwd_seed(h_ref, acc_ref, t):
    for lo, n in halves(t):
        acc_ref[lo:lo + n, :] = h_ref[lo:lo + n, :].astype(jnp.float32)


def first_forward(dm, x_hbm, y_hbm, wi_hbm, wo_hbm, z_out, v_out, ws_out, h_out, q_out,
                  h, yb, acc, wi, wo, vb, zb, ws, load_sem, z_sem, v_sem, io_sem):
    t, d, f, nf, nl = dm
    nu = nf * nl
    bits, peers = place()
    piece = d // 16

    def loads(u, slot):
        layer, tile = u // nf, u % nf
        lo = pl.multiple_of(tile * f, f)
        return (local(wi_hbm.at[layer, :, pl.ds(lo, f)], wi.at[slot], load_sem.at[slot, 0]),
                local(wo_hbm.at[layer, pl.ds(lo, f), :], wo.at[slot], load_sem.at[slot, 1]))

    def stores(u, slot):
        return local(zb.at[slot], z_out.at[u], z_sem.at[slot]), local(vb.at[slot], v_out.at[u], v_sem.at[slot])

    x_in = local(x_hbm, h, io_sem.at[0])
    y_in = local(y_hbm, yb, io_sem.at[1])
    x_in.start()
    for cp in loads(0, 0):
        cp.start()
    y_in.start()
    x_in.wait()
    fwd_seed(h, acc, t)

    @pl.loop(0, nu)
    def _(u):
        slot = lax.rem(u, 2)
        for cp in loads(u, slot):
            cp.wait()

        @pl.when(u + 1 < nu)
        def _():
            for cp in loads(u + 1, 1 - slot):
                cp.start()

        @pl.when(u >= 2)
        def _():
            for cp in stores(u - 2, slot):
                cp.wait()
        wot = wo[slot].T
        _, keep, _ = route(bits, peers, lax.rem(u, 2), d)
        rows = pl.ds(keep[4], piece)
        vb[slot, 0] = wi[slot].astype(jnp.bfloat16)
        vb[slot, 1] = wot.astype(jnp.bfloat16)

        @pl.when(bits[0] == 0)
        def _():
            ws[u] = wi[slot, rows, :]

        @pl.when(bits[0] == 1)
        def _():
            wi[slot] = wot
            ws[u] = wi[slot, rows, :]

        fwd_unit(h, vb.at[slot, 0], vb.at[slot, 1], acc, zb.at[slot], t)
        for cp in stores(u, slot):
            cp.start()

        @pl.when(u == nf - 1)
        def _():
            fwd_close(h, acc, t)
            fwd_seed(h, acc, t)
            out = local(h, h_out, io_sem.at[0])
            out.start()
            out.wait()

    y_in.wait()
    for lo, n in halves(t):
        hl = acc[lo:lo + n, :].astype(jnp.bfloat16).astype(jnp.float32)
        h[lo:lo + n, :] = (hl - yb[lo:lo + n, :].astype(jnp.float32)).astype(jnp.bfloat16)
    out = local(h, q_out, io_sem.at[0])
    out.start()
    ws_cp = local(ws, ws_out, io_sem.at[1])
    ws_cp.start()
    for u in (nu - 2, nu - 1):
        for cp in stores(u, u % 2):
            cp.wait()
    out.wait()
    ws_cp.wait()


def second_forward(dm, scale, rho, gs_hbm, ws_hbm, x_hbm, y_hbm, z_out, v_out, h_out, q_out, sq_out,
                   h, yb, acc, gs, ws, vb, zb, nb, send_sem, recv_sem, nsend_sem, nrecv_sem, z_sem, v_sem, io_sem):
    t, d, f, nf, nl = dm
    nu = nf * nl
    bits, peers = place()
    core = bits[0]
    piece = d // 16
    enter(peers)
    ins = (local(gs_hbm, gs, io_sem.at[0]), local(ws_hbm, ws, io_sem.at[1]), local(x_hbm, h, io_sem.at[2]), local(y_hbm, yb, io_sem.at[3]))
    for cp in ins:
        cp.start()
    ins[0].wait()

    def square(u, total):
        g = gs[u] * scale
        return total + jnp.sum((g * g).reshape(piece // 8, 8, f // 128, 128), axis=(0, 2))
    nb[0] = lax.fori_loop(0, nu, square, jnp.zeros((8, 128), jnp.float32))
    for k in range(5):
        cp = remote(nb.at[2 * k], nb.at[2 * k + 1], nsend_sem.at[k], nrecv_sem.at[k], peers[k])
        cp.start()
        cp.wait()
        nb[2 * k + 2] = nb[2 * k] + nb[2 * k + 1]
    coef = rho / jnp.sqrt(jnp.sum(nb[10], keepdims=True))
    ins[1].wait()

    def hop(u, k):
        ps, keep, _ = route(bits, peers, lax.rem(u, 2), d)
        if k == 4:
            ref = vb.at[u, core]
            return remote(ref, ref, send_sem.at[u, 4], recv_sem.at[u, 4], peers[0])
        n = piece << k
        ref = vb.at[u, core, pl.ds(pl.multiple_of(keep[4 - k], 16), n), :]
        return remote(ref, ref, send_sem.at[u, k], recv_sem.at[u, k], ps[3 - k])

    @pl.loop(0, nu)
    def _(u):
        _, keep, _ = route(bits, peers, lax.rem(u, 2), d)
        new = ws[u] + coef * (gs[u] * scale)
        vb[u, core, pl.ds(pl.multiple_of(keep[4], 16), piece), :] = new.astype(jnp.bfloat16)
        hop(u, 0).start()

    ins[2].wait()
    fwd_seed(h, acc, t)

    def z_store(u, slot):
        return local(zb.at[slot], z_out.at[u], z_sem.at[slot])

    @pl.loop(0, nu + VG_LAG[4])
    def _(it):
        for k in range(4):
            u = it - VG_LAG[k]

            @pl.when((u >= 0) & (u < nu))
            def _():
                hop(u, k).wait_recv()
                hop(u, k + 1).start()
        u = it - VG_LAG[4]

        @pl.when(u >= 0)
        def _():
            slot = lax.rem(u, 2)
            hop(u, 4).wait_recv()
            local(vb.at[u], v_out.at[u], v_sem.at[u]).start()

            @pl.when(u >= 2)
            def _():
                z_store(u - 2, slot).wait()
            fwd_unit(h, vb.at[u, 0], vb.at[u, 1], acc, zb.at[slot], t)
            z_store(u, slot).start()

            @pl.when(u == nf - 1)
            def _():
                fwd_close(h, acc, t)
                fwd_seed(h, acc, t)
                out = local(h, h_out, io_sem.at[0])
                out.start()
                out.wait()

    ins[3].wait()
    total = jnp.zeros((8, 128), jnp.float32)
    for lo, n in halves(t):
        hl = acc[lo:lo + n, :].astype(jnp.bfloat16).astype(jnp.float32)
        e = hl - yb[lo:lo + n, :].astype(jnp.float32)
        h[lo:lo + n, :] = e.astype(jnp.bfloat16)
        total = total + jnp.sum((e * e).reshape(n // 8, 8, d // 128, 128), axis=(0, 2))
    nb[0] = total
    out = local(h, q_out, io_sem.at[0])
    sq = local(nb.at[0], sq_out, io_sem.at[1])
    out.start()
    sq.start()

    @pl.loop(0, nu)
    def _(u):
        local(vb.at[u], v_out.at[u], v_sem.at[u]).wait()
        for k in range(5):
            hop(u, k).wait_send()
    z_store(nu - 2, nu % 2).wait()
    z_store(nu - 1, (nu - 1) % 2).wait()
    out.wait()
    sq.wait()


def backward(dm, scale, final, *refs):
    t, d, f, nf, nl = dm
    nu = nf * nl
    if final:
        (x_hbm, h_hbm, q_hbm, z_hbm, v_hbm, ws_hbm, sq_hbm, w_out, sq_out, *scr) = refs
    else:
        (x_hbm, h_hbm, q_hbm, z_hbm, v_hbm, g_out, *scr) = refs
    (q, tmp, tb, eb, acc, zb, vb, cbuf, obuf, sbuf, r1, r2, r3, r4, gs,
     load_sem, io_sem, csend_sem, send_sem, recv_sem, credit, *more) = scr
    if final:
        nb, ag_send, ag_recv, ag_loc, nsend_sem, nrecv_sem = more
    rbuf = (r1, r2, r3, r4)
    bits, peers = place()
    core = bits[0]
    piece = d // 16
    slots = cbuf.shape[0]
    enter(peers)

    def unit_of(it):
        return (nl - 1 - it // nf) * nf + lax.rem(it, nf)

    def loads(it, slot):
        u = unit_of(it)
        return local(z_hbm.at[u], zb.at[slot], load_sem.at[slot, 0]), local(v_hbm.at[u], vb.at[slot], load_sem.at[slot, 1])

    q_in = local(q_hbm, q, io_sem.at[0])
    h_in = local(h_hbm, tmp, io_sem.at[1])
    q_in.start()
    for cp in loads(0, 0):
        cp.start()
    h_in.start()
    if final:
        ws_in = local(ws_hbm, gs, io_sem.at[2])
        sq_in = local(sq_hbm, nb.at[0], io_sem.at[3])
        ws_in.start()
        sq_in.start()
        ws_in.wait()
        sq_in.wait()
    q_in.wait()
    fwd_seed(q, acc, t)
    transpose_into(tb.at[1], q, t)
    h_in.wait()
    transpose_into(tb.at[0], tmp, t)
    x_in = local(x_hbm, tmp, io_sem.at[1])
    x_in.start()

    def core_copy(it):
        slot = lax.rem(it, 2)
        return remote(sbuf.at[slot], cbuf.at[lax.rem(it, slots)], csend_sem.at[slot], recv_sem.at[0, it], peers[0])

    def rs_copy(it, k):
        ps, _, send = route(bits, peers, lax.rem(it, 2), d)
        n = d >> (k + 1)
        return remote(cbuf.at[lax.rem(it, slots), pl.ds(send[k], n), :], rbuf[k].at[it], send_sem.at[it, k], recv_sem.at[k + 1, it], ps[k])

    def ag_copy(it, k):
        ps, keep, _ = route(bits, peers, lax.rem(it, 2), d)
        u = unit_of(it)
        if k == 4:
            ref = w_out.at[u, core]
            return remote(ref, ref, ag_send.at[it, 4], ag_recv.at[it, 4], peers[0])
        n = piece << k
        ref = w_out.at[u, core, pl.ds(keep[4 - k], n), :]
        src = gs.at[u] if k == 0 else ref
        return remote(src, ref, ag_send.at[it, k], ag_recv.at[it, k], ps[3 - k])

    def ag_local(it):
        _, keep, _ = route(bits, peers, lax.rem(it, 2), d)
        u = unit_of(it)
        return local(gs.at[u], w_out.at[u, core, pl.ds(keep[4], piece), :], ag_loc.at[it])

    n_it = nu + (AG_LAG[4] if final else RS_LAG[4])

    @pl.loop(0, n_it)
    def _(it):
        @pl.when(it == nf)
        def _():
            fwd_close(q, acc, t)
            transpose_into(tb.at[1], q, t)
            x_in.wait()
            transpose_into(tb.at[0], tmp, t)

        @pl.when(it < nu)
        def _():
            slot = lax.rem(it, 2)
            for cp in loads(it, slot):
                cp.wait()

            @pl.when(it + 1 < nu)
            def _():
                for cp in loads(it + 1, 1 - slot):
                    cp.start()
            for lo, n in halves(t):
                back = dot(q[lo:lo + n, :], vb[slot, 1])
                a, slope = gelu_and_grad(zb[slot, lo:lo + n, :].astype(jnp.float32))
                eb[1, lo:lo + n, :] = a.astype(jnp.bfloat16)
                eb[0, lo:lo + n, :] = (back * slope).astype(jnp.bfloat16)

            @pl.when(it >= 2)
            def _():
                core_copy(it - 2).wait_send()
            other = 1 - core
            sbuf[slot] = dot(tb[other], eb[other])

            @pl.when(it >= slots)
            def _():
                pl.semaphore_wait(credit, 1)
            core_copy(it).start()
            obuf[slot] = dot(tb[core], eb[core])

            @pl.when(it < nf)
            def _():
                for lo, n in halves(t):
                    acc[lo:lo + n, :] += dot(eb[0, lo:lo + n, :], vb[slot, 0], NT)

        j0 = it - RS_LAG[0]

        @pl.when((j0 >= 0) & (j0 < nu))
        def _():
            cs = lax.rem(j0, slots)
            core_copy(j0).wait_recv()
            cbuf[cs] = cbuf[cs] + obuf[lax.rem(j0, 2)]
            rs_copy(j0, 0).start()

        for k in range(4):
            j = it - RS_LAG[k + 1]

            @pl.when((j >= 0) & (j < nu))
            def _():
                cs = lax.rem(j, slots)
                _, keep, _ = route(bits, peers, lax.rem(j, 2), d)
                n = d >> (k + 1)
                rows = pl.ds(keep[k + 1], n)
                rs_copy(j, k).wait_recv()
                if k < 3:
                    cbuf[cs, rows, :] = cbuf[cs, rows, :] + rbuf[k][j]
                    rs_copy(j, k + 1).start()
                else:
                    total = cbuf[cs, rows, :] + rbuf[k][j]
                    u = unit_of(j)
                    gs[u] = gs[u] - LEARN_RATE * (total * scale) if final else total
                    for kk in range(4):
                        rs_copy(j, kk).wait_send()

                    @pl.when(j + slots < nu)
                    def _():
                        pl.semaphore_signal(credit, inc=1, device_id=(peers[0],), device_id_type=MESH)
                    if final:
                        ag_local(j).start()
                        ag_copy(j, 0).start()
        if final:
            for k in range(4):
                j = it - AG_LAG[k]

                @pl.when((j >= 0) & (j < nu))
                def _():
                    ag_copy(j, k).wait_recv()
                    if k == 0:
                        ag_local(j).wait()
                    ag_copy(j, k + 1).start()

            @pl.when(it < 5)
            def _():
                for k in range(5):
                    @pl.when(it == k)
                    def _():
                        cp = remote(nb.at[2 * k], nb.at[2 * k + 1], nsend_sem.at[k], nrecv_sem.at[k], peers[k])
                        cp.start()
                        cp.wait()
                        nb[2 * k + 2] = nb[2 * k] + nb[2 * k + 1]

    core_copy(nu - 2).wait_send()
    core_copy(nu - 1).wait_send()
    if final:
        sq_cp = local(nb.at[10], sq_out, io_sem.at[3])
        sq_cp.start()

        @pl.loop(0, nu)
        def _(it):
            ag_copy(it, 4).wait_recv()
            for k in range(5):
                ag_copy(it, k).wait_send()
        sq_cp.wait()
    else:
        g_cp = local(gs, g_out, io_sem.at[0])
        g_cp.start()
        g_cp.wait()


def sds(shape, dtype):
    return jax.ShapeDtypeStruct(shape, dtype)


def call(kernel, n_in, outs, scratch, name, collective_id=None):
    params = dict(vmem_limit_bytes=VMEM_CAP)
    if collective_id is not None:
        params.update(collective_id=collective_id, has_side_effects=True)
    return pl.pallas_call(
        kernel,
        out_shape=outs,
        in_specs=[ANY] * n_in,
        out_specs=[ANY] * len(outs),
        scratch_shapes=scratch,
        compiler_params=pltpu.CompilerParams(**params),
        name=name,
    )


def local_step(n_dev, tile_f, x_loc, y_loc, w_in, w_out):
    nl, d, ff = w_in.shape
    f = tile_f
    nf = ff // f
    nu = nl * nf
    t = x_loc.shape[0] * x_loc.shape[1]
    piece = d // 16
    dm = (t, d, f, nf, nl)
    scale = 1.0 / (t * n_dev * d)
    rho = RHO_FRAC * math.sqrt(nl * (d + ff))
    bf, f32 = jnp.bfloat16, jnp.float32
    V, DMA = pltpu.VMEM, pltpu.SemaphoreType.DMA
    x = x_loc.reshape(t, d)
    y = y_loc.reshape(t, d)
    z_s, v_s, w_s, a_s = sds((nu, t, f), bf), sds((nu, 2, d, f), bf), sds((nu, piece, f), f32), sds((t, d), bf)

    z, v, ws, h1, q = call(
        functools.partial(first_forward, dm), 4, [z_s, v_s, w_s, a_s, a_s],
        [V((t, d), bf), V((t, d), bf), V((t, d), f32), V((2, d, f), f32), V((2, f, d), f32), V((2, 2, d, f), bf), V((2, t, f), bf), V((nu, piece, f), f32),
         DMA((2, 2)), DMA((2,)), DMA((2,)), DMA((2,))], "fwd_a")(x, y, w_in, w_out)

    slots = min(CORE_SLOTS, nu)
    bwd_scratch = [
        V((t, d), bf), V((t, d), bf), V((2, d, t), bf), V((2, t, f), bf), V((t, d), f32), V((2, t, f), bf), V((2, 2, d, f), bf),
        V((slots, d, f), f32), V((2, d, f), f32), V((2, d, f), f32),
        V((nu, d // 2, f), f32), V((nu, d // 4, f), f32), V((nu, d // 8, f), f32), V((nu, d // 16, f), f32), V((nu, piece, f), f32),
        DMA((2, 2)), DMA((4,)), DMA((2,)), DMA((nu, 4)), DMA((5, nu)), pltpu.SemaphoreType.REGULAR]
    (g,) = call(functools.partial(backward, dm, scale, False), 5, [w_s], bwd_scratch, "bwd_a", 0)(x, h1, q, z, v)

    z, v, h1, q, sq = call(
        functools.partial(second_forward, dm, scale, rho), 4, [z_s, v_s, a_s, a_s, sds((8, 128), f32)],
        [V((t, d), bf), V((t, d), bf), V((t, d), f32), V((nu, piece, f), f32), V((nu, piece, f), f32), V((nu, 2, d, f), bf), V((2, t, f), bf), V((11, 8, 128), f32),
         DMA((nu, 5)), DMA((nu, 5)), DMA((5,)), DMA((5,)), DMA((2,)), DMA((nu,)), DMA((4,))], "fwd_b", 1)(g, ws, x, y)

    w_new, sq = call(
        functools.partial(backward, dm, scale, True), 7, [sds((nu, 2, d, f), f32), sds((8, 128), f32)],
        bwd_scratch + [V((11, 8, 128), f32), DMA((nu, 5)), DMA((nu, 5)), DMA((nu,)), DMA((5,)), DMA((5,))], "bwd_b", 2)(x, h1, q, z, v, ws, sq)

    w_new = w_new.reshape(nl, nf, 2, d, f)
    new_in = w_new[:, :, 0].transpose(0, 2, 1, 3).reshape(nl, d, ff)
    new_out = w_new[:, :, 1].transpose(0, 1, 3, 2).reshape(nl, ff, d)
    loss = 0.5 * (jnp.sum(sq) * scale)
    return new_in, new_out, loss


def solution(mesh):
    step = functools.partial(local_step, mesh.shape["data"], TILE_F)
    return jax.shard_map(step, mesh=mesh, in_specs=(P("data"), P("data"), P(), P()), out_specs=(P(), P(), P()), check_vma=False)
```

time: 1650 us -> 813 us (0.49)
  waiting for transfers between devices: 1060 us -> 0 us
  Pallas kernels: 0 us -> 718 us
  matrix products: 382 us -> 0 us
  other arithmetic: 116 us -> 1.28 us
  local copies, waits for them, and re-layouts: 29.6 us -> 90.4 us
  blocking collectives: 41.7 us -> 0 us
  between operations: 20.8 us -> 2.45 us
    psum x2 -> x0, waiting for transfers between devices: 1060 us -> none  [the longest x1 551 us: local_step(): grad_out = [lax.psum(part_sum, 'data') * tok_scale for part_sum in sums_out]]
    pallas_call x0 -> x4, Pallas kernels: none -> 718 us  [the longest x1 346 us: local_step(): call(functools.partial(backward, dm, scale, True), 7, [sds((nu, 2, d, f),...]
    dot_general x40 -> x0, matrix products: 382 us -> none  [the longest x8 105 us: micro_grads(): jnp.einsum('bsd,bsf->df', h_list[layer_idx], d_pre, preferred_element_typ...]
    another operation x4 -> x0, other arithmetic: 66.5 us -> none  [the longest x2 36 us: local_step(): jnp.stack([w_in[layer_idx] - LEARN_RATE * (total_in[layer_idx] * tok_scal...]
    transpose x0 -> x2, local copies, waits for them, and re-layouts: none -> 44.6 us  [local_step(): new_out = w_new[:, :, 1].transpose(0, 1, 3, 2).reshape(nl, ff, d)]
    psum x1 -> x0, blocking collectives: 41.7 us -> none  [local_step(): total_sq = lax.psum(second_sq, 'data')]
    unnamed x104 -> x4, local copies, waits for them, and re-layouts: 10.6 us -> 41.6 us
    convert_element_type x2 -> x0, other arithmetic: 30.6 us -> none  [the longest x1 16.4 us: local_step(): (w_in[layer_idx] + perturb_coef * grad_in[layer_idx]).astype(jnp.bfloat16)]
  transfers between devices with their start and end apart: 2 -> 0, of which waited for: 2 -> 0; matrix products, arithmetic and copies ran while one was open for 0% -> 0% of each run, Pallas kernels for 0% -> 0%
where the time goes in v1:
time: 813 us; the launch traced here: 812 us
  Pallas kernels  718 us (88%)
  local copies, waits for them, and re-layouts  90.4 us (11%)
    pallas_call x1, Pallas kernels, local_step(): call(functools.partial(backward, dm, scale, True), 7, [sds((nu, 2, d, f),...  346 us
    pallas_call x1, Pallas kernels, local_step(): call(functools.partial(backward, dm, scale, False), 5, [w_s], bwd_scratch...  185 us
    pallas_call x1, Pallas kernels, local_step(): call(functools.partial(second_forward, dm, scale, rho), 4, [z_s, v_s, a_s...  122 us
    pallas_call x1, Pallas kernels, local_step(): call(functools.partial(first_forward, dm), 4, [z_s, v_s, w_s, a_s, a_s],...  65.3 us
    transpose x2, local copies, waits for them, and re-layouts, local_step(): new_out = w_new[:, :, 1].transpose(0, 1, 3, 2).reshape(nl, ff, d)  44.6 us
    unnamed x4, local copies, waits for them, and re-layouts  41.6 us

profile of v1, /device:TPU:0, one launch (start us, length us, event | category | flops | bytes accessed | tf_op | source)
XLA Modules:
  0.0 812.2 jit_solution(17893938937634212512)
XLA Ops:
  0.6 2.1 copy.11
  2.8 2.1 reshape.21.x_hbm.refs_0_
  4.9 2.1 copy.12
  7.0 2.1 reshape.22.y_hbm
  9.2 65.3 %fwd_a.1 = (bf16[24,1568,256]{2,1,0:T(8,128)(2,1)}, bf16[24,2,768,256]{3,2,1,0:T(8,128)(2,1)}, f32[24,48,256]{2,1,0:T(8,128)}, bf16[1568,768]{1,0:T(8,128)(2,1)}, bf16[1568,768]{1,0:T(8,128)(2,1)}) custom-call(bf16[1568,768]{1,0:T(8,128)(2,1)} %reshape.21.x_hbm.refs_0_, bf16[1568,768]{1,0:T(8,128)(2,1)} %reshape.22.y_hbm, f32[2,768,3072]{2,1,0:T(8,128)} %wi_hbm.1, ...), custom_call_target="tpu_custom_call" | custom-call | tf_op jit(solution)/shard_map/fwd_a/pallas_call | solution.py:527
  74.4 184.9 %bwd_a.1.gs_hbm = f32[24,48,256]{2,1,0:T(8,128)} custom-call(bf16[1568,768]{1,0:T(8,128)(2,1)} %reshape.21.x_hbm.refs_0_, bf16[1568,768]{1,0:T(8,128)(2,1)} %get-tuple-element.15.refs_1_, bf16[1568,768]{1,0:T(8,128)(2,1)} %get-tuple-element.16.refs_2_, bf16[24,1568,256]{2,1,0:T(8,128)(2,1)} %get-tuple-element.17.refs_3_, ...), custom_call_target="tpu_custom_call" | custom-call | tf_op jit(solution)/shard_map/bwd_a/pallas_call | solution.py:538
  259.3 122.4 %fwd_b.1 = (bf16[24,1568,256]{2,1,0:T(8,128)(2,1)}, bf16[24,2,768,256]{3,2,1,0:T(8,128)(2,1)}, bf16[1568,768]{1,0:T(8,128)(2,1)}, bf16[1568,768]{1,0:T(8,128)(2,1)}, f32[8,128]{1,0:T(8,128)}) custom-call(f32[24,48,256]{2,1,0:T(8,128)} %bwd_a.1.gs_hbm, f32[24,48,256]{2,1,0:T(8,128)} %get-tuple-element.19.ws_hbm.refs_5_, ...), custom_call_target="tpu_custom_call" | custom-call | tf_op jit(solution)/shard_map/fwd_b/pallas_call | solution.py:540
  381.7 345.5 %bwd_b.1 = (f32[24,2,768,256]{3,2,1,0:T(8,128)}, f32[8,128]{1,0:T(8,128)}) custom-call(bf16[1568,768]{1,0:T(8,128)(2,1)} %reshape.21.x_hbm.refs_0_, bf16[1568,768]{1,0:T(8,128)(2,1)} %get-tuple-element.20.refs_1_, bf16[1568,768]{1,0:T(8,128)(2,1)} %get-tuple-element.21.refs_2_, bf16[24,1568,256]{2,1,0:T(8,128)(2,1)} %get-tuple-element.22.refs_3_, ...), custom_call_target="tpu_custom_call" | custom-call | tf_op jit(solution)/shard_map/bwd_b/pallas_call | solution.py:545
  727.2 1.3 reduce_sum.9
  729.1 26.0 %slice_bitcast_fusion = (f32[2,12,256,768]{2,3,1,0:T(8,128)}, f32[2,12,1,768,256]{4,3,2,1,0:T(8,128)}) fusion(f32[2,12,2,768,256]{4,3,2,1,0:T(8,128)} %bitcast.12), kind=kLoop, calls=%fused_computation | loop fusion | bytes 75497472 | tf_op jit(solution)/shard_map/transpose | solution.py:551
  755.1 18.6 %copy.14 = f32[2,12,256,768]{3,2,1,0:T(8,128)} copy(f32[2,12,256,768]{2,3,1,0:T(8,128)} %get-tuple-element.30) | data formatting | bytes 37748736 | tf_op jit(solution)/shard_map/transpose | solution.py:551
  773.7 18.6 %copy.16 = f32[2,12,1,768,256]{3,4,1,0,2:T(8,128)} copy(f32[2,12,1,768,256]{4,3,2,1,0:T(8,128)} %get-tuple-element.31) | data formatting | bytes 37748736
  792.4 18.6 %copy.15 = f32[2,768,3072]{2,1,0:T(8,128)} copy(f32[2,768,3072]{1,2,0:T(8,128)} %bitcast.11) | data formatting | bytes 37748736

commit v2 on v1

--- a/solution.py
+++ b/solution.py
@@ -20,7 +20,7 @@
 CORE_SLOTS = 14
 RS_LAG = (1, 4, 6, 9, 11)
 AG_LAG = (13, 15, 17, 20, 22)
-VG_LAG = (0, 2, 4, 6, 8)
+VG_LAG = (0, 2, 4, 6, 9, 10)
 
 
 def dot(lhs, rhs, dims=NN):
@@ -98,12 +98,15 @@
         dst[:, full * 128:t] = src[full * 128:t, :].T
 
 
-def fwd_unit(h_ref, vin_ref, vout_ref, acc_ref, z_ref, t):
+def fwd_pair(h_ref, v_ref, acc_ref, a_ref, z_ref, t, f):
     for lo, n in halves(t):
-        z = dot(h_ref[lo:lo + n, :], vin_ref[...]).astype(jnp.bfloat16)
-        z_ref[lo:lo + n, :] = z
-        a = gelu(z.astype(jnp.float32)).astype(jnp.bfloat16)
-        acc_ref[lo:lo + n, :] += dot(a, vout_ref[...], NT)
+        for j in range(2):
+            z = dot(h_ref[lo:lo + n, :], v_ref[j, 0]).astype(jnp.bfloat16)
+            z_ref[j, lo:lo + n, :] = z
+            a_ref[lo:lo + n, j * f:(j + 1) * f] = gelu(z.astype(jnp.float32)).astype(jnp.bfloat16)
+    v_out = jnp.concatenate([v_ref[0, 1], v_ref[1, 1]], axis=1)
+    for lo, n in halves(t):
+        acc_ref[lo:lo + n, :] += dot(a_ref[lo:lo + n, :], v_out, NT)
 
 
 def fwd_close(h_ref, acc_ref, t):
@@ -117,20 +120,21 @@
 
 
 def first_forward(dm, x_hbm, y_hbm, wi_hbm, wo_hbm, z_out, v_out, ws_out, h_out, q_out,
-                  h, yb, acc, wi, wo, vb, zb, ws, load_sem, z_sem, v_sem, io_sem):
+                  h, yb, acc, ab, wi, wo, vb, zb, ws, load_sem, z_sem, v_sem, io_sem):
     t, d, f, nf, nl = dm
     nu = nf * nl
     bits, peers = place()
     piece = d // 16
 
-    def loads(u, slot):
-        layer, tile = u // nf, u % nf
-        lo = pl.multiple_of(tile * f, f)
-        return (local(wi_hbm.at[layer, :, pl.ds(lo, f)], wi.at[slot], load_sem.at[slot, 0]),
-                local(wo_hbm.at[layer, pl.ds(lo, f), :], wo.at[slot], load_sem.at[slot, 1]))
-
-    def stores(u, slot):
-        return local(zb.at[slot], z_out.at[u], z_sem.at[slot]), local(vb.at[slot], v_out.at[u], v_sem.at[slot])
+    def loads(p, slot):
+        layer, tile = p // (nf // 2), lax.rem(p, nf // 2)
+        lo = pl.multiple_of(tile * 2 * f, 2 * f)
+        return (local(wi_hbm.at[layer, :, pl.ds(lo, 2 * f)], wi.at[slot], load_sem.at[slot, 0]),
+                local(wo_hbm.at[layer, pl.ds(lo, 2 * f), :], wo.at[slot], load_sem.at[slot, 1]))
+
+    def stores(p, slot):
+        two = pl.ds(2 * p, 2)
+        return local(zb.at[slot], z_out.at[two], z_sem.at[slot]), local(vb.at[slot], v_out.at[two], v_sem.at[slot])
 
     x_in = local(x_hbm, h, io_sem.at[0])
     y_in = local(y_hbm, yb, io_sem.at[1])
@@ -141,41 +145,43 @@
     x_in.wait()
     fwd_seed(h, acc, t)
 
-    @pl.loop(0, nu)
-    def _(u):
-        slot = lax.rem(u, 2)
-        for cp in loads(u, slot):
+    @pl.loop(0, nu // 2)
+    def _(p):
+        slot = lax.rem(p, 2)
+        for cp in loads(p, slot):
             cp.wait()
 
-        @pl.when(u + 1 < nu)
-        def _():
-            for cp in loads(u + 1, 1 - slot):
+        @pl.when(p + 1 < nu // 2)
+        def _():
+            for cp in loads(p + 1, 1 - slot):
                 cp.start()
 
-        @pl.when(u >= 2)
-        def _():
-            for cp in stores(u - 2, slot):
+        @pl.when(p >= 2)
+        def _():
+            for cp in stores(p - 2, slot):
                 cp.wait()
-        wot = wo[slot].T
-        _, keep, _ = route(bits, peers, lax.rem(u, 2), d)
-        rows = pl.ds(keep[4], piece)
-        vb[slot, 0] = wi[slot].astype(jnp.bfloat16)
-        vb[slot, 1] = wot.astype(jnp.bfloat16)
-
-        @pl.when(bits[0] == 0)
-        def _():
-            ws[u] = wi[slot, rows, :]
-
-        @pl.when(bits[0] == 1)
-        def _():
-            wi[slot] = wot
-            ws[u] = wi[slot, rows, :]
-
-        fwd_unit(h, vb.at[slot, 0], vb.at[slot, 1], acc, zb.at[slot], t)
-        for cp in stores(u, slot):
+        for j in range(2):
+            cols = slice(j * f, (j + 1) * f)
+            wot = wo[slot, cols, :].T
+            _, keep, _ = route(bits, peers, j, d)
+            rows = pl.ds(keep[4], piece)
+            vb[slot, j, 0] = wi[slot, :, cols].astype(jnp.bfloat16)
+            vb[slot, j, 1] = wot.astype(jnp.bfloat16)
+
+            @pl.when(bits[0] == 0)
+            def _():
+                ws[2 * p + j] = wi[slot, rows, cols]
+
+            @pl.when(bits[0] == 1)
+            def _():
+                wi[slot, :, cols] = wot
+                ws[2 * p + j] = wi[slot, rows, cols]
+
+        fwd_pair(h, vb.at[slot], acc, ab, zb.at[slot], t, f)
+        for cp in stores(p, slot):
             cp.start()
 
-        @pl.when(u == nf - 1)
+        @pl.when(p == nf // 2 - 1)
         def _():
             fwd_close(h, acc, t)
             fwd_seed(h, acc, t)
@@ -191,15 +197,15 @@
     out.start()
     ws_cp = local(ws, ws_out, io_sem.at[1])
     ws_cp.start()
-    for u in (nu - 2, nu - 1):
-        for cp in stores(u, u % 2):
+    for p in range(max(nu // 2 - 2, 0), nu // 2):
+        for cp in stores(p, p % 2):
             cp.wait()
     out.wait()
     ws_cp.wait()
 
 
 def second_forward(dm, scale, rho, gs_hbm, ws_hbm, x_hbm, y_hbm, z_out, v_out, h_out, q_out, sq_out,
-                   h, yb, acc, gs, ws, vb, zb, nb, send_sem, recv_sem, nsend_sem, nrecv_sem, z_sem, v_sem, io_sem):
+                   h, yb, acc, ab, gs, ws, vb, zb, nb, send_sem, recv_sem, nsend_sem, nrecv_sem, z_sem, v_sem, io_sem):
     t, d, f, nf, nl = dm
     nu = nf * nl
     bits, peers = place()
@@ -232,43 +238,46 @@
         ref = vb.at[u, core, pl.ds(pl.multiple_of(keep[4 - k], 16), n), :]
         return remote(ref, ref, send_sem.at[u, k], recv_sem.at[u, k], ps[3 - k])
 
-    @pl.loop(0, nu)
-    def _(u):
-        _, keep, _ = route(bits, peers, lax.rem(u, 2), d)
-        new = ws[u] + coef * (gs[u] * scale)
-        vb[u, core, pl.ds(pl.multiple_of(keep[4], 16), piece), :] = new.astype(jnp.bfloat16)
-        hop(u, 0).start()
-
     ins[2].wait()
     fwd_seed(h, acc, t)
 
-    def z_store(u, slot):
-        return local(zb.at[slot], z_out.at[u], z_sem.at[slot])
-
-    @pl.loop(0, nu + VG_LAG[4])
+    def z_store(p, slot):
+        return local(zb.at[slot], z_out.at[pl.ds(2 * p, 2)], z_sem.at[slot])
+
+    @pl.loop(0, nu + VG_LAG[5])
     def _(it):
-        for k in range(4):
+        @pl.when(it < nu)
+        def _():
+            _, keep, _ = route(bits, peers, lax.rem(it, 2), d)
+            new = ws[it] + coef * (gs[it] * scale)
+            vb[it, core, pl.ds(pl.multiple_of(keep[4], 16), piece), :] = new.astype(jnp.bfloat16)
+            hop(it, 0).start()
+        for k in range(1, 5):
             u = it - VG_LAG[k]
 
             @pl.when((u >= 0) & (u < nu))
             def _():
-                hop(u, k).wait_recv()
-                hop(u, k + 1).start()
-        u = it - VG_LAG[4]
+                hop(u, k - 1).wait_recv()
+                hop(u, k).start()
+        u = it - VG_LAG[5]
 
         @pl.when(u >= 0)
         def _():
-            slot = lax.rem(u, 2)
             hop(u, 4).wait_recv()
             local(vb.at[u], v_out.at[u], v_sem.at[u]).start()
 
-            @pl.when(u >= 2)
-            def _():
-                z_store(u - 2, slot).wait()
-            fwd_unit(h, vb.at[u, 0], vb.at[u, 1], acc, zb.at[slot], t)
-            z_store(u, slot).start()
-
-            @pl.when(u == nf - 1)
+        @pl.when((u >= 0) & (lax.rem(u, 2) == 1))
+        def _():
+            p = u // 2
+            slot = lax.rem(p, 2)
+
+            @pl.when(p >= 2)
+            def _():
+                z_store(p - 2, slot).wait()
+            fwd_pair(h, vb.at[pl.ds(2 * p, 2)], acc, ab, zb.at[slot], t, f)
+            z_store(p, slot).start()
+
+            @pl.when(p == nf // 2 - 1)
             def _():
                 fwd_close(h, acc, t)
                 fwd_seed(h, acc, t)
@@ -294,8 +303,8 @@
         local(vb.at[u], v_out.at[u], v_sem.at[u]).wait()
         for k in range(5):
             hop(u, k).wait_send()
-    z_store(nu - 2, nu % 2).wait()
-    z_store(nu - 1, (nu - 1) % 2).wait()
+    for p in range(max(nu // 2 - 2, 0), nu // 2):
+        z_store(p, p % 2).wait()
     out.wait()
     sq.wait()
 
@@ -489,6 +498,13 @@
         g_cp.wait()
 
 
+def finish(scale, f, w_ref, sq_ref, in_ref, out_ref, loss_ref):
+    for j in range(2):
+        in_ref[0, :, j * f:(j + 1) * f] = w_ref[j, 0]
+        out_ref[0, j * f:(j + 1) * f, :] = w_ref[j, 1].T
+    loss_ref[0, 0] = 0.5 * (jnp.sum(sq_ref[...]) * scale)
+
+
 def sds(shape, dtype):
     return jax.ShapeDtypeStruct(shape, dtype)
 
@@ -520,13 +536,14 @@
     rho = RHO_FRAC * math.sqrt(nl * (d + ff))
     bf, f32 = jnp.bfloat16, jnp.float32
     V, DMA = pltpu.VMEM, pltpu.SemaphoreType.DMA
-    x = x_loc.reshape(t, d)
-    y = y_loc.reshape(t, d)
+    x = x_loc.transpose(1, 0, 2).reshape(t, d)
+    y = y_loc.transpose(1, 0, 2).reshape(t, d)
     z_s, v_s, w_s, a_s = sds((nu, t, f), bf), sds((nu, 2, d, f), bf), sds((nu, piece, f), f32), sds((t, d), bf)
 
     z, v, ws, h1, q = call(
         functools.partial(first_forward, dm), 4, [z_s, v_s, w_s, a_s, a_s],
-        [V((t, d), bf), V((t, d), bf), V((t, d), f32), V((2, d, f), f32), V((2, f, d), f32), V((2, 2, d, f), bf), V((2, t, f), bf), V((nu, piece, f), f32),
+        [V((t, d), bf), V((t, d), bf), V((t, d), f32), V((t, 2 * f), bf), V((2, d, 2 * f), f32), V((2, 2 * f, d), f32), V((2, 2, 2, d, f), bf), V((2, 2, t, f), bf),
+         V((nu, piece, f), f32),
          DMA((2, 2)), DMA((2,)), DMA((2,)), DMA((2,))], "fwd_a")(x, y, w_in, w_out)
 
     slots = min(CORE_SLOTS, nu)
@@ -539,18 +556,24 @@
 
     z, v, h1, q, sq = call(
         functools.partial(second_forward, dm, scale, rho), 4, [z_s, v_s, a_s, a_s, sds((8, 128), f32)],
-        [V((t, d), bf), V((t, d), bf), V((t, d), f32), V((nu, piece, f), f32), V((nu, piece, f), f32), V((nu, 2, d, f), bf), V((2, t, f), bf), V((11, 8, 128), f32),
+        [V((t, d), bf), V((t, d), bf), V((t, d), f32), V((t, 2 * f), bf), V((nu, piece, f), f32), V((nu, piece, f), f32), V((nu, 2, d, f), bf), V((2, 2, t, f), bf),
+         V((11, 8, 128), f32),
          DMA((nu, 5)), DMA((nu, 5)), DMA((5,)), DMA((5,)), DMA((2,)), DMA((nu,)), DMA((4,))], "fwd_b", 1)(g, ws, x, y)
 
     w_new, sq = call(
         functools.partial(backward, dm, scale, True), 7, [sds((nu, 2, d, f), f32), sds((8, 128), f32)],
         bwd_scratch + [V((11, 8, 128), f32), DMA((nu, 5)), DMA((nu, 5)), DMA((nu,)), DMA((5,)), DMA((5,))], "bwd_b", 2)(x, h1, q, z, v, ws, sq)
 
-    w_new = w_new.reshape(nl, nf, 2, d, f)
-    new_in = w_new[:, :, 0].transpose(0, 2, 1, 3).reshape(nl, d, ff)
-    new_out = w_new[:, :, 1].transpose(0, 1, 3, 2).reshape(nl, ff, d)
-    loss = 0.5 * (jnp.sum(sq) * scale)
-    return new_in, new_out, loss
+    new_in, new_out, loss = pl.pallas_call(
+        functools.partial(finish, scale, f),
+        grid=(nl, nf // 2),
+        in_specs=[pl.BlockSpec((2, 2, d, f), lambda i, j: (i * (nf // 2) + j, 0, 0, 0)), pl.BlockSpec((8, 128), lambda i, j: (0, 0))],
+        out_specs=[pl.BlockSpec((1, d, 2 * f), lambda i, j: (i, 0, j)), pl.BlockSpec((1, 2 * f, d), lambda i, j: (i, j, 0)),
+                   pl.BlockSpec((1, 1), lambda i, j: (0, 0), memory_space=pltpu.SMEM)],
+        out_shape=[sds((nl, d, ff), f32), sds((nl, ff, d), f32), sds((1, 1), f32)],
+        compiler_params=pltpu.CompilerParams(vmem_limit_bytes=VMEM_CAP),
+        name="finish")(w_new, sq)
+    return new_in, new_out, loss.reshape(())
 
 
 def solution(mesh):

time: 813 us -> 714 us (0.88)
  local copies, waits for them, and re-layouts: 90.4 us -> 0 us
    transpose x2 -> x0, local copies, waits for them, and re-layouts: 44.6 us -> none  [local_step(): new_out = w_new[:, :, 1].transpose(0, 1, 3, 2).reshape(nl, ff, d)]
    unnamed x4 -> x0, local copies, waits for them, and re-layouts: 41.6 us -> none
    pallas_call x0 -> x1, Pallas kernels: none -> 28.9 us  [local_step(): pl.pallas_call(functools.partial(finish, scale, f), grid=(nl, nf // 2), i...]
    pallas_call x1, Pallas kernels: 122 us -> 103 us  [local_step(): call(functools.partial(second_forward, dm, scale, rho), 4, [z_s, v_s, a_s...]
    pallas_call x1, Pallas kernels: 65.3 us -> 47.1 us  [local_step(): call(functools.partial(first_forward, dm), 4, [z_s, v_s, w_s, a_s, a_s],...]
where the time goes in v2:
time: 714 us; the launch traced here: 713 us
  Pallas kernels  713 us (100%)
    pallas_call x1, Pallas kernels, local_step(): call(functools.partial(backward, dm, scale, True), 7, [sds((nu, 2, d, f),...  348 us
    pallas_call x1, Pallas kernels, local_step(): call(functools.partial(backward, dm, scale, False), 5, [w_s], bwd_scratch...  185 us
    pallas_call x1, Pallas kernels, local_step(): call(functools.partial(second_forward, dm, scale, rho), 4, [z_s, v_s, a_s...  103 us
    pallas_call x1, Pallas kernels, local_step(): call(functools.partial(first_forward, dm), 4, [z_s, v_s, w_s, a_s, a_s],...  47.1 us
    pallas_call x1, Pallas kernels, local_step(): pl.pallas_call(functools.partial(finish, scale, f), grid=(nl, nf // 2), i...  28.9 us

profile of v2, /device:TPU:0, one launch (start us, length us, event | category | flops | bytes accessed | tf_op | source)
XLA Modules:
  0.0 713.2 jit_solution(8548500554239804947)
XLA Ops:
  0.6 47.1 %fwd_a.1 = (bf16[24,1568,256]{2,1,0:T(8,128)(2,1)}, bf16[24,2,768,256]{3,2,1,0:T(8,128)(2,1)}, f32[24,48,256]{2,1,0:T(8,128)}, bf16[1568,768]{1,0:T(8,128)(2,1)}, bf16[1568,768]{1,0:T(8,128)(2,1)}) custom-call(bf16[1568,768]{1,0:T(8,128)(2,1)} %bitcast.7, bf16[1568,768]{1,0:T(8,128)(2,1)} %bitcast.11, f32[2,768,3072]{2,1,0:T(8,128)} %wi_hbm.1, ...), custom_call_target="tpu_custom_call" | custom-call | tf_op jit(solution)/shard_map/fwd_a/pallas_call | solution.py:543
  47.8 184.8 %bwd_a.1.gs_hbm = f32[24,48,256]{2,1,0:T(8,128)} custom-call(bf16[1568,768]{1,0:T(8,128)(2,1)} %bitcast.8, bf16[1568,768]{1,0:T(8,128)(2,1)} %get-tuple-element.18.refs_1_, bf16[1568,768]{1,0:T(8,128)(2,1)} %get-tuple-element.19.refs_2_, bf16[24,1568,256]{2,1,0:T(8,128)(2,1)} %get-tuple-element.20.refs_3_, bf16[24,2,768,256]{3,2,1,0:T(8,128)(2,1)} %get-tuple-element.21.refs_4_), custom_call_target="tpu_custom_call" | custom-call | tf_op jit(solution)/shard_map/bwd_a/pallas_call | solution.py:555
  232.6 103.4 %fwd_b.1 = (bf16[24,1568,256]{2,1,0:T(8,128)(2,1)}, bf16[24,2,768,256]{3,2,1,0:T(8,128)(2,1)}, bf16[1568,768]{1,0:T(8,128)(2,1)}, bf16[1568,768]{1,0:T(8,128)(2,1)}, f32[8,128]{1,0:T(8,128)}) custom-call(f32[24,48,256]{2,1,0:T(8,128)} %bwd_a.1.gs_hbm, f32[24,48,256]{2,1,0:T(8,128)} %get-tuple-element.22.ws_hbm.refs_5_, bf16[1568,768]{1,0:T(8,128)(2,1)} %bitcast.9, ...), custom_call_target="tpu_custom_call" | custom-call | tf_op jit(solution)/shard_map/fwd_b/pallas_call | solution.py:557
  336.0 348.3 %bwd_b.1 = (f32[24,2,768,256]{3,2,1,0:T(8,128)}, f32[8,128]{1,0:T(8,128)}) custom-call(bf16[1568,768]{1,0:T(8,128)(2,1)} %bitcast.10, bf16[1568,768]{1,0:T(8,128)(2,1)} %get-tuple-element.23.refs_1_, bf16[1568,768]{1,0:T(8,128)(2,1)} %get-tuple-element.24.refs_2_, bf16[24,1568,256]{2,1,0:T(8,128)(2,1)} %get-tuple-element.25.refs_3_, ...), custom_call_target="tpu_custom_call" | custom-call | tf_op jit(solution)/shard_map/bwd_b/pallas_call | solution.py:563
  684.3 28.9 %finish.1 = (f32[2,768,3072]{2,1,0:T(8,128)}, f32[2,3072,768]{2,1,0:T(8,128)}, f32[1,1]{1,0:T(1,128)}) custom-call(f32[24,2,768,256]{3,2,1,0:T(8,128)} %get-tuple-element.28.w_ref, f32[8,128]{1,0:T(8,128)} %get-tuple-element.29.sq_ref), custom_call_target="tpu_custom_call" | custom-call | tf_op jit(solution)/shard_map/finish/pallas_call | solution.py:567

commit v3 on v2

--- a/solution.py
+++ b/solution.py
@@ -51,8 +51,9 @@
     return bits, peers
 
 
-def route(bits, peers, parity, rows):
-    _, bx, by, ba, bb = bits
+def route(bits, peers, unit, rows):
+    core, bx, by, ba, bb = bits
+    parity = lax.rem(unit + core, 2)
     _, px, py, pa, pb = peers
     b1 = jnp.where(parity == 0, bx, by)
     b3 = jnp.where(parity == 0, by, bx)
@@ -230,7 +231,7 @@
     ins[1].wait()
 
     def hop(u, k):
-        ps, keep, _ = route(bits, peers, lax.rem(u, 2), d)
+        ps, keep, _ = route(bits, peers, u, d)
         if k == 4:
             ref = vb.at[u, core]
             return remote(ref, ref, send_sem.at[u, 4], recv_sem.at[u, 4], peers[0])
@@ -248,7 +249,7 @@
     def _(it):
         @pl.when(it < nu)
         def _():
-            _, keep, _ = route(bits, peers, lax.rem(it, 2), d)
+            _, keep, _ = route(bits, peers, it, d)
             new = ws[it] + coef * (gs[it] * scale)
             vb[it, core, pl.ds(pl.multiple_of(keep[4], 16), piece), :] = new.astype(jnp.bfloat16)
             hop(it, 0).start()
@@ -360,12 +361,12 @@
         return remote(sbuf.at[slot], cbuf.at[lax.rem(it, slots)], csend_sem.at[slot], recv_sem.at[0, it], peers[0])
 
     def rs_copy(it, k):
-        ps, _, send = route(bits, peers, lax.rem(it, 2), d)
+        ps, _, send = route(bits, peers, it, d)
         n = d >> (k + 1)
         return remote(cbuf.at[lax.rem(it, slots), pl.ds(send[k], n), :], rbuf[k].at[it], send_sem.at[it, k], recv_sem.at[k + 1, it], ps[k])
 
     def ag_copy(it, k):
-        ps, keep, _ = route(bits, peers, lax.rem(it, 2), d)
+        ps, keep, _ = route(bits, peers, it, d)
         u = unit_of(it)
         if k == 4:
             ref = w_out.at[u, core]
@@ -376,7 +377,7 @@
         return remote(src, ref, ag_send.at[it, k], ag_recv.at[it, k], ps[3 - k])
 
     def ag_local(it):
-        _, keep, _ = route(bits, peers, lax.rem(it, 2), d)
+        _, keep, _ = route(bits, peers, it, d)
         u = unit_of(it)
         return local(gs.at[u], w_out.at[u, core, pl.ds(keep[4], piece), :], ag_loc.at[it])
 
@@ -439,7 +440,7 @@
             @pl.when((j >= 0) & (j < nu))
             def _():
                 cs = lax.rem(j, slots)
-                _, keep, _ = route(bits, peers, lax.rem(j, 2), d)
+                _, keep, _ = route(bits, peers, j, d)
                 n = d >> (k + 1)
                 rows = pl.ds(keep[k + 1], n)
                 rs_copy(j, k).wait_recv()

time: 714 us -> 711 us (level)
  no operation moved by 1% of the time
where the time goes in v3:
time: 711 us; the launch traced here: 710 us
  Pallas kernels  710 us (100%)
    pallas_call x1, Pallas kernels, local_step(): call(functools.partial(backward, dm, scale, True), 7, [sds((nu, 2, d, f),...  346 us
    pallas_call x1, Pallas kernels, local_step(): call(functools.partial(backward, dm, scale, False), 5, [w_s], bwd_scratch...  185 us
    pallas_call x1, Pallas kernels, local_step(): call(functools.partial(second_forward, dm, scale, rho), 4, [z_s, v_s, a_s...  103 us
    pallas_call x1, Pallas kernels, local_step(): call(functools.partial(first_forward, dm), 4, [z_s, v_s, w_s, a_s, a_s],...  47 us
    pallas_call x1, Pallas kernels, local_step(): pl.pallas_call(functools.partial(finish, scale, f), grid=(nl, nf // 2), i...  28.9 us

profile of v3, /device:TPU:0, one launch (start us, length us, event | category | flops | bytes accessed | tf_op | source)
XLA Modules:
  0.0 710.4 jit_solution(17836079854689708401)
XLA Ops:
  0.6 47.0 %fwd_a.1 = (bf16[24,1568,256]{2,1,0:T(8,128)(2,1)}, bf16[24,2,768,256]{3,2,1,0:T(8,128)(2,1)}, f32[24,48,256]{2,1,0:T(8,128)}, bf16[1568,768]{1,0:T(8,128)(2,1)}, bf16[1568,768]{1,0:T(8,128)(2,1)}) custom-call(bf16[1568,768]{1,0:T(8,128)(2,1)} %bitcast.7, bf16[1568,768]{1,0:T(8,128)(2,1)} %bitcast.11, f32[2,768,3072]{2,1,0:T(8,128)} %wi_hbm.1, ...), custom_call_target="tpu_custom_call" | custom-call | tf_op jit(solution)/shard_map/fwd_a/pallas_call | solution.py:544
  47.6 184.9 %bwd_a.1.gs_hbm = f32[24,48,256]{2,1,0:T(8,128)} custom-call(bf16[1568,768]{1,0:T(8,128)(2,1)} %bitcast.8, bf16[1568,768]{1,0:T(8,128)(2,1)} %get-tuple-element.18.refs_1_, bf16[1568,768]{1,0:T(8,128)(2,1)} %get-tuple-element.19.refs_2_, bf16[24,1568,256]{2,1,0:T(8,128)(2,1)} %get-tuple-element.20.refs_3_, bf16[24,2,768,256]{3,2,1,0:T(8,128)(2,1)} %get-tuple-element.21.refs_4_), custom_call_target="tpu_custom_call" | custom-call | tf_op jit(solution)/shard_map/bwd_a/pallas_call | solution.py:556
  232.5 103.4 %fwd_b.1 = (bf16[24,1568,256]{2,1,0:T(8,128)(2,1)}, bf16[24,2,768,256]{3,2,1,0:T(8,128)(2,1)}, bf16[1568,768]{1,0:T(8,128)(2,1)}, bf16[1568,768]{1,0:T(8,128)(2,1)}, f32[8,128]{1,0:T(8,128)}) custom-call(f32[24,48,256]{2,1,0:T(8,128)} %bwd_a.1.gs_hbm, f32[24,48,256]{2,1,0:T(8,128)} %get-tuple-element.22.ws_hbm.refs_5_, bf16[1568,768]{1,0:T(8,128)(2,1)} %bitcast.9, ...), custom_call_target="tpu_custom_call" | custom-call | tf_op jit(solution)/shard_map/fwd_b/pallas_call | solution.py:558
  335.9 345.6 %bwd_b.1 = (f32[24,2,768,256]{3,2,1,0:T(8,128)}, f32[8,128]{1,0:T(8,128)}) custom-call(bf16[1568,768]{1,0:T(8,128)(2,1)} %bitcast.10, bf16[1568,768]{1,0:T(8,128)(2,1)} %get-tuple-element.23.refs_1_, bf16[1568,768]{1,0:T(8,128)(2,1)} %get-tuple-element.24.refs_2_, bf16[24,1568,256]{2,1,0:T(8,128)(2,1)} %get-tuple-element.25.refs_3_, ...), custom_call_target="tpu_custom_call" | custom-call | tf_op jit(solution)/shard_map/bwd_b/pallas_call | solution.py:564
  681.5 28.9 %finish.1 = (f32[2,768,3072]{2,1,0:T(8,128)}, f32[2,3072,768]{2,1,0:T(8,128)}, f32[1,1]{1,0:T(1,128)}) custom-call(f32[24,2,768,256]{3,2,1,0:T(8,128)} %get-tuple-element.28.w_ref, f32[8,128]{1,0:T(8,128)} %get-tuple-element.29.sq_ref), custom_call_target="tpu_custom_call" | custom-call | tf_op jit(solution)/shard_map/finish/pallas_call | solution.py:568

commit v4 on v3

--- a/solution.py
+++ b/solution.py
@@ -17,10 +17,10 @@
 GELU_C = math.sqrt(2.0 / math.pi)
 GELU_K = 0.044715
 VMEM_CAP = 67043328
-CORE_SLOTS = 14
-RS_LAG = (1, 4, 6, 9, 11)
-AG_LAG = (13, 15, 17, 20, 22)
-VG_LAG = (0, 2, 4, 6, 9, 10)
+CORE_SLOTS = 9
+RS_LAG = (0, 1, 4, 5, 6)
+AG_LAG = (1, 2, 4, 5)
+VG_LAG = (0, 2, 3, 5, 7, 9)
 
 
 def dot(lhs, rhs, dims=NN):
@@ -59,21 +59,73 @@
     b3 = jnp.where(parity == 0, by, bx)
     p1 = jnp.where(parity == 0, px, py)
     p3 = jnp.where(parity == 0, py, px)
+    step = rows // 16
     keep, send, base = [0], [], 0
     n = rows
     for bit in (b1, ba, b3, bb):
         n //= 2
-        keep.append(pl.multiple_of(base + bit * n, 8))
-        send.append(pl.multiple_of(base + (1 - bit) * n, 8))
+        keep.append(pl.multiple_of(base + bit * n, step))
+        send.append(pl.multiple_of(base + (1 - bit) * n, step))
         base = base + bit * n
-    return (p1, pa, p3, pb), keep, send
-
-
-def enter(peers):
+    return (p1, pa, p3, pb), keep, send, (b1, ba, b3, bb)
+
+
+def arrive(peers):
     barrier = pltpu.get_barrier_semaphore()
     for peer in peers:
         pl.semaphore_signal(barrier, inc=1, device_id=(peer,), device_id_type=MESH)
-    pl.semaphore_wait(barrier, len(peers))
+    return functools.partial(pl.semaphore_wait, barrier, len(peers))
+
+
+def others(bits, me_bits):
+    me = lax.axis_index("data")
+    out = []
+    for mask in range(1, 1 << len(me_bits)):
+        peer = me
+        for i, k in enumerate(me_bits):
+            if mask >> i & 1:
+                peer = peer + (1 << k) * (1 - 2 * bits[k])
+        out.append(peer)
+    return out
+
+
+def exchange_sum(buf, first, peers, send_sem, recv_sem, sem0):
+    copies = [remote(buf.at[first], buf.at[first + 1 + i], send_sem.at[sem0 + i], recv_sem.at[sem0 + i], peer) for i, peer in enumerate(peers)]
+    for cp in copies:
+        cp.start()
+    total = buf[first]
+    for i, cp in enumerate(copies):
+        cp.wait()
+        total = total + buf[first + 1 + i]
+    buf[first + len(peers) + 1] = total
+
+
+def gather_hops(bits, peers, unit, d, full, piece_src=None):
+    ps, keep, send, _ = route(bits, peers, unit, d)
+    piece = d // 16
+
+    def rows(base, n):
+        return full.at[pl.ds(base, n), :]
+
+    def hop(k, part, sem_s, sem_r):
+        peer = ps[3 - k] if k < 4 else peers[0]
+        if k == 0:
+            ref = rows(keep[4], piece)
+        elif part == 0:
+            ref = rows(keep[5 - k], piece << (k - 1))
+        else:
+            ref = rows(send[4 - k], piece << (k - 1))
+        src = piece_src if piece_src is not None and part == 0 and k <= 1 else ref
+        return remote(src, ref, sem_s, sem_r, peer)
+
+    def arrived(k, sem_s, sem_r):
+        ref = rows(send[3 - k], piece << k)
+        return remote(ref, ref, sem_s, sem_r, ps[3 - k])
+
+    def sent(sem_s, sem_r):
+        ref = rows(0, 15 * piece)
+        return remote(ref, ref, sem_s, sem_r, ps[0])
+    return hop, arrived, sent
 
 
 def remote(src, dst, send_sem, recv_sem, peer):
@@ -121,7 +173,7 @@
 
 
 def first_forward(dm, x_hbm, y_hbm, wi_hbm, wo_hbm, z_out, v_out, ws_out, h_out, q_out,
-                  h, yb, acc, ab, wi, wo, vb, zb, ws, load_sem, z_sem, v_sem, io_sem):
+                  h, yb, acc, ab, wi, wo, wt, vb, zb, ws, load_sem, z_sem, v_sem, io_sem):
     t, d, f, nf, nl = dm
     nu = nf * nl
     bits, peers = place()
@@ -164,19 +216,12 @@
         for j in range(2):
             cols = slice(j * f, (j + 1) * f)
             wot = wo[slot, cols, :].T
-            _, keep, _ = route(bits, peers, j, d)
+            _, keep, _, _ = route(bits, peers, j, d)
             rows = pl.ds(keep[4], piece)
             vb[slot, j, 0] = wi[slot, :, cols].astype(jnp.bfloat16)
             vb[slot, j, 1] = wot.astype(jnp.bfloat16)
-
-            @pl.when(bits[0] == 0)
-            def _():
-                ws[2 * p + j] = wi[slot, rows, cols]
-
-            @pl.when(bits[0] == 1)
-            def _():
-                wi[slot, :, cols] = wot
-                ws[2 * p + j] = wi[slot, rows, cols]
+            wt[...] = wot
+            ws[2 * p + j] = jnp.where(bits[0] == 0, wi[slot, rows, cols], wt[rows, :])
 
         fwd_pair(h, vb.at[slot], acc, ab, zb.at[slot], t, f)
         for cp in stores(p, slot):
@@ -212,7 +257,8 @@
     bits, peers = place()
     core = bits[0]
     piece = d // 16
-    enter(peers)
+    near, far = others(bits, (0, 1, 2)), others(bits, (3, 4))
+    wait_all = arrive(near + far)
     ins = (local(gs_hbm, gs, io_sem.at[0]), local(ws_hbm, ws, io_sem.at[1]), local(x_hbm, h, io_sem.at[2]), local(y_hbm, yb, io_sem.at[3]))
     for cp in ins:
         cp.start()
@@ -222,22 +268,21 @@
         g = gs[u] * scale
         return total + jnp.sum((g * g).reshape(piece // 8, 8, f // 128, 128), axis=(0, 2))
     nb[0] = lax.fori_loop(0, nu, square, jnp.zeros((8, 128), jnp.float32))
-    for k in range(5):
-        cp = remote(nb.at[2 * k], nb.at[2 * k + 1], nsend_sem.at[k], nrecv_sem.at[k], peers[k])
-        cp.start()
-        cp.wait()
-        nb[2 * k + 2] = nb[2 * k] + nb[2 * k + 1]
-    coef = rho / jnp.sqrt(jnp.sum(nb[10], keepdims=True))
+    wait_all()
+    exchange_sum(nb, 0, near, nsend_sem, nrecv_sem, 0)
+    exchange_sum(nb, 8, far, nsend_sem, nrecv_sem, 7)
+    coef = rho / jnp.sqrt(jnp.sum(nb[12], keepdims=True))
     ins[1].wait()
 
-    def hop(u, k):
-        ps, keep, _ = route(bits, peers, u, d)
-        if k == 4:
-            ref = vb.at[u, core]
-            return remote(ref, ref, send_sem.at[u, 4], recv_sem.at[u, 4], peers[0])
-        n = piece << k
-        ref = vb.at[u, core, pl.ds(pl.multiple_of(keep[4 - k], 16), n), :]
-        return remote(ref, ref, send_sem.at[u, k], recv_sem.at[u, k], ps[3 - k])
+    def hops(u):
+        return gather_hops(bits, peers, u, d, vb.at[u, core])
+
+    def sems(u, k):
+        return send_sem.at[u, 0 if k < 4 else 1], recv_sem.at[u, k]
+
+    def core_arrived(u):
+        ref = vb.at[u, 1 - core]
+        return remote(ref, ref, *sems(u, 4), peers[0])
 
     ins[2].wait()
     fwd_seed(h, acc, t)
@@ -249,22 +294,27 @@
     def _(it):
         @pl.when(it < nu)
         def _():
-            _, keep, _ = route(bits, peers, it, d)
+            _, keep, _, _ = route(bits, peers, it, d)
             new = ws[it] + coef * (gs[it] * scale)
-            vb[it, core, pl.ds(pl.multiple_of(keep[4], 16), piece), :] = new.astype(jnp.bfloat16)
-            hop(it, 0).start()
+            vb[it, core, pl.ds(keep[4], piece), :] = new.astype(jnp.bfloat16)
+            hop, _, _ = hops(it)
+            hop(0, 0, *sems(it, 0)).start()
+            hop(1, 0, *sems(it, 1)).start()
         for k in range(1, 5):
             u = it - VG_LAG[k]
 
             @pl.when((u >= 0) & (u < nu))
             def _():
-                hop(u, k - 1).wait_recv()
-                hop(u, k).start()
+                hop, arrived, _ = hops(u)
+                arrived(k - 1, *sems(u, k - 1)).wait_recv()
+                hop(k, 1, *sems(u, k)).start()
+                if k < 4:
+                    hop(k + 1, 0, *sems(u, k + 1)).start()
         u = it - VG_LAG[5]
 
         @pl.when(u >= 0)
         def _():
-            hop(u, 4).wait_recv()
+            core_arrived(u).wait_recv()
             local(vb.at[u], v_out.at[u], v_sem.at[u]).start()
 
         @pl.when((u >= 0) & (lax.rem(u, 2) == 1))
@@ -302,8 +352,8 @@
     @pl.loop(0, nu)
     def _(u):
         local(vb.at[u], v_out.at[u], v_sem.at[u]).wait()
-        for k in range(5):
-            hop(u, k).wait_send()
+        hops(u)[2](*sems(u, 0)).wait_send()
+        core_arrived(u).wait_send()
     for p in range(max(nu // 2 - 2, 0), nu // 2):
         z_store(p, p % 2).wait()
     out.wait()
@@ -326,7 +376,8 @@
     core = bits[0]
     piece = d // 16
     slots = cbuf.shape[0]
-    enter(peers)
+    near, far = others(bits, (0, 1, 2)), others(bits, (3, 4))
+    wait_all = arrive(near + far if final else peers)
 
     def unit_of(it):
         return (nl - 1 - it // nf) * nf + lax.rem(it, nf)
@@ -355,33 +406,63 @@
     transpose_into(tb.at[0], tmp, t)
     x_in = local(x_hbm, tmp, io_sem.at[1])
     x_in.start()
+    wait_all()
 
     def core_copy(it):
         slot = lax.rem(it, 2)
-        return remote(sbuf.at[slot], cbuf.at[lax.rem(it, slots)], csend_sem.at[slot], recv_sem.at[0, it], peers[0])
-
-    def rs_copy(it, k):
-        ps, _, send = route(bits, peers, it, d)
+        return remote(sbuf.at[slot], cbuf.at[lax.rem(it, slots)], csend_sem.at[slot], recv_sem.at[0, it, 0], peers[0])
+
+    def rs_sends(it, k):
+        ps, _, send, on = route(bits, peers, it, d)
         n = d >> (k + 1)
-        return remote(cbuf.at[lax.rem(it, slots), pl.ds(send[k], n), :], rbuf[k].at[it], send_sem.at[it, k], recv_sem.at[k + 1, it], ps[k])
-
-    def ag_copy(it, k):
-        ps, keep, _ = route(bits, peers, it, d)
-        u = unit_of(it)
-        if k == 4:
-            ref = w_out.at[u, core]
-            return remote(ref, ref, ag_send.at[it, 4], ag_recv.at[it, 4], peers[0])
-        n = piece << k
-        ref = w_out.at[u, core, pl.ds(keep[4 - k], n), :]
-        src = gs.at[u] if k == 0 else ref
-        return remote(src, ref, ag_send.at[it, k], ag_recv.at[it, k], ps[3 - k])
-
-    def ag_local(it):
-        _, keep, _ = route(bits, peers, it, d)
-        u = unit_of(it)
-        return local(gs.at[u], w_out.at[u, core, pl.ds(keep[4], piece), :], ag_loc.at[it])
-
-    n_it = nu + (AG_LAG[4] if final else RS_LAG[4])
+        cs = lax.rem(it, slots)
+
+        def part(off, m, sem):
+            return remote(cbuf.at[cs, pl.ds(send[k] + off, m), :], rbuf[k].at[it, pl.ds(off, m), :], send_sem.at[it], sem, ps[k])
+        if k == 3:
+            return [part(0, n, recv_sem.at[1, it, k])]
+        m = n // 2
+        step = d // 16
+        return [part(pl.multiple_of((1 - on[k + 1]) * m, step), m, recv_sem.at[1, it, k]),
+                part(pl.multiple_of(on[k + 1] * m, step), m, recv_sem.at[2, it, k])]
+
+    def rs_add(it, k, kept):
+        ps, keep, send, _ = route(bits, peers, it, d)
+        cs = lax.rem(it, slots)
+        if k == 3:
+            base, m = keep[4], d >> 4
+        else:
+            base, m = (keep[k + 2] if kept else send[k + 1]), d >> (k + 2)
+        here = rbuf[k].at[it, pl.ds(pl.multiple_of(base - keep[k + 1], d // 16), m), :]
+        mine = cbuf.at[cs, pl.ds(base, m), :]
+        remote(mine, here, send_sem.at[it], recv_sem.at[2 if kept else 1, it, k], ps[k]).wait_recv()
+        total = mine[...] + here[...]
+        if k == 3:
+            return total
+        mine[...] = total
+
+    def rs_sent(it):
+        ref = cbuf.at[lax.rem(it, slots), pl.ds(0, 15 * piece), :]
+        return remote(ref, ref, send_sem.at[it], recv_sem.at[1, it, 3], peers[0])
+
+    if final:
+        def hops(it):
+            u = unit_of(it)
+            return gather_hops(bits, peers, it, d, w_out.at[u, core], gs.at[u])
+
+        def sems(it, k):
+            return ag_send.at[it, 0 if k < 4 else 1], ag_recv.at[it, k]
+
+        def core_arrived(it):
+            ref = w_out.at[unit_of(it), 1 - core]
+            return remote(ref, ref, *sems(it, 4), peers[0])
+
+        def ag_local(it):
+            _, keep, _, _ = route(bits, peers, it, d)
+            u = unit_of(it)
+            return local(gs.at[u], w_out.at[u, core, pl.ds(keep[4], piece), :], ag_loc.at[it])
+
+    n_it = nu + RS_LAG[4] + (AG_LAG[3] if final else 0)
 
     @pl.loop(0, n_it)
     def _(it):
@@ -432,66 +513,67 @@
             cs = lax.rem(j0, slots)
             core_copy(j0).wait_recv()
             cbuf[cs] = cbuf[cs] + obuf[lax.rem(j0, 2)]
-            rs_copy(j0, 0).start()
+            for cp in rs_sends(j0, 0):
+                cp.start()
 
         for k in range(4):
             j = it - RS_LAG[k + 1]
 
             @pl.when((j >= 0) & (j < nu))
             def _():
-                cs = lax.rem(j, slots)
-                _, keep, _ = route(bits, peers, j, d)
-                n = d >> (k + 1)
-                rows = pl.ds(keep[k + 1], n)
-                rs_copy(j, k).wait_recv()
+                if k > 0:
+                    rs_add(j, k - 1, True)
                 if k < 3:
-                    cbuf[cs, rows, :] = cbuf[cs, rows, :] + rbuf[k][j]
-                    rs_copy(j, k + 1).start()
+                    rs_add(j, k, False)
+                    for cp in rs_sends(j, k + 1):
+                        cp.start()
                 else:
-                    total = cbuf[cs, rows, :] + rbuf[k][j]
+                    total = rs_add(j, k, False)
                     u = unit_of(j)
                     gs[u] = gs[u] - LEARN_RATE * (total * scale) if final else total
-                    for kk in range(4):
-                        rs_copy(j, kk).wait_send()
+                    rs_sent(j).wait_send()
 
                     @pl.when(j + slots < nu)
                     def _():
                         pl.semaphore_signal(credit, inc=1, device_id=(peers[0],), device_id_type=MESH)
                     if final:
                         ag_local(j).start()
-                        ag_copy(j, 0).start()
+                        hop, _, _ = hops(j)
+                        hop(0, 0, *sems(j, 0)).start()
+                        hop(1, 0, *sems(j, 1)).start()
         if final:
-            for k in range(4):
-                j = it - AG_LAG[k]
+            for k in range(1, 5):
+                j = it - RS_LAG[4] - AG_LAG[k - 1]
 
                 @pl.when((j >= 0) & (j < nu))
                 def _():
-                    ag_copy(j, k).wait_recv()
-                    if k == 0:
+                    hop, arrived, _ = hops(j)
+                    if k == 1:
                         ag_local(j).wait()
-                    ag_copy(j, k + 1).start()
-
-            @pl.when(it < 5)
-            def _():
-                for k in range(5):
-                    @pl.when(it == k)
-                    def _():
-                        cp = remote(nb.at[2 * k], nb.at[2 * k + 1], nsend_sem.at[k], nrecv_sem.at[k], peers[k])
-                        cp.start()
-                        cp.wait()
-                        nb[2 * k + 2] = nb[2 * k] + nb[2 * k + 1]
+                    arrived(k - 1, *sems(j, k - 1)).wait_recv()
+                    hop(k, 1, *sems(j, k)).start()
+                    if k < 4:
+                        hop(k + 1, 0, *sems(j, k + 1)).start()
+
+            @pl.when(it == 1)
+            def _():
+                exchange_sum(nb, 0, near, nsend_sem, nrecv_sem, 0)
+
+            @pl.when(it == 2)
+            def _():
+                exchange_sum(nb, 8, far, nsend_sem, nrecv_sem, 7)
 
     core_copy(nu - 2).wait_send()
     core_copy(nu - 1).wait_send()
     if final:
-        sq_cp = local(nb.at[10], sq_out, io_sem.at[3])
+        sq_cp = local(nb.at[12], sq_out, io_sem.at[3])
         sq_cp.start()
 
         @pl.loop(0, nu)
         def _(it):
-            ag_copy(it, 4).wait_recv()
-            for k in range(5):
-                ag_copy(it, k).wait_send()
+            core_arrived(it).wait_recv()
+            hops(it)[2](*sems(it, 0)).wait_send()
+            core_arrived(it).wait_send()
         sq_cp.wait()
     else:
         g_cp = local(gs, g_out, io_sem.at[0])
@@ -543,7 +625,7 @@
 
     z, v, ws, h1, q = call(
         functools.partial(first_forward, dm), 4, [z_s, v_s, w_s, a_s, a_s],
-        [V((t, d), bf), V((t, d), bf), V((t, d), f32), V((t, 2 * f), bf), V((2, d, 2 * f), f32), V((2, 2 * f, d), f32), V((2, 2, 2, d, f), bf), V((2, 2, t, f), bf),
+        [V((t, d), bf), V((t, d), bf), V((t, d), f32), V((t, 2 * f), bf), V((2, d, 2 * f), f32), V((2, 2 * f, d), f32), V((d, f), f32), V((2, 2, 2, d, f), bf), V((2, 2, t, f), bf),
          V((nu, piece, f), f32),
          DMA((2, 2)), DMA((2,)), DMA((2,)), DMA((2,))], "fwd_a")(x, y, w_in, w_out)
 
@@ -552,18 +634,18 @@
         V((t, d), bf), V((t, d), bf), V((2, d, t), bf), V((2, t, f), bf), V((t, d), f32), V((2, t, f), bf), V((2, 2, d, f), bf),
         V((slots, d, f), f32), V((2, d, f), f32), V((2, d, f), f32),
         V((nu, d // 2, f), f32), V((nu, d // 4, f), f32), V((nu, d // 8, f), f32), V((nu, d // 16, f), f32), V((nu, piece, f), f32),
-        DMA((2, 2)), DMA((4,)), DMA((2,)), DMA((nu, 4)), DMA((5, nu)), pltpu.SemaphoreType.REGULAR]
+        DMA((2, 2)), DMA((4,)), DMA((2,)), DMA((nu,)), DMA((3, nu, 4)), pltpu.SemaphoreType.REGULAR]
     (g,) = call(functools.partial(backward, dm, scale, False), 5, [w_s], bwd_scratch, "bwd_a", 0)(x, h1, q, z, v)
 
     z, v, h1, q, sq = call(
         functools.partial(second_forward, dm, scale, rho), 4, [z_s, v_s, a_s, a_s, sds((8, 128), f32)],
         [V((t, d), bf), V((t, d), bf), V((t, d), f32), V((t, 2 * f), bf), V((nu, piece, f), f32), V((nu, piece, f), f32), V((nu, 2, d, f), bf), V((2, 2, t, f), bf),
-         V((11, 8, 128), f32),
-         DMA((nu, 5)), DMA((nu, 5)), DMA((5,)), DMA((5,)), DMA((2,)), DMA((nu,)), DMA((4,))], "fwd_b", 1)(g, ws, x, y)
+         V((13, 8, 128), f32),
+         DMA((nu, 2)), DMA((nu, 5)), DMA((10,)), DMA((10,)), DMA((2,)), DMA((nu,)), DMA((4,))], "fwd_b", 1)(g, ws, x, y)
 
     w_new, sq = call(
         functools.partial(backward, dm, scale, True), 7, [sds((nu, 2, d, f), f32), sds((8, 128), f32)],
-        bwd_scratch + [V((11, 8, 128), f32), DMA((nu, 5)), DMA((nu, 5)), DMA((nu,)), DMA((5,)), DMA((5,))], "bwd_b", 2)(x, h1, q, z, v, ws, sq)
+        bwd_scratch + [V((13, 8, 128), f32), DMA((nu, 2)), DMA((nu, 5)), DMA((nu,)), DMA((10,)), DMA((10,))], "bwd_b", 2)(x, h1, q, z, v, ws, sq)
 
     new_in, new_out, loss = pl.pallas_call(
         functools.partial(finish, scale, f),

time: 711 us -> 654 us (0.920)
  Pallas kernels: 710 us -> 651 us
    pallas_call x1, Pallas kernels: 346 us -> 307 us  [local_step(): call(functools.partial(backward, dm, scale, True), 7, [sds((nu, 2, d, f),...]
    pallas_call x1, Pallas kernels: 185 us -> 172 us  [local_step(): call(functools.partial(backward, dm, scale, False), 5, [w_s], bwd_scratch...]
where the time goes in v4:
time: 654 us; the launch traced here: 652 us
  Pallas kernels  651 us (100%)
    pallas_call x1, Pallas kernels, local_step(): call(functools.partial(backward, dm, scale, True), 7, [sds((nu, 2, d, f),...  307 us
    pallas_call x1, Pallas kernels, local_step(): call(functools.partial(backward, dm, scale, False), 5, [w_s], bwd_scratch...  172 us
    pallas_call x1, Pallas kernels, local_step(): call(functools.partial(second_forward, dm, scale, rho), 4, [z_s, v_s, a_s...  103 us
    pallas_call x1, Pallas kernels, local_step(): call(functools.partial(first_forward, dm), 4, [z_s, v_s, w_s, a_s, a_s],...  40 us
    pallas_call x1, Pallas kernels, local_step(): pl.pallas_call(functools.partial(finish, scale, f), grid=(nl, nf // 2), i...  28.9 us

profile of v4, /device:TPU:0, one launch (start us, length us, event | category | flops | bytes accessed | tf_op | source)
XLA Modules:
  0.0 651.9 jit_solution(1123734447180162663)
XLA Ops:
  0.6 40.0 %fwd_a.1 = (bf16[24,1568,256]{2,1,0:T(8,128)(2,1)}, bf16[24,2,768,256]{3,2,1,0:T(8,128)(2,1)}, f32[24,48,256]{2,1,0:T(8,128)}, bf16[1568,768]{1,0:T(8,128)(2,1)}, bf16[1568,768]{1,0:T(8,128)(2,1)}) custom-call(bf16[1568,768]{1,0:T(8,128)(2,1)} %bitcast.7, bf16[1568,768]{1,0:T(8,128)(2,1)} %bitcast.11, f32[2,768,3072]{2,1,0:T(8,128)} %wi_hbm.1, ...), custom_call_target="tpu_custom_call" | custom-call | tf_op jit(solution)/shard_map/fwd_a/pallas_call | solution.py:626
  40.7 172.4 %bwd_a.1.gs_hbm = f32[24,48,256]{2,1,0:T(8,128)} custom-call(bf16[1568,768]{1,0:T(8,128)(2,1)} %bitcast.8, bf16[1568,768]{1,0:T(8,128)(2,1)} %get-tuple-element.18.refs_1_, bf16[1568,768]{1,0:T(8,128)(2,1)} %get-tuple-element.19.refs_2_, bf16[24,1568,256]{2,1,0:T(8,128)(2,1)} %get-tuple-element.20.refs_3_, bf16[24,2,768,256]{3,2,1,0:T(8,128)(2,1)} %get-tuple-element.21.refs_4_), custom_call_target="tpu_custom_call" | custom-call | tf_op jit(solution)/shard_map/bwd_a/pallas_call | solution.py:638
  213.0 102.8 %fwd_b.1 = (bf16[24,1568,256]{2,1,0:T(8,128)(2,1)}, bf16[24,2,768,256]{3,2,1,0:T(8,128)(2,1)}, bf16[1568,768]{1,0:T(8,128)(2,1)}, bf16[1568,768]{1,0:T(8,128)(2,1)}, f32[8,128]{1,0:T(8,128)}) custom-call(f32[24,48,256]{2,1,0:T(8,128)} %bwd_a.1.gs_hbm, f32[24,48,256]{2,1,0:T(8,128)} %get-tuple-element.22.ws_hbm.refs_5_, bf16[1568,768]{1,0:T(8,128)(2,1)} %bitcast.9, ...), custom_call_target="tpu_custom_call" | custom-call | tf_op jit(solution)/shard_map/fwd_b/pallas_call | solution.py:640
  315.8 307.1 %bwd_b.1 = (f32[24,2,768,256]{3,2,1,0:T(8,128)}, f32[8,128]{1,0:T(8,128)}) custom-call(bf16[1568,768]{1,0:T(8,128)(2,1)} %bitcast.10, bf16[1568,768]{1,0:T(8,128)(2,1)} %get-tuple-element.23.refs_1_, bf16[1568,768]{1,0:T(8,128)(2,1)} %get-tuple-element.24.refs_2_, bf16[24,1568,256]{2,1,0:T(8,128)(2,1)} %get-tuple-element.25.refs_3_, ...), custom_call_target="tpu_custom_call" | custom-call | tf_op jit(solution)/shard_map/bwd_b/pallas_call | solution.py:646
  622.9 28.9 %finish.1 = (f32[2,768,3072]{2,1,0:T(8,128)}, f32[2,3072,768]{2,1,0:T(8,128)}, f32[1,1]{1,0:T(1,128)}) custom-call(f32[24,2,768,256]{3,2,1,0:T(8,128)} %get-tuple-element.28.w_ref, f32[8,128]{1,0:T(8,128)} %get-tuple-element.29.sq_ref), custom_call_target="tpu_custom_call" | custom-call | tf_op jit(solution)/shard_map/finish/pallas_call | solution.py:650

commit v5 on v4

v5 whole, which is shorter than its diff:
```python
import math
import functools
import jax
import jax.numpy as jnp
from jax import lax
from jax.experimental import pallas as pl
from jax.experimental.pallas import tpu as pltpu
from jax.sharding import PartitionSpec as P

RHO_FRAC = 0.1
LEARN_RATE = 1.0
TILE_F = 256
MESH = pl.DeviceIdType.MESH
ANY = pl.BlockSpec(memory_space=pl.ANY)
NN = (((1,), (0,)), ((), ()))
NT = (((1,), (1,)), ((), ()))
GELU_C = math.sqrt(2.0 / math.pi)
GELU_K = 0.044715
VMEM_CAP = 67043328
CORE_SLOTS = 9
RS_LAG = (0, 1, 4, 5, 6)
AG_LAG = (1, 2, 4, 5)
VG_LAG = (0, 2, 3, 5, 7, 9)


def dot(lhs, rhs, dims=NN):
    return lax.dot_general(lhs, rhs, dims, preferred_element_type=jnp.float32)


def gelu_parts(z):
    sq = z * z
    th = jnp.tanh(GELU_C * (z + GELU_K * (sq * z)))
    cdf = 0.5 * (1.0 + th)
    return sq, th, cdf


def gelu(z):
    return z * gelu_parts(z)[2]


def gelu_and_grad(z):
    sq, th, cdf = gelu_parts(z)
    slope = cdf + (0.5 * z) * ((1.0 - th * th) * (GELU_C + (3.0 * GELU_K * GELU_C) * sq))
    return z * cdf, slope


def place(axis="data"):
    me = lax.axis_index(axis)
    bits = [lax.rem(lax.div(me, 1 << k), 2) for k in range(5)]
    peers = [me + (1 << k) * (1 - 2 * bits[k]) for k in range(5)]
    return bits, peers


def route(bits, peers, unit, rows):
    core, bx, by, ba, bb = bits
    parity = lax.rem(unit + core, 2)
    _, px, py, pa, pb = peers
    b1 = jnp.where(parity == 0, bx, by)
    b3 = jnp.where(parity == 0, by, bx)
    p1 = jnp.where(parity == 0, px, py)
    p3 = jnp.where(parity == 0, py, px)
    step = rows // 16
    keep, send, base = [0], [], 0
    n = rows
    for bit in (b1, ba, b3, bb):
        n //= 2
        keep.append(pl.multiple_of(base + bit * n, step))
        send.append(pl.multiple_of(base + (1 - bit) * n, step))
        base = base + bit * n
    return (p1, pa, p3, pb), keep, send, (b1, ba, b3, bb)


def arrive(peers):
    barrier = pltpu.get_barrier_semaphore()
    for peer in peers:
        pl.semaphore_signal(barrier, inc=1, device_id=(peer,), device_id_type=MESH)
    return functools.partial(pl.semaphore_wait, barrier, len(peers))


def others(bits, me_bits):
    me = lax.axis_index("data")
    out = []
    for mask in range(1, 1 << len(me_bits)):
        peer = me
        for i, k in enumerate(me_bits):
            if mask >> i & 1:
                peer = peer + (1 << k) * (1 - 2 * bits[k])
        out.append(peer)
    return out


def exchange_sum(buf, first, peers, send_sem, recv_sem, sem0):
    copies = [remote(buf.at[first], buf.at[first + 1 + i], send_sem.at[sem0 + i], recv_sem.at[sem0 + i], peer) for i, peer in enumerate(peers)]
    for cp in copies:
        cp.start()
    total = buf[first]
    for i, cp in enumerate(copies):
        cp.wait()
        total = total + buf[first + 1 + i]
    buf[first + len(peers) + 1] = total


def gather_hops(bits, peers, unit, d, full, piece_src=None):
    ps, keep, send, _ = route(bits, peers, unit, d)
    piece = d // 16

    def rows(base, n):
        return full.at[pl.ds(base, n), :]

    def hop(k, part, sem_s, sem_r):
        peer = ps[3 - k] if k < 4 else peers[0]
        if k == 0:
            ref = rows(keep[4], piece)
        elif part == 0:
            ref = rows(keep[5 - k], piece << (k - 1))
        else:
            ref = rows(send[4 - k], piece << (k - 1))
        src = piece_src if piece_src is not None and part == 0 and k <= 1 else ref
        return remote(src, ref, sem_s, sem_r, peer)

    def arrived(k, sem_s, sem_r):
        ref = rows(send[3 - k], piece << k)
        return remote(ref, ref, sem_s, sem_r, ps[3 - k])

    def sent(sem_s, sem_r):
        ref = rows(0, 15 * piece)
        return remote(ref, ref, sem_s, sem_r, ps[0])
    return hop, arrived, sent


def remote(src, dst, send_sem, recv_sem, peer):
    return pltpu.make_async_remote_copy(src_ref=src, dst_ref=dst, send_sem=send_sem, recv_sem=recv_sem, device_id=(peer,), device_id_type=MESH)


def local(src, dst, sem):
    return pltpu.make_async_copy(src, dst, sem)


def halves(t):
    return [(0, t // 2), (t // 2, t // 2)] if t % 32 == 0 else [(0, t)]


def transpose_into(dst, src, t):
    full = t // 128
    if full:
        @pl.loop(0, full)
        def _(i):
            lo = pl.multiple_of(i * 128, 128)
            dst[:, pl.ds(lo, 128)] = src[pl.ds(lo, 128), :].T
    if t % 128:
        dst[:, full * 128:t] = src[full * 128:t, :].T


def fwd_pair(h_ref, v_ref, acc_ref, a_ref, z_ref, t, f):
    for lo, n in halves(t):
        for j in range(2):
            z = dot(h_ref[lo:lo + n, :], v_ref[j, 0]).astype(jnp.bfloat16)
            z_ref[j, lo:lo + n, :] = z
            a_ref[j, lo:lo + n, :] = gelu(z.astype(jnp.float32)).astype(jnp.bfloat16)
    v_out = jnp.concatenate([v_ref[0, 1], v_ref[1, 1]], axis=1)
    for lo, n in halves(t):
        acc_ref[lo:lo + n, :] += dot(jnp.concatenate([a_ref[0, lo:lo + n, :], a_ref[1, lo:lo + n, :]], axis=1), v_out, NT)


def fwd_close(h_ref, acc_ref, t):
    for lo, n in halves(t):
        h_ref[lo:lo + n, :] = acc_ref[lo:lo + n, :].astype(jnp.bfloat16)


def fwd_seed(h_ref, acc_ref, t):
    for lo, n in halves(t):
        acc_ref[lo:lo + n, :] = h_ref[lo:lo + n, :].astype(jnp.float32)


def fold(v):
    r, c = v.shape
    return jnp.sum(v.reshape(r // 8, 8, c // 128, 128), axis=(0, 2))


def loss_close(h_ref, y_ref, acc_ref, t, total_ref):
    n = 112 if t % 112 == 0 else t
    total_ref[...] = jnp.zeros((8, 128), jnp.float32)

    @pl.loop(0, t // n)
    def _(i):
        rows = pl.ds(pl.multiple_of(i * n, n), n)
        e = acc_ref[rows, :].astype(jnp.bfloat16).astype(jnp.float32) - y_ref[rows, :].astype(jnp.float32)
        q = e.astype(jnp.bfloat16)
        h_ref[rows, :] = q
        acc_ref[rows, :] = q.astype(jnp.float32)
        total_ref[...] += fold(e * e)


def unit_of(it, nf, nl):
    return (nl - 1 - it // nf) * nf + lax.rem(it, nf)


def first_pass(dm, scale, x_hbm, y_hbm, wi_hbm, wo_hbm, z_out, v_out, ws_out, g_out, n_out,
               h, tmp, tb, eb, acc, wi, wo, wt, zb, vb, ws, cbuf, obuf, sbuf, r1, r2, r3, r4, gs, nb,
               load_sem, z_sem, v_sem, io_sem, csend_sem, send_sem, recv_sem, credit, nsend_sem, nrecv_sem):
    t, d, f, nf, nl = dm
    nu = nf * nl
    bits, peers = place()
    piece = d // 16
    near, far = others(bits, (0, 1, 2)), others(bits, (3, 4))
    wait_all = arrive(near + far)

    def loads(p, slot):
        layer, tile = p // (nf // 2), lax.rem(p, nf // 2)
        lo = pl.multiple_of(tile * 2 * f, 2 * f)
        return (local(wi_hbm.at[layer, :, pl.ds(lo, 2 * f)], wi.at[slot], load_sem.at[slot, 0]),
                local(wo_hbm.at[layer, pl.ds(lo, 2 * f), :], wo.at[slot], load_sem.at[slot, 1]))

    def stores(p, slot):
        two = pl.ds(2 * p, 2)
        return local(zb.at[slot], z_out.at[two], z_sem.at[slot]), local(vb.at[slot], v_out.at[two], v_sem.at[slot])

    x_in = local(x_hbm, h, io_sem.at[0])
    y_in = local(y_hbm, tmp, io_sem.at[1])
    x_in.start()
    for cp in loads(0, 0):
        cp.start()
    y_in.start()
    x_in.wait()
    fwd_seed(h, acc, t)

    @pl.loop(0, nu // 2)
    def _(p):
        slot = lax.rem(p, 2)
        for cp in loads(p, slot):
            cp.wait()

        @pl.when(p + 1 < nu // 2)
        def _():
            for cp in loads(p + 1, 1 - slot):
                cp.start()

        @pl.when(p >= 2)
        def _():
            for cp in stores(p - 2, slot):
                cp.wait()
        for j in range(2):
            cols = slice(j * f, (j + 1) * f)
            wot = wo[slot, cols, :].T
            _, keep, _, _ = route(bits, peers, j, d)
            rows = pl.ds(keep[4], piece)
            vb[slot, j, 0] = wi[slot, :, cols].astype(jnp.bfloat16)
            vb[slot, j, 1] = wot.astype(jnp.bfloat16)
            wt[...] = wot
            ws[2 * p + j] = jnp.where(bits[0] == 0, wi[slot, rows, cols], wt[rows, :])

        fwd_pair(h, vb.at[slot], acc, eb, zb.at[slot], t, f)
        for cp in stores(p, slot):
            cp.start()

        @pl.when(p == nf // 2 - 1)
        def _():
            fwd_close(h, acc, t)
            fwd_seed(h, acc, t)
            transpose_into(tb.at[0], h, t)

    np_ = nu // 2
    if np_ >= 2:
        for cp in stores(np_ - 2, np_ % 2):
            cp.wait()
    spare = np_ % 2

    def tiles(it, slot):
        u = unit_of(it, nf, nl)
        return (local(z_out.at[u], zb.at[spare, slot], load_sem.at[slot, 0]), local(v_out.at[u], vb.at[spare, slot], load_sem.at[slot, 1]))
    for cp in tiles(0, 0):
        cp.start()
    ws_cp = local(ws, ws_out, io_sem.at[2])
    ws_cp.start()
    y_in.wait()
    loss_close(h, tmp, acc, t, nb.at[0])
    transpose_into(tb.at[1], h, t)
    x_again = local(x_hbm, tmp, io_sem.at[1])
    x_again.start()
    for cp in stores(np_ - 1, (np_ - 1) % 2):
        cp.wait()
    wait_all()
    nb[0] = jnp.zeros((8, 128), jnp.float32)

    def on_total(j, u, total):
        gs[u] = total
        g = total * scale
        nb[0] += fold(g * g)

    backward_phase(dm, bits, peers, h, tmp, tb, eb, acc, zb.at[spare], vb.at[spare], cbuf, obuf, sbuf, (r1, r2, r3, r4),
                   csend_sem, send_sem, recv_sem, credit, tiles, x_again.wait, on_total)
    g_cp = local(gs, g_out, io_sem.at[0])
    g_cp.start()
    exchange_sum(nb, 0, near, nsend_sem, nrecv_sem, 0)
    exchange_sum(nb, 8, far, nsend_sem, nrecv_sem, 7)
    n_cp = local(nb.at[12], n_out, io_sem.at[1])
    n_cp.start()
    ws_cp.wait()
    g_cp.wait()
    n_cp.wait()


def second_forward(dm, scale, rho, gs_hbm, ws_hbm, n_hbm, x_hbm, y_hbm, z_out, v_out, h_out, q_out, sq_out,
                   h, yb, acc, ab, gs, ws, vb, zb, nb, send_sem, recv_sem, z_sem, v_sem, io_sem):
    t, d, f, nf, nl = dm
    nu = nf * nl
    bits, peers = place()
    core = bits[0]
    piece = d // 16
    wait_all = arrive(peers)
    ins = (local(gs_hbm, gs, io_sem.at[0]), local(ws_hbm, ws, io_sem.at[1]), local(x_hbm, h, io_sem.at[2]), local(y_hbm, yb, io_sem.at[3]))
    n_in = local(n_hbm, nb, io_sem.at[4])
    n_in.start()
    for cp in ins:
        cp.start()
    n_in.wait()
    coef = rho / jnp.sqrt(jnp.sum(nb[...], keepdims=True))
    ins[0].wait()
    ins[1].wait()
    wait_all()

    def hops(u):
        return gather_hops(bits, peers, u, d, vb.at[u, core])

    def sems(u, k):
        return send_sem.at[u, 0 if k < 4 else 1], recv_sem.at[u, k]

    def core_arrived(u):
        ref = vb.at[u, 1 - core]
        return remote(ref, ref, *sems(u, 4), peers[0])

    ins[2].wait()
    fwd_seed(h, acc, t)

    def z_store(p, slot):
        return local(zb.at[slot], z_out.at[pl.ds(2 * p, 2)], z_sem.at[slot])

    @pl.loop(0, nu + VG_LAG[5])
    def _(it):
        @pl.when(it < nu)
        def _():
            _, keep, _, _ = route(bits, peers, it, d)
            new = ws[it] + coef * (gs[it] * scale)
            vb[it, core, pl.ds(keep[4], piece), :] = new.astype(jnp.bfloat16)
            hop, _, _ = hops(it)
            hop(0, 0, *sems(it, 0)).start()
            hop(1, 0, *sems(it, 1)).start()
        for k in range(1, 5):
            u = it - VG_LAG[k]

            @pl.when((u >= 0) & (u < nu))
            def _():
                hop, arrived, _ = hops(u)
                arrived(k - 1, *sems(u, k - 1)).wait_recv()
                hop(k, 1, *sems(u, k)).start()
                if k < 4:
                    hop(k + 1, 0, *sems(u, k + 1)).start()
        u = it - VG_LAG[5]

        @pl.when(u >= 0)
        def _():
            core_arrived(u).wait_recv()
            local(vb.at[u], v_out.at[u], v_sem.at[u]).start()

        @pl.when((u >= 0) & (lax.rem(u, 2) == 1))
        def _():
            p = u // 2
            slot = lax.rem(p, 2)

            @pl.when(p >= 2)
            def _():
                z_store(p - 2, slot).wait()
            fwd_pair(h, vb.at[pl.ds(2 * p, 2)], acc, ab, zb.at[slot], t, f)
            z_store(p, slot).start()

            @pl.when(p == nf // 2 - 1)
            def _():
                fwd_close(h, acc, t)
                fwd_seed(h, acc, t)
                out = local(h, h_out, io_sem.at[0])
                out.start()
                out.wait()

    ins[3].wait()
    loss_close(h, yb, acc, t, nb)
    out = local(h, q_out, io_sem.at[0])
    sq = local(nb, sq_out, io_sem.at[1])
    out.start()
    sq.start()

    @pl.loop(0, nu)
    def _(u):
        local(vb.at[u], v_out.at[u], v_sem.at[u]).wait()
        hops(u)[2](*sems(u, 0)).wait_send()
        core_arrived(u).wait_send()
    for p in range(max(nu // 2 - 2, 0), nu // 2):
        z_store(p, p % 2).wait()
    out.wait()
    sq.wait()


def backward_phase(dm, bits, peers, q, tmp, tb, eb, acc, zb, vb, cbuf, obuf, sbuf, rbuf, csend_sem, send_sem, recv_sem, credit,
                   tiles, x_ready, on_total, extra_its=0, extra=None):
    t, d, f, nf, nl = dm
    nu = nf * nl
    core = bits[0]
    piece = d // 16
    slots = cbuf.shape[0]

    def core_copy(it):
        slot = lax.rem(it, 2)
        return remote(sbuf.at[slot], cbuf.at[lax.rem(it, slots)], csend_sem.at[slot], recv_sem.at[0, it, 0], peers[0])

    def rs_sends(it, k):
        ps, _, send, on = route(bits, peers, it, d)
        n = d >> (k + 1)
        cs = lax.rem(it, slots)

        def part(off, m, sem):
            return remote(cbuf.at[cs, pl.ds(send[k] + off, m), :], rbuf[k].at[it, pl.ds(off, m), :], send_sem.at[it], sem, ps[k])
        if k == 3:
            return [part(0, n, recv_sem.at[1, it, k])]
        m = n // 2
        return [part(pl.multiple_of((1 - on[k + 1]) * m, piece), m, recv_sem.at[1, it, k]),
                part(pl.multiple_of(on[k + 1] * m, piece), m, recv_sem.at[2, it, k])]

    def rs_add(it, k, kept):
        ps, keep, send, _ = route(bits, peers, it, d)
        cs = lax.rem(it, slots)
        if k == 3:
            base, m = keep[4], d >> 4
        else:
            base, m = (keep[k + 2] if kept else send[k + 1]), d >> (k + 2)
        here = rbuf[k].at[it, pl.ds(pl.multiple_of(base - keep[k + 1], piece), m), :]
        mine = cbuf.at[cs, pl.ds(base, m), :]
        remote(mine, here, send_sem.at[it], recv_sem.at[2 if kept else 1, it, k], ps[k]).wait_recv()
        total = mine[...] + here[...]
        if k == 3:
            return total
        mine[...] = total

    def rs_sent(it):
        ref = cbuf.at[lax.rem(it, slots), pl.ds(0, 15 * piece), :]
        return remote(ref, ref, send_sem.at[it], recv_sem.at[1, it, 3], peers[0])

    @pl.loop(0, nu + RS_LAG[4] + extra_its)
    def _(it):
        @pl.when(it == nf)
        def _():
            fwd_close(q, acc, t)
            transpose_into(tb.at[1], q, t)
            x_ready()
            transpose_into(tb.at[0], tmp, t)

        @pl.when(it < nu)
        def _():
            slot = lax.rem(it, 2)
            for cp in tiles(it, slot):
                cp.wait()

            @pl.when(it + 1 < nu)
            def _():
                for cp in tiles(it + 1, 1 - slot):
                    cp.start()
            for lo, n in halves(t):
                back = dot(q[lo:lo + n, :], vb[slot, 1])
                a, slope = gelu_and_grad(zb[slot, lo:lo + n, :].astype(jnp.float32))
                eb[1, lo:lo + n, :] = a.astype(jnp.bfloat16)
                eb[0, lo:lo + n, :] = (back * slope).astype(jnp.bfloat16)

            @pl.when(it >= 2)
            def _():
                core_copy(it - 2).wait_send()
            sbuf[slot] = dot(tb[1 - core], eb[1 - core])

            @pl.when(it >= slots)
            def _():
                pl.semaphore_wait(credit, 1)
            core_copy(it).start()
            obuf[slot] = dot(tb[core], eb[core])

            @pl.when(it < nf)
            def _():
                for lo, n in halves(t):
                    acc[lo:lo + n, :] += dot(eb[0, lo:lo + n, :], vb[slot, 0], NT)

        j0 = it - RS_LAG[0]

        @pl.when((j0 >= 0) & (j0 < nu))
        def _():
            cs = lax.rem(j0, slots)
            core_copy(j0).wait_recv()
            cbuf[cs] = cbuf[cs] + obuf[lax.rem(j0, 2)]
            for cp in rs_sends(j0, 0):
                cp.start()

        for k in range(4):
            j = it - RS_LAG[k + 1]

            @pl.when((j >= 0) & (j < nu))
            def _():
                if k > 0:
                    rs_add(j, k - 1, True)
                total = rs_add(j, k, False)
                if k < 3:
                    for cp in rs_sends(j, k + 1):
                        cp.start()
                else:
                    on_total(j, unit_of(j, nf, nl), total)
                    rs_sent(j).wait_send()

                    @pl.when(j + slots < nu)
                    def _():
                        pl.semaphore_signal(credit, inc=1, device_id=(peers[0],), device_id_type=MESH)
        if extra is not None:
            extra(it)

    core_copy(nu - 2).wait_send()
    core_copy(nu - 1).wait_send()


def second_backward(dm, scale, x_hbm, h_hbm, q_hbm, z_hbm, v_hbm, ws_hbm, sq_hbm, w_out, sq_out,
                    q, tmp, tb, eb, acc, zb, vb, cbuf, obuf, sbuf, r1, r2, r3, r4, gs,
                    load_sem, io_sem, csend_sem, send_sem, recv_sem, credit, nb, ag_send, ag_recv, ag_loc, nsend_sem, nrecv_sem):
    t, d, f, nf, nl = dm
    nu = nf * nl
    bits, peers = place()
    core = bits[0]
    piece = d // 16
    near, far = others(bits, (0, 1, 2)), others(bits, (3, 4))
    wait_all = arrive(near + far)

    def tiles(it, slot):
        u = unit_of(it, nf, nl)
        return local(z_hbm.at[u], zb.at[slot], load_sem.at[slot, 0]), local(v_hbm.at[u], vb.at[slot], load_sem.at[slot, 1])

    q_in = local(q_hbm, q, io_sem.at[0])
    h_in = local(h_hbm, tmp, io_sem.at[1])
    ws_in = local(ws_hbm, gs, io_sem.at[2])
    sq_in = local(sq_hbm, nb.at[0], io_sem.at[3])
    q_in.start()
    for cp in tiles(0, 0):
        cp.start()
    for cp in (h_in, ws_in, sq_in):
        cp.start()
    q_in.wait()
    fwd_seed(q, acc, t)
    transpose_into(tb.at[1], q, t)
    h_in.wait()
    transpose_into(tb.at[0], tmp, t)
    x_in = local(x_hbm, tmp, io_sem.at[1])
    x_in.start()
    ws_in.wait()
    sq_in.wait()
    wait_all()

    def hops(it):
        return gather_hops(bits, peers, it, d, w_out.at[unit_of(it, nf, nl), core], gs.at[unit_of(it, nf, nl)])

    def sems(it, k):
        return ag_send.at[it, 0 if k < 4 else 1], ag_recv.at[it, k]

    def core_arrived(it):
        ref = w_out.at[unit_of(it, nf, nl), 1 - core]
        return remote(ref, ref, *sems(it, 4), peers[0])

    def ag_local(it):
        _, keep, _, _ = route(bits, peers, it, d)
        u = unit_of(it, nf, nl)
        return local(gs.at[u], w_out.at[u, core, pl.ds(keep[4], piece), :], ag_loc.at[it])

    def on_total(j, u, total):
        gs[u] = gs[u] - LEARN_RATE * (total * scale)
        ag_local(j).start()
        hop, _, _ = hops(j)
        hop(0, 0, *sems(j, 0)).start()
        hop(1, 0, *sems(j, 1)).start()

    def extra(it):
        for k in range(1, 5):
            j = it - RS_LAG[4] - AG_LAG[k - 1]

            @pl.when((j >= 0) & (j < nu))
            def _():
                hop, arrived, _ = hops(j)
                if k == 1:
                    ag_local(j).wait()
                arrived(k - 1, *sems(j, k - 1)).wait_recv()
                hop(k, 1, *sems(j, k)).start()
                if k < 4:
                    hop(k + 1, 0, *sems(j, k + 1)).start()

        @pl.when(it == 1)
        def _():
            exchange_sum(nb, 0, near, nsend_sem, nrecv_sem, 0)

        @pl.when(it == 2)
        def _():
            exchange_sum(nb, 8, far, nsend_sem, nrecv_sem, 7)

    backward_phase(dm, bits, peers, q, tmp, tb, eb, acc, zb, vb, cbuf, obuf, sbuf, (r1, r2, r3, r4),
                   csend_sem, send_sem, recv_sem, credit, tiles, x_in.wait, on_total, AG_LAG[3], extra)
    sq_cp = local(nb.at[12], sq_out, io_sem.at[3])
    sq_cp.start()

    @pl.loop(0, nu)
    def _(it):
        core_arrived(it).wait_recv()
        hops(it)[2](*sems(it, 0)).wait_send()
        core_arrived(it).wait_send()
    sq_cp.wait()


def finish(scale, w_ref, sq_ref, in_ref, out_ref, loss_ref):
    in_ref[0] = w_ref[0, 0]
    out_ref[0] = w_ref[0, 1].T
    loss_ref[0, 0] = 0.5 * (jnp.sum(sq_ref[...]) * scale)


def sds(shape, dtype):
    return jax.ShapeDtypeStruct(shape, dtype)


def call(kernel, n_in, outs, scratch, name, collective_id=None):
    params = dict(vmem_limit_bytes=VMEM_CAP)
    if collective_id is not None:
        params.update(collective_id=collective_id, has_side_effects=True)
    return pl.pallas_call(
        kernel,
        out_shape=outs,
        in_specs=[ANY] * n_in,
        out_specs=[ANY] * len(outs),
        scratch_shapes=scratch,
        compiler_params=pltpu.CompilerParams(**params),
        name=name,
    )


def local_step(n_dev, tile_f, x_loc, y_loc, w_in, w_out):
    nl, d, ff = w_in.shape
    f = tile_f
    nf = ff // f
    nu = nl * nf
    t = x_loc.shape[0] * x_loc.shape[1]
    piece = d // 16
    dm = (t, d, f, nf, nl)
    scale = 1.0 / (t * n_dev * d)
    rho = RHO_FRAC * math.sqrt(nl * (d + ff))
    bf, f32 = jnp.bfloat16, jnp.float32
    V, DMA = pltpu.VMEM, pltpu.SemaphoreType.DMA
    x = x_loc.transpose(1, 0, 2).reshape(t, d)
    y = y_loc.transpose(1, 0, 2).reshape(t, d)
    z_s, v_s, w_s, a_s = sds((nu, t, f), bf), sds((nu, 2, d, f), bf), sds((nu, piece, f), f32), sds((t, d), bf)

    REG = pltpu.SemaphoreType.REGULAR
    slots = min(CORE_SLOTS, nu)
    n_s = sds((8, 128), f32)
    reduce_bufs = [V((slots, d, f), f32), V((2, d, f), f32), V((2, d, f), f32),
                   V((nu, d // 2, f), f32), V((nu, d // 4, f), f32), V((nu, d // 8, f), f32), V((nu, d // 16, f), f32), V((nu, piece, f), f32)]
    acts = [V((t, d), bf), V((t, d), bf), V((2, d, t), bf), V((2, t, f), bf), V((t, d), f32)]

    z, v, ws, g, norm = call(
        functools.partial(first_pass, dm, scale), 4, [z_s, v_s, w_s, w_s, n_s],
        acts + [V((2, d, 2 * f), f32), V((2, 2 * f, d), f32), V((d, f), f32), V((2, 2, t, f), bf), V((2, 2, 2, d, f), bf), V((nu, piece, f), f32)]
        + reduce_bufs + [V((13, 8, 128), f32), DMA((2, 2)), DMA((2,)), DMA((2,)), DMA((3,)), DMA((2,)), DMA((nu,)), DMA((3, nu, 4)), REG, DMA((10,)), DMA((10,))],
        "pass_a", 0)(x, y, w_in, w_out)

    z, v, h1, q, sq = call(
        functools.partial(second_forward, dm, scale, rho), 5, [z_s, v_s, a_s, a_s, n_s],
        [V((t, d), bf), V((t, d), bf), V((t, d), f32), V((2, t, f), bf), V((nu, piece, f), f32), V((nu, piece, f), f32), V((nu, 2, d, f), bf), V((2, 2, t, f), bf),
         V((8, 128), f32), DMA((nu, 2)), DMA((nu, 5)), DMA((2,)), DMA((nu,)), DMA((5,))], "fwd_b", 1)(g, ws, norm, x, y)

    w_new, sq = call(
        functools.partial(second_backward, dm, scale), 7, [sds((nu, 2, d, f), f32), n_s],
        acts + [V((2, t, f), bf), V((2, 2, d, f), bf)] + reduce_bufs + [DMA((2, 2)), DMA((4,)), DMA((2,)), DMA((nu,)), DMA((3, nu, 4)), REG,
         V((13, 8, 128), f32), DMA((nu, 2)), DMA((nu, 5)), DMA((nu,)), DMA((10,)), DMA((10,))], "bwd_b", 2)(x, h1, q, z, v, ws, sq)

    new_in, new_out, loss = pl.pallas_call(
        functools.partial(finish, scale),
        grid=(nl, nf),
        in_specs=[pl.BlockSpec((1, 2, d, f), lambda i, j: (i * nf + j, 0, 0, 0)), pl.BlockSpec((8, 128), lambda i, j: (0, 0))],
        out_specs=[pl.BlockSpec((1, d, f), lambda i, j: (i, 0, j)), pl.BlockSpec((1, f, d), lambda i, j: (i, j, 0)),
                   pl.BlockSpec((1, 1), lambda i, j: (0, 0), memory_space=pltpu.SMEM)],
        out_shape=[sds((nl, d, ff), f32), sds((nl, ff, d), f32), sds((1, 1), f32)],
        compiler_params=pltpu.CompilerParams(vmem_limit_bytes=VMEM_CAP),
        name="finish")(w_new, sq)
    return new_in, new_out, loss.reshape(())


def solution(mesh):
    step = functools.partial(local_step, mesh.shape["data"], TILE_F)
    return jax.shard_map(step, mesh=mesh, in_specs=(P("data"), P("data"), P(), P()), out_specs=(P(), P(), P()), check_vma=False)
```

time: 654 us -> 664 us (1.015)
  Pallas kernels: 651 us -> 662 us
    pallas_call x5 -> x4, Pallas kernels: 651 us -> 662 us  [the longest x1 308 us: local_step(): call(functools.partial(second_backward, dm, scale), 7, [sds((nu, 2, d, f)...]
where the time goes in v5:
time: 664 us; the launch traced here: 663 us
  Pallas kernels  662 us (100%)
    pallas_call x1, Pallas kernels, local_step(): call(functools.partial(second_backward, dm, scale), 7, [sds((nu, 2, d, f)...  308 us
    pallas_call x1, Pallas kernels, local_step(): call(functools.partial(first_pass, dm, scale), 4, [z_s, v_s, w_s, w_s, n_...  225 us
    pallas_call x1, Pallas kernels, local_step(): call(functools.partial(second_forward, dm, scale, rho), 5, [z_s, v_s, a_s...  94.1 us
    pallas_call x1, Pallas kernels, local_step(): pl.pallas_call(functools.partial(finish, scale), grid=(nl, nf), in_specs=...  34.7 us

profile of v5, /device:TPU:0, one launch (start us, length us, event | category | flops | bytes accessed | tf_op | source)
XLA Modules:
  0.0 662.5 jit_solution(3343401127981179232)
XLA Ops:
  0.6 225.3 %pass_a.1 = (bf16[24,1568,256]{2,1,0:T(8,128)(2,1)}, bf16[24,2,768,256]{3,2,1,0:T(8,128)(2,1)}, f32[24,48,256]{2,1,0:T(8,128)}, f32[24,48,256]{2,1,0:T(8,128)}, f32[8,128]{1,0:T(8,128)}) custom-call(bf16[1568,768]{1,0:T(8,128)(2,1)} %bitcast.7, bf16[1568,768]{1,0:T(8,128)(2,1)} %bitcast.10, f32[2,768,3072]{2,1,0:T(8,128)} %wi_hbm.1, f32[2,3072,768]{2,1,0:T(8,128)} %wo_hbm.1), custom_call_target="tpu_custom_call" | custom-call | tf_op jit(solution)/shard_map/pass_a/pallas_call | solution.py:662
  226.0 94.1 %fwd_b.1 = (bf16[24,1568,256]{2,1,0:T(8,128)(2,1)}, bf16[24,2,768,256]{3,2,1,0:T(8,128)(2,1)}, bf16[1568,768]{1,0:T(8,128)(2,1)}, bf16[1568,768]{1,0:T(8,128)(2,1)}, f32[8,128]{1,0:T(8,128)}) custom-call(f32[24,48,256]{2,1,0:T(8,128)} %get-tuple-element.16.gs_hbm, f32[24,48,256]{2,1,0:T(8,128)} %get-tuple-element.17.ws_hbm, ...), custom_call_target="tpu_custom_call" | custom-call | tf_op jit(solution)/shard_map/fwd_b/pallas_call | solution.py:668
  320.1 307.7 %bwd_b.1 = (f32[24,2,768,256]{3,2,1,0:T(8,128)}, f32[8,128]{1,0:T(8,128)}) custom-call(bf16[1568,768]{1,0:T(8,128)(2,1)} %bitcast.9, bf16[1568,768]{1,0:T(8,128)(2,1)} %get-tuple-element.19.h_hbm, bf16[1568,768]{1,0:T(8,128)(2,1)} %get-tuple-element.20.q_hbm, bf16[24,1568,256]{2,1,0:T(8,128)(2,1)} %get-tuple-element.21.z_hbm, ...), custom_call_target="tpu_custom_call" | custom-call | tf_op jit(solution)/shard_map/bwd_b/pallas_call | solution.py:673
  627.8 34.7 %finish.1 = (f32[2,768,3072]{2,1,0:T(8,128)}, f32[2,3072,768]{2,1,0:T(8,128)}, f32[1,1]{1,0:T(1,128)}) custom-call(f32[24,2,768,256]{3,2,1,0:T(8,128)} %get-tuple-element.24.w_ref, f32[8,128]{1,0:T(8,128)} %get-tuple-element.25.sq_ref), custom_call_target="tpu_custom_call" | custom-call | tf_op jit(solution)/shard_map/finish/pallas_call | solution.py:678

commit v6 on v5

--- a/solution.py
+++ b/solution.py
@@ -18,8 +18,9 @@
 GELU_K = 0.044715
 VMEM_CAP = 67043328
 CORE_SLOTS = 9
-RS_LAG = (0, 1, 4, 5, 6)
-AG_LAG = (1, 2, 4, 5)
+LAG_A = (0, 1, 4, 5, 7)
+LAG_B = (0, 1, 4, 6, 7)
+AG_LAG = (2, 3, 5, 6)
 VG_LAG = (0, 2, 3, 5, 7, 9)
 
 
@@ -53,21 +54,20 @@
 
 def route(bits, peers, unit, rows):
     core, bx, by, ba, bb = bits
-    parity = lax.rem(unit + core, 2)
     _, px, py, pa, pb = peers
-    b1 = jnp.where(parity == 0, bx, by)
-    b3 = jnp.where(parity == 0, by, bx)
-    p1 = jnp.where(parity == 0, px, py)
-    p3 = jnp.where(parity == 0, py, px)
+    swap = lax.rem(unit + core, 2) == 1
+    b1, p1 = jnp.where(swap, by, bx), jnp.where(swap, py, px)
+    b3, p3 = jnp.where(swap, bx, by), jnp.where(swap, px, py)
+    axes = (b1, ba, b3, bb)
     step = rows // 16
     keep, send, base = [0], [], 0
     n = rows
-    for bit in (b1, ba, b3, bb):
+    for bit in axes:
         n //= 2
         keep.append(pl.multiple_of(base + bit * n, step))
         send.append(pl.multiple_of(base + (1 - bit) * n, step))
         base = base + bit * n
-    return (p1, pa, p3, pb), keep, send, (b1, ba, b3, bb)
+    return (p1, pa, p3, pb), keep, send, axes
 
 
 def arrive(peers):
@@ -156,10 +156,10 @@
         for j in range(2):
             z = dot(h_ref[lo:lo + n, :], v_ref[j, 0]).astype(jnp.bfloat16)
             z_ref[j, lo:lo + n, :] = z
-            a_ref[j, lo:lo + n, :] = gelu(z.astype(jnp.float32)).astype(jnp.bfloat16)
+            a_ref[lo:lo + n, j * f:(j + 1) * f] = gelu(z.astype(jnp.float32)).astype(jnp.bfloat16)
     v_out = jnp.concatenate([v_ref[0, 1], v_ref[1, 1]], axis=1)
     for lo, n in halves(t):
-        acc_ref[lo:lo + n, :] += dot(jnp.concatenate([a_ref[0, lo:lo + n, :], a_ref[1, lo:lo + n, :]], axis=1), v_out, NT)
+        acc_ref[lo:lo + n, :] += dot(a_ref[lo:lo + n, :], v_out, NT)
 
 
 def fwd_close(h_ref, acc_ref, t):
@@ -174,20 +174,27 @@
 
 def fold(v):
     r, c = v.shape
-    return jnp.sum(v.reshape(r // 8, 8, c // 128, 128), axis=(0, 2))
-
-
-def loss_close(h_ref, y_ref, acc_ref, t, total_ref):
-    n = 112 if t % 112 == 0 else t
-    total_ref[...] = jnp.zeros((8, 128), jnp.float32)
-
-    @pl.loop(0, t // n)
-    def _(i):
-        rows = pl.ds(pl.multiple_of(i * n, n), n)
+    rows = jnp.sum(v.reshape(r // 8, 8, c), axis=0)
+    return sum(rows[:, lo:lo + 128] for lo in range(0, c, 128))
+
+
+def loss_close(h_ref, y_ref, acc_ref, t, d, total_ref=None):
+    def rows_of(rows):
         e = acc_ref[rows, :].astype(jnp.bfloat16).astype(jnp.float32) - y_ref[rows, :].astype(jnp.float32)
         q = e.astype(jnp.bfloat16)
         h_ref[rows, :] = q
         acc_ref[rows, :] = q.astype(jnp.float32)
+        return e
+    if total_ref is None:
+        for lo, n in halves(t):
+            rows_of(slice(lo, lo + n))
+        return
+    n = 112 if t % 112 == 0 else t
+    total_ref[...] = jnp.zeros((8, 128), jnp.float32)
+
+    @pl.loop(0, t // n)
+    def _(i):
+        e = rows_of(pl.ds(pl.multiple_of(i * n, n), n))
         total_ref[...] += fold(e * e)
 
 
@@ -196,7 +203,7 @@
 
 
 def first_pass(dm, scale, x_hbm, y_hbm, wi_hbm, wo_hbm, z_out, v_out, ws_out, g_out, n_out,
-               h, tmp, tb, eb, acc, wi, wo, wt, zb, vb, ws, cbuf, obuf, sbuf, r1, r2, r3, r4, gs, nb,
+               h, tmp, tb, eb, acc, ab, wi, wo, zb, vb, ws, cbuf, obuf, sbuf, r1, r2, r3, r4, gs, nb,
                load_sem, z_sem, v_sem, io_sem, csend_sem, send_sem, recv_sem, credit, nsend_sem, nrecv_sem):
     t, d, f, nf, nl = dm
     nu = nf * nl
@@ -242,14 +249,14 @@
         for j in range(2):
             cols = slice(j * f, (j + 1) * f)
             wot = wo[slot, cols, :].T
-            _, keep, _, _ = route(bits, peers, j, d)
+            _, keep, _, _ = route(bits, peers, 2 * p + j, d)
             rows = pl.ds(keep[4], piece)
             vb[slot, j, 0] = wi[slot, :, cols].astype(jnp.bfloat16)
             vb[slot, j, 1] = wot.astype(jnp.bfloat16)
-            wt[...] = wot
-            ws[2 * p + j] = jnp.where(bits[0] == 0, wi[slot, rows, cols], wt[rows, :])
-
-        fwd_pair(h, vb.at[slot], acc, eb, zb.at[slot], t, f)
+            obuf[j] = wot
+            ws[2 * p + j] = jnp.where(bits[0] == 0, wi[slot, rows, cols], obuf[j, rows, :])
+
+        fwd_pair(h, vb.at[slot], acc, ab, zb.at[slot], t, f)
         for cp in stores(p, slot):
             cp.start()
 
@@ -273,7 +280,7 @@
     ws_cp = local(ws, ws_out, io_sem.at[2])
     ws_cp.start()
     y_in.wait()
-    loss_close(h, tmp, acc, t, nb.at[0])
+    loss_close(h, tmp, acc, t, d)
     transpose_into(tb.at[1], h, t)
     x_again = local(x_hbm, tmp, io_sem.at[1])
     x_again.start()
@@ -288,7 +295,7 @@
         nb[0] += fold(g * g)
 
     backward_phase(dm, bits, peers, h, tmp, tb, eb, acc, zb.at[spare], vb.at[spare], cbuf, obuf, sbuf, (r1, r2, r3, r4),
-                   csend_sem, send_sem, recv_sem, credit, tiles, x_again.wait, on_total)
+                   csend_sem, send_sem, recv_sem, credit, tiles, x_again.wait, on_total, LAG_A)
     g_cp = local(gs, g_out, io_sem.at[0])
     g_cp.start()
     exchange_sum(nb, 0, near, nsend_sem, nrecv_sem, 0)
@@ -329,9 +336,6 @@
         ref = vb.at[u, 1 - core]
         return remote(ref, ref, *sems(u, 4), peers[0])
 
-    ins[2].wait()
-    fwd_seed(h, acc, t)
-
     def z_store(p, slot):
         return local(zb.at[slot], z_out.at[pl.ds(2 * p, 2)], z_sem.at[slot])
 
@@ -370,6 +374,11 @@
             @pl.when(p >= 2)
             def _():
                 z_store(p - 2, slot).wait()
+
+            @pl.when(p == 0)
+            def _():
+                ins[2].wait()
+                fwd_seed(h, acc, t)
             fwd_pair(h, vb.at[pl.ds(2 * p, 2)], acc, ab, zb.at[slot], t, f)
             z_store(p, slot).start()
 
@@ -382,7 +391,7 @@
                 out.wait()
 
     ins[3].wait()
-    loss_close(h, yb, acc, t, nb)
+    loss_close(h, yb, acc, t, d, nb)
     out = local(h, q_out, io_sem.at[0])
     sq = local(nb, sq_out, io_sem.at[1])
     out.start()
@@ -400,7 +409,7 @@
 
 
 def backward_phase(dm, bits, peers, q, tmp, tb, eb, acc, zb, vb, cbuf, obuf, sbuf, rbuf, csend_sem, send_sem, recv_sem, credit,
-                   tiles, x_ready, on_total, extra_its=0, extra=None):
+                   tiles, x_ready, on_total, lag, extra_its=0, extra=None):
     t, d, f, nf, nl = dm
     nu = nf * nl
     core = bits[0]
@@ -412,7 +421,7 @@
         return remote(sbuf.at[slot], cbuf.at[lax.rem(it, slots)], csend_sem.at[slot], recv_sem.at[0, it, 0], peers[0])
 
     def rs_sends(it, k):
-        ps, _, send, on = route(bits, peers, it, d)
+        ps, _, send, on = route(bits, peers, unit_of(it, nf, nl), d)
         n = d >> (k + 1)
         cs = lax.rem(it, slots)
 
@@ -425,7 +434,7 @@
                 part(pl.multiple_of(on[k + 1] * m, piece), m, recv_sem.at[2, it, k])]
 
     def rs_add(it, k, kept):
-        ps, keep, send, _ = route(bits, peers, it, d)
+        ps, keep, send, _ = route(bits, peers, unit_of(it, nf, nl), d)
         cs = lax.rem(it, slots)
         if k == 3:
             base, m = keep[4], d >> 4
@@ -443,7 +452,7 @@
         ref = cbuf.at[lax.rem(it, slots), pl.ds(0, 15 * piece), :]
         return remote(ref, ref, send_sem.at[it], recv_sem.at[1, it, 3], peers[0])
 
-    @pl.loop(0, nu + RS_LAG[4] + extra_its)
+    @pl.loop(0, nu + lag[4] + extra_its)
     def _(it):
         @pl.when(it == nf)
         def _():
@@ -484,7 +493,7 @@
                 for lo, n in halves(t):
                     acc[lo:lo + n, :] += dot(eb[0, lo:lo + n, :], vb[slot, 0], NT)
 
-        j0 = it - RS_LAG[0]
+        j0 = it - lag[0]
 
         @pl.when((j0 >= 0) & (j0 < nu))
         def _():
@@ -495,7 +504,7 @@
                 cp.start()
 
         for k in range(4):
-            j = it - RS_LAG[k + 1]
+            j = it - lag[k + 1]
 
             @pl.when((j >= 0) & (j < nu))
             def _():
@@ -555,7 +564,7 @@
     wait_all()
 
     def hops(it):
-        return gather_hops(bits, peers, it, d, w_out.at[unit_of(it, nf, nl), core], gs.at[unit_of(it, nf, nl)])
+        return gather_hops(bits, peers, unit_of(it, nf, nl), d, w_out.at[unit_of(it, nf, nl), core], gs.at[unit_of(it, nf, nl)])
 
     def sems(it, k):
         return ag_send.at[it, 0 if k < 4 else 1], ag_recv.at[it, k]
@@ -565,7 +574,7 @@
         return remote(ref, ref, *sems(it, 4), peers[0])
 
     def ag_local(it):
-        _, keep, _, _ = route(bits, peers, it, d)
+        _, keep, _, _ = route(bits, peers, unit_of(it, nf, nl), d)
         u = unit_of(it, nf, nl)
         return local(gs.at[u], w_out.at[u, core, pl.ds(keep[4], piece), :], ag_loc.at[it])
 
@@ -578,7 +587,7 @@
 
     def extra(it):
         for k in range(1, 5):
-            j = it - RS_LAG[4] - AG_LAG[k - 1]
+            j = it - LAG_B[4] - AG_LAG[k - 1]
 
             @pl.when((j >= 0) & (j < nu))
             def _():
@@ -599,7 +608,7 @@
             exchange_sum(nb, 8, far, nsend_sem, nrecv_sem, 7)
 
     backward_phase(dm, bits, peers, q, tmp, tb, eb, acc, zb, vb, cbuf, obuf, sbuf, (r1, r2, r3, r4),
-                   csend_sem, send_sem, recv_sem, credit, tiles, x_in.wait, on_total, AG_LAG[3], extra)
+                   csend_sem, send_sem, recv_sem, credit, tiles, x_in.wait, on_total, LAG_B, AG_LAG[3], extra)
     sq_cp = local(nb.at[12], sq_out, io_sem.at[3])
     sq_cp.start()
 
@@ -611,9 +620,10 @@
     sq_cp.wait()
 
 
-def finish(scale, w_ref, sq_ref, in_ref, out_ref, loss_ref):
-    in_ref[0] = w_ref[0, 0]
-    out_ref[0] = w_ref[0, 1].T
+def finish(scale, f, w_ref, sq_ref, in_ref, out_ref, loss_ref):
+    for j in range(w_ref.shape[0]):
+        in_ref[0, :, j * f:(j + 1) * f] = w_ref[j, 0]
+        out_ref[0, j * f:(j + 1) * f, :] = w_ref[j, 1].T
     loss_ref[0, 0] = 0.5 * (jnp.sum(sq_ref[...]) * scale)
 
 
@@ -661,13 +671,13 @@
 
     z, v, ws, g, norm = call(
         functools.partial(first_pass, dm, scale), 4, [z_s, v_s, w_s, w_s, n_s],
-        acts + [V((2, d, 2 * f), f32), V((2, 2 * f, d), f32), V((d, f), f32), V((2, 2, t, f), bf), V((2, 2, 2, d, f), bf), V((nu, piece, f), f32)]
+        acts + [V((t, 2 * f), bf), V((2, d, 2 * f), f32), V((2, 2 * f, d), f32), V((2, 2, t, f), bf), V((2, 2, 2, d, f), bf), V((nu, piece, f), f32)]
         + reduce_bufs + [V((13, 8, 128), f32), DMA((2, 2)), DMA((2,)), DMA((2,)), DMA((3,)), DMA((2,)), DMA((nu,)), DMA((3, nu, 4)), REG, DMA((10,)), DMA((10,))],
         "pass_a", 0)(x, y, w_in, w_out)
 
     z, v, h1, q, sq = call(
         functools.partial(second_forward, dm, scale, rho), 5, [z_s, v_s, a_s, a_s, n_s],
-        [V((t, d), bf), V((t, d), bf), V((t, d), f32), V((2, t, f), bf), V((nu, piece, f), f32), V((nu, piece, f), f32), V((nu, 2, d, f), bf), V((2, 2, t, f), bf),
+        [V((t, d), bf), V((t, d), bf), V((t, d), f32), V((t, 2 * f), bf), V((nu, piece, f), f32), V((nu, piece, f), f32), V((nu, 2, d, f), bf), V((2, 2, t, f), bf),
          V((8, 128), f32), DMA((nu, 2)), DMA((nu, 5)), DMA((2,)), DMA((nu,)), DMA((5,))], "fwd_b", 1)(g, ws, norm, x, y)
 
     w_new, sq = call(
@@ -676,10 +686,10 @@
          V((13, 8, 128), f32), DMA((nu, 2)), DMA((nu, 5)), DMA((nu,)), DMA((10,)), DMA((10,))], "bwd_b", 2)(x, h1, q, z, v, ws, sq)
 
     new_in, new_out, loss = pl.pallas_call(
-        functools.partial(finish, scale),
-        grid=(nl, nf),
-        in_specs=[pl.BlockSpec((1, 2, d, f), lambda i, j: (i * nf + j, 0, 0, 0)), pl.BlockSpec((8, 128), lambda i, j: (0, 0))],
-        out_specs=[pl.BlockSpec((1, d, f), lambda i, j: (i, 0, j)), pl.BlockSpec((1, f, d), lambda i, j: (i, j, 0)),
+        functools.partial(finish, scale, f),
+        grid=(nl, nf // 4),
+        in_specs=[pl.BlockSpec((4, 2, d, f), lambda i, j: (i * (nf // 4) + j, 0, 0, 0)), pl.BlockSpec((8, 128), lambda i, j: (0, 0))],
+        out_specs=[pl.BlockSpec((1, d, 4 * f), lambda i, j: (i, 0, j)), pl.BlockSpec((1, 4 * f, d), lambda i, j: (i, j, 0)),
                    pl.BlockSpec((1, 1), lambda i, j: (0, 0), memory_space=pltpu.SMEM)],
         out_shape=[sds((nl, d, ff), f32), sds((nl, ff, d), f32), sds((1, 1), f32)],
         compiler_params=pltpu.CompilerParams(vmem_limit_bytes=VMEM_CAP),

time: 664 us -> 639 us (0.962)
  Pallas kernels: 662 us -> 638 us
    pallas_call x1, Pallas kernels: 225 us -> 211 us  [local_step(): call(functools.partial(first_pass, dm, scale), 4, [z_s, v_s, w_s, w_s, n_...]
    pallas_call x1, Pallas kernels: 34.7 us -> 25.3 us  [local_step(): pl.pallas_call(functools.partial(finish, scale, f), grid=(nl, nf // 4), i...]
where the time goes in v6:
time: 639 us
  Pallas kernels  638 us (100%)
    pallas_call x1, Pallas kernels, local_step(): call(functools.partial(second_backward, dm, scale), 7, [sds((nu, 2, d, f)...  310 us
    pallas_call x1, Pallas kernels, local_step(): call(functools.partial(first_pass, dm, scale), 4, [z_s, v_s, w_s, w_s, n_...  211 us
    pallas_call x1, Pallas kernels, local_step(): call(functools.partial(second_forward, dm, scale, rho), 5, [z_s, v_s, a_s...  92.1 us
    pallas_call x1, Pallas kernels, local_step(): pl.pallas_call(functools.partial(finish, scale, f), grid=(nl, nf // 4), i...  25.3 us

profile of v6, /device:TPU:0, one launch (start us, length us, event | category | flops | bytes accessed | tf_op | source)
XLA Modules:
  0.0 639.2 jit_solution(6037208071134626448)
XLA Ops:
  0.6 211.4 %pass_a.1 = (bf16[24,1568,256]{2,1,0:T(8,128)(2,1)}, bf16[24,2,768,256]{3,2,1,0:T(8,128)(2,1)}, f32[24,48,256]{2,1,0:T(8,128)}, f32[24,48,256]{2,1,0:T(8,128)}, f32[8,128]{1,0:T(8,128)}) custom-call(bf16[1568,768]{1,0:T(8,128)(2,1)} %bitcast.7, bf16[1568,768]{1,0:T(8,128)(2,1)} %bitcast.10, f32[2,768,3072]{2,1,0:T(8,128)} %wi_hbm.1, f32[2,3072,768]{2,1,0:T(8,128)} %wo_hbm.1), custom_call_target="tpu_custom_call" | custom-call | tf_op jit(solution)/shard_map/pass_a/pallas_call | solution.py:672
  212.0 92.1 %fwd_b.1 = (bf16[24,1568,256]{2,1,0:T(8,128)(2,1)}, bf16[24,2,768,256]{3,2,1,0:T(8,128)(2,1)}, bf16[1568,768]{1,0:T(8,128)(2,1)}, bf16[1568,768]{1,0:T(8,128)(2,1)}, f32[8,128]{1,0:T(8,128)}) custom-call(f32[24,48,256]{2,1,0:T(8,128)} %get-tuple-element.16.gs_hbm, f32[24,48,256]{2,1,0:T(8,128)} %get-tuple-element.17.ws_hbm, ...), custom_call_target="tpu_custom_call" | custom-call | tf_op jit(solution)/shard_map/fwd_b/pallas_call | solution.py:678
  304.2 309.7 %bwd_b.1 = (f32[24,2,768,256]{3,2,1,0:T(8,128)}, f32[8,128]{1,0:T(8,128)}) custom-call(bf16[1568,768]{1,0:T(8,128)(2,1)} %bitcast.9, bf16[1568,768]{1,0:T(8,128)(2,1)} %get-tuple-element.19.h_hbm, bf16[1568,768]{1,0:T(8,128)(2,1)} %get-tuple-element.20.q_hbm, bf16[24,1568,256]{2,1,0:T(8,128)(2,1)} %get-tuple-element.21.z_hbm, ...), custom_call_target="tpu_custom_call" | custom-call | tf_op jit(solution)/shard_map/bwd_b/pallas_call | solution.py:683
  613.9 25.3 %finish.1 = (f32[2,768,3072]{2,1,0:T(8,128)}, f32[2,3072,768]{2,1,0:T(8,128)}, f32[1,1]{1,0:T(1,128)}) custom-call(f32[24,2,768,256]{3,2,1,0:T(8,128)} %get-tuple-element.24.w_ref, f32[8,128]{1,0:T(8,128)} %get-tuple-element.25.sq_ref), custom_call_target="tpu_custom_call" | custom-call | tf_op jit(solution)/shard_map/finish/pallas_call | solution.py:688

commit v7 on v6

--- a/solution.py
+++ b/solution.py
@@ -19,8 +19,7 @@
 VMEM_CAP = 67043328
 CORE_SLOTS = 9
 LAG_A = (0, 1, 4, 5, 7)
-LAG_B = (0, 1, 4, 6, 7)
-AG_LAG = (2, 3, 5, 6)
+LAG_B = (0, 1, 2, 3, 4, 4, 5, 7, 8, 9, 12)
 VG_LAG = (0, 2, 3, 5, 7, 9)
 
 
@@ -70,6 +69,32 @@
     return (p1, pa, p3, pb), keep, send, axes
 
 
+def chain_route(bits, peers, unit, d):
+    core, bx, by, ba, bb = bits
+    _, px, py, pa, _ = peers
+    swap = lax.rem(unit + core, 2) == 1
+    b1, p1 = jnp.where(swap, by, bx), jnp.where(swap, py, px)
+    b3, p3 = jnp.where(swap, bx, by), jnp.where(swap, px, py)
+    piece, chunk, pair, half = d // 16, d // 8, d // 4, d // 2
+    me = lax.axis_index("data")
+
+    def rows(base, n):
+        return pl.ds(pl.multiple_of(base, piece), n)
+    kx = b1 * half
+    own = kx + (2 * bb + ba) * chunk
+    mate = 2 * (kx + bb * pair) + chunk - own
+    r = dict(
+        half=rows(kx, half), other_half=rows((1 - b1) * half, half),
+        pair=rows(kx + bb * pair, pair), other_pair=rows(kx + (1 - bb) * pair, pair),
+        own=rows(own, chunk), mate=rows(mate, chunk),
+        far_end=rows(kx + (1 - bb) * 3 * chunk, chunk), far_mid=rows(kx + (2 - bb) * chunk, chunk),
+        keep=rows(own + b3 * piece, piece), send=rows(own + (1 - b3) * piece, piece),
+        x_send_first=(rows((1 - b1) * half + (1 - bb) * pair, pair), rows((1 - bb) * pair, pair)),
+        x_send_second=(rows((1 - b1) * half + bb * pair, pair), rows(bb * pair, pair)),
+    )
+    return r, p1, pa, me + 8 * (1 - 2 * bb), p3
+
+
 def arrive(peers):
     barrier = pltpu.get_barrier_semaphore()
     for peer in peers:
@@ -202,9 +227,9 @@
     return (nl - 1 - it // nf) * nf + lax.rem(it, nf)
 
 
-def first_pass(dm, scale, x_hbm, y_hbm, wi_hbm, wo_hbm, z_out, v_out, ws_out, g_out, n_out,
-               h, tmp, tb, eb, acc, ab, wi, wo, zb, vb, ws, cbuf, obuf, sbuf, r1, r2, r3, r4, gs, nb,
-               load_sem, z_sem, v_sem, io_sem, csend_sem, send_sem, recv_sem, credit, nsend_sem, nrecv_sem):
+def first_pass(dm, scale, x_hbm, y_hbm, wi_hbm, wo_hbm, z_out, v_out, ws_out, wc_out, g_out, n_out,
+               h, tmp, tb, eb, acc, ab, wi, wo, zb, vb, ws, wc, cbuf, obuf, sbuf, r1, r2, r3, r4, nb,
+               load_sem, z_sem, v_sem, io_sem, csend_sem, core_sem, send_sem, recv_sem, credit, nsend_sem, nrecv_sem):
     t, d, f, nf, nl = dm
     nu = nf * nl
     bits, peers = place()
@@ -255,6 +280,8 @@
             vb[slot, j, 1] = wot.astype(jnp.bfloat16)
             obuf[j] = wot
             ws[2 * p + j] = jnp.where(bits[0] == 0, wi[slot, rows, cols], obuf[j, rows, :])
+            rows = chain_route(bits, peers, j, d)[0]['keep']
+            wc[2 * p + j] = jnp.where(bits[0] == 0, wi[slot, rows, cols], obuf[j, rows, :])
 
         fwd_pair(h, vb.at[slot], acc, ab, zb.at[slot], t, f)
         for cp in stores(p, slot):
@@ -278,7 +305,9 @@
     for cp in tiles(0, 0):
         cp.start()
     ws_cp = local(ws, ws_out, io_sem.at[2])
+    wc_cp = local(wc, wc_out, io_sem.at[3])
     ws_cp.start()
+    wc_cp.start()
     y_in.wait()
     loss_close(h, tmp, acc, t, d)
     transpose_into(tb.at[1], h, t)
@@ -289,20 +318,23 @@
     wait_all()
     nb[0] = jnp.zeros((8, 128), jnp.float32)
 
-    def on_total(j, u, total):
-        gs[u] = total
+    ws_cp.wait()
+
+    def on_total(u, total):
+        ws[u] = total
         g = total * scale
         nb[0] += fold(g * g)
 
-    backward_phase(dm, bits, peers, h, tmp, tb, eb, acc, zb.at[spare], vb.at[spare], cbuf, obuf, sbuf, (r1, r2, r3, r4),
-                   csend_sem, send_sem, recv_sem, credit, tiles, x_again.wait, on_total, LAG_A)
-    g_cp = local(gs, g_out, io_sem.at[0])
+    start, events = halving(dm, bits, peers, cbuf, (r1, r2, r3, r4), send_sem, recv_sem, credit, LAG_A[1:], on_total)
+    backward_phase(dm, bits, peers, h, tmp, tb, eb, acc, zb.at[spare], vb.at[spare], cbuf, obuf, sbuf,
+                   csend_sem, core_sem, credit, tiles, x_again.wait, LAG_A[0], start, events)
+    g_cp = local(ws, g_out, io_sem.at[0])
     g_cp.start()
     exchange_sum(nb, 0, near, nsend_sem, nrecv_sem, 0)
     exchange_sum(nb, 8, far, nsend_sem, nrecv_sem, 7)
     n_cp = local(nb.at[12], n_out, io_sem.at[1])
     n_cp.start()
-    ws_cp.wait()
+    wc_cp.wait()
     g_cp.wait()
     n_cp.wait()
 
@@ -408,51 +440,24 @@
     sq.wait()
 
 
-def backward_phase(dm, bits, peers, q, tmp, tb, eb, acc, zb, vb, cbuf, obuf, sbuf, rbuf, csend_sem, send_sem, recv_sem, credit,
-                   tiles, x_ready, on_total, lag, extra_its=0, extra=None):
+def backward_phase(dm, bits, peers, q, tmp, tb, eb, acc, zb, vb, cbuf, obuf, sbuf, csend_sem, core_sem, credit,
+                   tiles, x_ready, core_lag, after_core, events):
     t, d, f, nf, nl = dm
     nu = nf * nl
     core = bits[0]
-    piece = d // 16
     slots = cbuf.shape[0]
 
     def core_copy(it):
         slot = lax.rem(it, 2)
-        return remote(sbuf.at[slot], cbuf.at[lax.rem(it, slots)], csend_sem.at[slot], recv_sem.at[0, it, 0], peers[0])
-
-    def rs_sends(it, k):
-        ps, _, send, on = route(bits, peers, unit_of(it, nf, nl), d)
-        n = d >> (k + 1)
-        cs = lax.rem(it, slots)
-
-        def part(off, m, sem):
-            return remote(cbuf.at[cs, pl.ds(send[k] + off, m), :], rbuf[k].at[it, pl.ds(off, m), :], send_sem.at[it], sem, ps[k])
-        if k == 3:
-            return [part(0, n, recv_sem.at[1, it, k])]
-        m = n // 2
-        return [part(pl.multiple_of((1 - on[k + 1]) * m, piece), m, recv_sem.at[1, it, k]),
-                part(pl.multiple_of(on[k + 1] * m, piece), m, recv_sem.at[2, it, k])]
-
-    def rs_add(it, k, kept):
-        ps, keep, send, _ = route(bits, peers, unit_of(it, nf, nl), d)
-        cs = lax.rem(it, slots)
-        if k == 3:
-            base, m = keep[4], d >> 4
-        else:
-            base, m = (keep[k + 2] if kept else send[k + 1]), d >> (k + 2)
-        here = rbuf[k].at[it, pl.ds(pl.multiple_of(base - keep[k + 1], piece), m), :]
-        mine = cbuf.at[cs, pl.ds(base, m), :]
-        remote(mine, here, send_sem.at[it], recv_sem.at[2 if kept else 1, it, k], ps[k]).wait_recv()
-        total = mine[...] + here[...]
-        if k == 3:
-            return total
-        mine[...] = total
-
-    def rs_sent(it):
-        ref = cbuf.at[lax.rem(it, slots), pl.ds(0, 15 * piece), :]
-        return remote(ref, ref, send_sem.at[it], recv_sem.at[1, it, 3], peers[0])
-
-    @pl.loop(0, nu + lag[4] + extra_its)
+        return remote(sbuf.at[slot], cbuf.at[lax.rem(it, slots)], csend_sem.at[slot], core_sem.at[it], peers[0])
+
+    def core_stage(j):
+        cs = lax.rem(j, slots)
+        core_copy(j).wait_recv()
+        cbuf[cs] = cbuf[cs] + obuf[lax.rem(j, 2)]
+        after_core(j)
+
+    @pl.loop(0, nu + max(lag for lag, _ in events))
     def _(it):
         @pl.when(it == nf)
         def _():
@@ -493,49 +498,240 @@
                 for lo, n in halves(t):
                     acc[lo:lo + n, :] += dot(eb[0, lo:lo + n, :], vb[slot, 0], NT)
 
-        j0 = it - lag[0]
-
-        @pl.when((j0 >= 0) & (j0 < nu))
-        def _():
-            cs = lax.rem(j0, slots)
-            core_copy(j0).wait_recv()
-            cbuf[cs] = cbuf[cs] + obuf[lax.rem(j0, 2)]
-            for cp in rs_sends(j0, 0):
-                cp.start()
-
-        for k in range(4):
-            j = it - lag[k + 1]
+        for lag, event in ((core_lag, core_stage), *events):
+            j = it - lag
 
             @pl.when((j >= 0) & (j < nu))
             def _():
-                if k > 0:
-                    rs_add(j, k - 1, True)
-                total = rs_add(j, k, False)
-                if k < 3:
-                    for cp in rs_sends(j, k + 1):
-                        cp.start()
-                else:
-                    on_total(j, unit_of(j, nf, nl), total)
-                    rs_sent(j).wait_send()
-
-                    @pl.when(j + slots < nu)
-                    def _():
-                        pl.semaphore_signal(credit, inc=1, device_id=(peers[0],), device_id_type=MESH)
-        if extra is not None:
-            extra(it)
+                event(j)
 
     core_copy(nu - 2).wait_send()
     core_copy(nu - 1).wait_send()
 
 
+def free_slot(j, nu, slots, credit, peer):
+    @pl.when(j + slots < nu)
+    def _():
+        pl.semaphore_signal(credit, inc=1, device_id=(peer,), device_id_type=MESH)
+
+
+def halving(dm, bits, peers, cbuf, rbuf, send_sem, recv_sem, credit, lags, on_total):
+    t, d, f, nf, nl = dm
+    nu = nf * nl
+    piece = d // 16
+    slots = cbuf.shape[0]
+
+    def rs_sends(it, k):
+        ps, _, send, on = route(bits, peers, it, d)
+        n = d >> (k + 1)
+        cs = lax.rem(it, slots)
+
+        def part(off, m, sem):
+            return remote(cbuf.at[cs, pl.ds(send[k] + off, m), :], rbuf[k].at[it, pl.ds(off, m), :], send_sem.at[it], sem, ps[k])
+        if k == 3:
+            return [part(0, n, recv_sem.at[0, it, k])]
+        m = n // 2
+        return [part(pl.multiple_of((1 - on[k + 1]) * m, piece), m, recv_sem.at[0, it, k]),
+                part(pl.multiple_of(on[k + 1] * m, piece), m, recv_sem.at[1, it, k])]
+
+    def rs_add(it, k, kept):
+        ps, keep, send, _ = route(bits, peers, it, d)
+        cs = lax.rem(it, slots)
+        if k == 3:
+            base, m = keep[4], d >> 4
+        else:
+            base, m = (keep[k + 2] if kept else send[k + 1]), d >> (k + 2)
+        here = rbuf[k].at[it, pl.ds(pl.multiple_of(base - keep[k + 1], piece), m), :]
+        mine = cbuf.at[cs, pl.ds(base, m), :]
+        remote(mine, here, send_sem.at[it], recv_sem.at[1 if kept else 0, it, k], ps[k]).wait_recv()
+        total = mine[...] + here[...]
+        if k == 3:
+            return total
+        mine[...] = total
+
+    def start(j):
+        for cp in rs_sends(j, 0):
+            cp.start()
+
+    def stage(k):
+        def event(j):
+            if k > 0:
+                rs_add(j, k - 1, True)
+            total = rs_add(j, k, False)
+            if k < 3:
+                for cp in rs_sends(j, k + 1):
+                    cp.start()
+            else:
+                on_total(unit_of(j, nf, nl), total)
+                ref = cbuf.at[lax.rem(j, slots), pl.ds(0, 15 * piece), :]
+                remote(ref, ref, send_sem.at[j], recv_sem.at[0, j, 3], peers[0]).wait_send()
+                free_slot(j, nu, slots, credit, peers[0])
+        return event
+    return start, [(lags[k], stage(k)) for k in range(4)]
+
+
+def chain(dm, bits, peers, cbuf, rbuf, gs, w_out, send_sem, recv_sem, credit, ag_send, ag_recv, ag_loc, lags, on_total):
+    t, d, f, nf, nl = dm
+    nu = nf * nl
+    core, _, _, ba, bb = bits
+    piece = d // 16
+    slots = cbuf.shape[0]
+    r1, r2, r3, r4, r5 = rbuf
+    at_end = ba == bb
+    chunk = d // 8
+    XU, XK, EU, EK, MU, MK, YY = range(7)
+
+    def send(j, src, dst, sem, peer):
+        remote(cbuf.at[lax.rem(j, slots), src, :], dst, send_sem.at[j], recv_sem.at[sem, j], peer).start()
+
+    def add(j, rows, buf, sem):
+        mine = cbuf.at[lax.rem(j, slots), rows, :]
+        remote(mine, buf, send_sem.at[j], recv_sem.at[sem, j], peers[0]).wait_recv()
+        mine[...] = mine[...] + buf[...]
+
+    def at(j):
+        return chain_route(bits, peers, unit_of(j, nf, nl), d)
+
+    def start(j):
+        r, p1, _, _, _ = at(j)
+        for (src, dst), sem in ((r["x_send_first"], XU), (r["x_send_second"], XK)):
+            send(j, src, r1.at[j, dst, :], sem, p1)
+
+    def rel(first):
+        return pl.ds(pl.multiple_of((1 - bb if first else bb) * (d // 4), piece), d // 4)
+
+    def s1(j):
+        r, _, pa, _, _ = at(j)
+        add(j, r["other_pair"], r1.at[j, rel(True), :], XU)
+
+        @pl.when(at_end)
+        def _():
+            send(j, r["other_pair"], r2.at[j], EU, pa)
+
+    def s2(j):
+        r, _, pa, pm, _ = at(j)
+        add(j, r["pair"], r1.at[j, rel(False), :], XK)
+
+        @pl.when(at_end)
+        def _():
+            send(j, r["mate"], r3.at[j], EK, pa)
+
+        @pl.when(jnp.logical_not(at_end))
+        def _():
+            add(j, r["other_pair"], r2.at[j], EU)
+            send(j, r["far_end"], r5.at[j, 0:chunk, :], MU, pm)
+            send(j, r["far_mid"], r5.at[j, chunk:2 * chunk, :], MK, pm)
+
+    def s3(j):
+        r, _, pa, _, p3 = at(j)
+
+        @pl.when(jnp.logical_not(at_end))
+        def _():
+            add(j, r["mate"], r5.at[j, 0:chunk, :], MU)
+            send(j, r["mate"], r3.at[j], EK, pa)
+            add(j, r["own"], r3.at[j], EK)
+            add(j, r["own"], r5.at[j, chunk:2 * chunk, :], MK)
+            send(j, r["send"], r4.at[j], YY, p3)
+
+    def s4(j):
+        r, _, _, _, p3 = at(j)
+
+        @pl.when(at_end)
+        def _():
+            add(j, r["own"], r3.at[j], EK)
+            send(j, r["send"], r4.at[j], YY, p3)
+
+    def full(j):
+        return w_out.at[unit_of(j, nf, nl), core]
+
+    def give(j, rows, sem_s, sem_r, peer, src=None):
+        ref = full(j).at[rows, :]
+        return remote(ref if src is None else src, ref, ag_send.at[j, sem_s], ag_recv.at[j, sem_r], peer)
+
+    def own_copy(j):
+        u = unit_of(j, nf, nl)
+        return local(gs.at[u], full(j).at[at(j)[0]["keep"], :], ag_loc.at[j])
+
+    def s5(j):
+        r, _, _, _, p3 = at(j)
+        u = unit_of(j, nf, nl)
+        mine = cbuf.at[lax.rem(j, slots), r["keep"], :]
+        remote(mine, r4.at[j], send_sem.at[j], recv_sem.at[YY, j], p3).wait_recv()
+        on_total(u, mine[...] + r4[j])
+        own_copy(j).start()
+        give(j, r["keep"], 0, 0, p3, gs.at[u]).start()
+        ref = cbuf.at[lax.rem(j, slots), pl.ds(0, 15 * piece), :]
+        remote(ref, ref, send_sem.at[j], recv_sem.at[YY, j], p3).wait_send()
+        free_slot(j, nu, slots, credit, peers[0])
+
+    def g1(j):
+        r, p1, pa, pm, p3 = at(j)
+        own_copy(j).wait()
+        give(j, r["send"], 0, 0, p3).wait_recv()
+        give(j, r["own"], 0, 1, pa).start()
+
+        @pl.when(jnp.logical_not(at_end))
+        def _():
+            give(j, r["own"], 1, 2, pm).start()
+        give(j, r["own"], 0, 3, p1).start()
+
+    def g2(j):
+        r, p1, pa, pm, _ = at(j)
+        give(j, r["mate"], 0, 1, pa).wait_recv()
+
+        @pl.when(jnp.logical_not(at_end))
+        def _():
+            give(j, r["mate"], 1, 2, pm).start()
+        give(j, r["mate"], 0, 3, p1).start()
+
+    def g3(j, r, p1, pa):
+        give(j, r["other_pair"], 1, 2, pa).wait_recv()
+        give(j, r["other_pair"], 0, 3, p1).start()
+        give(j, r["half"], 2, 4, peers[0]).start()
+
+    def g3_middle(j):
+        r, p1, pa, _, _ = at(j)
+
+        @pl.when(jnp.logical_not(at_end))
+        def _():
+            g3(j, r, p1, pa)
+            give(j, r["other_pair"], 1, 2, pa).start()
+
+    def g3_end(j):
+        r, p1, pa, _, _ = at(j)
+
+        @pl.when(at_end)
+        def _():
+            g3(j, r, p1, pa)
+
+    def g4(j):
+        r, p1, _, _, _ = at(j)
+        give(j, r["other_half"], 0, 3, p1).wait_recv()
+        give(j, r["other_half"], 2, 4, peers[0]).start()
+
+    def finish_unit(j):
+        ref = w_out.at[unit_of(j, nf, nl), 1 - core]
+        last = remote(ref, ref, ag_send.at[j, 2], ag_recv.at[j, 4], peers[0])
+        last.wait_recv()
+        last.wait_send()
+        ref = full(j).at[pl.ds(0, 11 * piece), :]
+        remote(ref, ref, ag_send.at[j, 0], ag_recv.at[j, 3], peers[0]).wait_send()
+
+        @pl.when(jnp.logical_not(at_end))
+        def _():
+            ref = full(j).at[pl.ds(0, 8 * piece), :]
+            remote(ref, ref, ag_send.at[j, 1], ag_recv.at[j, 2], peers[0]).wait_send()
+
+    steps = (s1, s2, s3, s4, s5, g1, g2, g3_middle, g3_end, g4)
+    return start, list(zip(lags, steps)), finish_unit
+
+
 def second_backward(dm, scale, x_hbm, h_hbm, q_hbm, z_hbm, v_hbm, ws_hbm, sq_hbm, w_out, sq_out,
-                    q, tmp, tb, eb, acc, zb, vb, cbuf, obuf, sbuf, r1, r2, r3, r4, gs,
-                    load_sem, io_sem, csend_sem, send_sem, recv_sem, credit, nb, ag_send, ag_recv, ag_loc, nsend_sem, nrecv_sem):
+                    q, tmp, tb, eb, acc, zb, vb, cbuf, obuf, sbuf, r1, r2, r3, r4, gs, r5,
+                    load_sem, io_sem, csend_sem, core_sem, send_sem, recv_sem, credit, nb, ag_send, ag_recv, ag_loc, nsend_sem, nrecv_sem):
     t, d, f, nf, nl = dm
     nu = nf * nl
     bits, peers = place()
-    core = bits[0]
-    piece = d // 16
     near, far = others(bits, (0, 1, 2)), others(bits, (3, 4))
     wait_all = arrive(near + far)
 
@@ -563,60 +759,28 @@
     sq_in.wait()
     wait_all()
 
-    def hops(it):
-        return gather_hops(bits, peers, unit_of(it, nf, nl), d, w_out.at[unit_of(it, nf, nl), core], gs.at[unit_of(it, nf, nl)])
-
-    def sems(it, k):
-        return ag_send.at[it, 0 if k < 4 else 1], ag_recv.at[it, k]
-
-    def core_arrived(it):
-        ref = w_out.at[unit_of(it, nf, nl), 1 - core]
-        return remote(ref, ref, *sems(it, 4), peers[0])
-
-    def ag_local(it):
-        _, keep, _, _ = route(bits, peers, unit_of(it, nf, nl), d)
-        u = unit_of(it, nf, nl)
-        return local(gs.at[u], w_out.at[u, core, pl.ds(keep[4], piece), :], ag_loc.at[it])
-
-    def on_total(j, u, total):
+    def on_total(u, total):
         gs[u] = gs[u] - LEARN_RATE * (total * scale)
-        ag_local(j).start()
-        hop, _, _ = hops(j)
-        hop(0, 0, *sems(j, 0)).start()
-        hop(1, 0, *sems(j, 1)).start()
-
-    def extra(it):
-        for k in range(1, 5):
-            j = it - LAG_B[4] - AG_LAG[k - 1]
-
-            @pl.when((j >= 0) & (j < nu))
-            def _():
-                hop, arrived, _ = hops(j)
-                if k == 1:
-                    ag_local(j).wait()
-                arrived(k - 1, *sems(j, k - 1)).wait_recv()
-                hop(k, 1, *sems(j, k)).start()
-                if k < 4:
-                    hop(k + 1, 0, *sems(j, k + 1)).start()
-
-        @pl.when(it == 1)
+
+    def sums(j):
+        @pl.when(j == 1)
         def _():
             exchange_sum(nb, 0, near, nsend_sem, nrecv_sem, 0)
 
-        @pl.when(it == 2)
+        @pl.when(j == 2)
         def _():
             exchange_sum(nb, 8, far, nsend_sem, nrecv_sem, 7)
 
-    backward_phase(dm, bits, peers, q, tmp, tb, eb, acc, zb, vb, cbuf, obuf, sbuf, (r1, r2, r3, r4),
-                   csend_sem, send_sem, recv_sem, credit, tiles, x_in.wait, on_total, LAG_B, AG_LAG[3], extra)
+    start, events, finish_unit = chain(dm, bits, peers, cbuf, (r1, r2, r3, r4, r5), gs, w_out, send_sem, recv_sem, credit,
+                                       ag_send, ag_recv, ag_loc, LAG_B[1:], on_total)
+    backward_phase(dm, bits, peers, q, tmp, tb, eb, acc, zb, vb, cbuf, obuf, sbuf,
+                   csend_sem, core_sem, credit, tiles, x_in.wait, LAG_B[0], start, [*events, (0, sums)])
     sq_cp = local(nb.at[12], sq_out, io_sem.at[3])
     sq_cp.start()
 
     @pl.loop(0, nu)
-    def _(it):
-        core_arrived(it).wait_recv()
-        hops(it)[2](*sems(it, 0)).wait_send()
-        core_arrived(it).wait_send()
+    def _(j):
+        finish_unit(j)
     sq_cp.wait()
 
 
@@ -669,10 +833,10 @@
                    V((nu, d // 2, f), f32), V((nu, d // 4, f), f32), V((nu, d // 8, f), f32), V((nu, d // 16, f), f32), V((nu, piece, f), f32)]
     acts = [V((t, d), bf), V((t, d), bf), V((2, d, t), bf), V((2, t, f), bf), V((t, d), f32)]
 
-    z, v, ws, g, norm = call(
-        functools.partial(first_pass, dm, scale), 4, [z_s, v_s, w_s, w_s, n_s],
-        acts + [V((t, 2 * f), bf), V((2, d, 2 * f), f32), V((2, 2 * f, d), f32), V((2, 2, t, f), bf), V((2, 2, 2, d, f), bf), V((nu, piece, f), f32)]
-        + reduce_bufs + [V((13, 8, 128), f32), DMA((2, 2)), DMA((2,)), DMA((2,)), DMA((3,)), DMA((2,)), DMA((nu,)), DMA((3, nu, 4)), REG, DMA((10,)), DMA((10,))],
+    z, v, ws, wc, g, norm = call(
+        functools.partial(first_pass, dm, scale), 4, [z_s, v_s, w_s, w_s, w_s, n_s],
+        acts + [V((t, 2 * f), bf), V((2, d, 2 * f), f32), V((2, 2 * f, d), f32), V((2, 2, t, f), bf), V((2, 2, 2, d, f), bf), V((nu, piece, f), f32), V((nu, piece, f), f32)]
+        + reduce_bufs[:-1] + [V((13, 8, 128), f32), DMA((2, 2)), DMA((2,)), DMA((2,)), DMA((4,)), DMA((2,)), DMA((nu,)), DMA((nu,)), DMA((2, nu, 4)), REG, DMA((10,)), DMA((10,))],
         "pass_a", 0)(x, y, w_in, w_out)
 
     z, v, h1, q, sq = call(
@@ -682,8 +846,8 @@
 
     w_new, sq = call(
         functools.partial(second_backward, dm, scale), 7, [sds((nu, 2, d, f), f32), n_s],
-        acts + [V((2, t, f), bf), V((2, 2, d, f), bf)] + reduce_bufs + [DMA((2, 2)), DMA((4,)), DMA((2,)), DMA((nu,)), DMA((3, nu, 4)), REG,
-         V((13, 8, 128), f32), DMA((nu, 2)), DMA((nu, 5)), DMA((nu,)), DMA((10,)), DMA((10,))], "bwd_b", 2)(x, h1, q, z, v, ws, sq)
+        acts + [V((2, t, f), bf), V((2, 2, d, f), bf)] + reduce_bufs + [V((nu, d // 4, f), f32), DMA((2, 2)), DMA((4,)), DMA((2,)), DMA((nu,)), DMA((nu,)), DMA((7, nu)), REG,
+         V((13, 8, 128), f32), DMA((nu, 3)), DMA((nu, 5)), DMA((nu,)), DMA((10,)), DMA((10,))], "bwd_b", 2)(x, h1, q, z, v, wc, sq)
 
     new_in, new_out, loss = pl.pallas_call(
         functools.partial(finish, scale, f),

time: 639 us -> 629 us (0.984)
  Pallas kernels: 638 us -> 628 us
    pallas_call x1, Pallas kernels: 310 us -> 301 us  [local_step(): call(functools.partial(second_backward, dm, scale), 7, [sds((nu, 2, d, f)...]
where the time goes in v7:
time: 629 us
  Pallas kernels  628 us (100%)
    pallas_call x1, Pallas kernels, local_step(): call(functools.partial(second_backward, dm, scale), 7, [sds((nu, 2, d, f)...  301 us
    pallas_call x1, Pallas kernels, local_step(): call(functools.partial(first_pass, dm, scale), 4, [z_s, v_s, w_s, w_s, w_...  210 us
    pallas_call x1, Pallas kernels, local_step(): call(functools.partial(second_forward, dm, scale, rho), 5, [z_s, v_s, a_s...  92.1 us
    pallas_call x1, Pallas kernels, local_step(): pl.pallas_call(functools.partial(finish, scale, f), grid=(nl, nf // 4), i...  25.3 us

profile of v7, /device:TPU:0, one launch (start us, length us, event | category | flops | bytes accessed | tf_op | source)
XLA Modules:
  0.0 629.2 jit_solution(5577831221327162559)
XLA Ops:
  0.6 210.2 %pass_a.1 = (bf16[24,1568,256]{2,1,0:T(8,128)(2,1)}, bf16[24,2,768,256]{3,2,1,0:T(8,128)(2,1)}, f32[24,48,256]{2,1,0:T(8,128)}, f32[24,48,256]{2,1,0:T(8,128)}, ...) custom-call(bf16[1568,768]{1,0:T(8,128)(2,1)} %bitcast.7, bf16[1568,768]{1,0:T(8,128)(2,1)} %bitcast.10, f32[2,768,3072]{2,1,0:T(8,128)} %wi_hbm.1, ...), custom_call_target="tpu_custom_call" | custom-call | tf_op jit(solution)/shard_map/pass_a/pallas_call | solution.py:836
  210.8 92.1 %fwd_b.1 = (bf16[24,1568,256]{2,1,0:T(8,128)(2,1)}, bf16[24,2,768,256]{3,2,1,0:T(8,128)(2,1)}, bf16[1568,768]{1,0:T(8,128)(2,1)}, bf16[1568,768]{1,0:T(8,128)(2,1)}, f32[8,128]{1,0:T(8,128)}) custom-call(f32[24,48,256]{2,1,0:T(8,128)} %get-tuple-element.17.gs_hbm, f32[24,48,256]{2,1,0:T(8,128)} %get-tuple-element.18.ws_hbm, ...), custom_call_target="tpu_custom_call" | custom-call | tf_op jit(solution)/shard_map/fwd_b/pallas_call | solution.py:842
  303.0 300.9 %bwd_b.1 = (f32[24,2,768,256]{3,2,1,0:T(8,128)}, f32[8,128]{1,0:T(8,128)}) custom-call(bf16[1568,768]{1,0:T(8,128)(2,1)} %bitcast.9, bf16[1568,768]{1,0:T(8,128)(2,1)} %get-tuple-element.20.h_hbm, bf16[1568,768]{1,0:T(8,128)(2,1)} %get-tuple-element.21.q_hbm, bf16[24,1568,256]{2,1,0:T(8,128)(2,1)} %get-tuple-element.22.z_hbm, ...), custom_call_target="tpu_custom_call" | custom-call | tf_op jit(solution)/shard_map/bwd_b/pallas_call | solution.py:847
  603.9 25.3 %finish.1 = (f32[2,768,3072]{2,1,0:T(8,128)}, f32[2,3072,768]{2,1,0:T(8,128)}, f32[1,1]{1,0:T(1,128)}) custom-call(f32[24,2,768,256]{3,2,1,0:T(8,128)} %get-tuple-element.26.w_ref, f32[8,128]{1,0:T(8,128)} %get-tuple-element.27.sq_ref), custom_call_target="tpu_custom_call" | custom-call | tf_op jit(solution)/shard_map/finish/pallas_call | solution.py:852

commit v8 on v7

--- a/solution.py
+++ b/solution.py
@@ -17,10 +17,18 @@
 GELU_C = math.sqrt(2.0 / math.pi)
 GELU_K = 0.044715
 VMEM_CAP = 67043328
+TILE = (8, 128)
 CORE_SLOTS = 9
 LAG_A = (0, 1, 4, 5, 7)
 LAG_B = (0, 1, 2, 3, 4, 4, 5, 7, 8, 9, 12)
 VG_LAG = (0, 2, 3, 5, 7, 9)
+
+
+steps = functools.partial(pl.loop, 0)
+
+
+def odd(i):
+    return lax.rem(i, 2)
 
 
 def dot(lhs, rhs, dims=NN):
@@ -54,7 +62,7 @@
 def route(bits, peers, unit, rows):
     core, bx, by, ba, bb = bits
     _, px, py, pa, pb = peers
-    swap = lax.rem(unit + core, 2) == 1
+    swap = odd(unit + core) == 1
     b1, p1 = jnp.where(swap, by, bx), jnp.where(swap, py, px)
     b3, p3 = jnp.where(swap, bx, by), jnp.where(swap, px, py)
     axes = (b1, ba, b3, bb)
@@ -72,7 +80,7 @@
 def chain_route(bits, peers, unit, d):
     core, bx, by, ba, bb = bits
     _, px, py, pa, _ = peers
-    swap = lax.rem(unit + core, 2) == 1
+    swap = odd(unit + core) == 1
     b1, p1 = jnp.where(swap, by, bx), jnp.where(swap, py, px)
     b3, p3 = jnp.where(swap, bx, by), jnp.where(swap, px, py)
     piece, chunk, pair, half = d // 16, d // 8, d // 4, d // 2
@@ -98,7 +106,7 @@
 def arrive(peers):
     barrier = pltpu.get_barrier_semaphore()
     for peer in peers:
-        pl.semaphore_signal(barrier, inc=1, device_id=(peer,), device_id_type=MESH)
+        pl.semaphore_signal(barrier, device_id=(peer,), device_id_type=MESH)
     return functools.partial(pl.semaphore_wait, barrier, len(peers))
 
 
@@ -168,7 +176,7 @@
 def transpose_into(dst, src, t):
     full = t // 128
     if full:
-        @pl.loop(0, full)
+        @steps(full)
         def _(i):
             lo = pl.multiple_of(i * 128, 128)
             dst[:, pl.ds(lo, 128)] = src[pl.ds(lo, 128), :].T
@@ -215,9 +223,9 @@
             rows_of(slice(lo, lo + n))
         return
     n = 112 if t % 112 == 0 else t
-    total_ref[...] = jnp.zeros((8, 128), jnp.float32)
-
-    @pl.loop(0, t // n)
+    total_ref[...] = jnp.zeros(TILE, jnp.float32)
+
+    @steps(t // n)
     def _(i):
         e = rows_of(pl.ds(pl.multiple_of(i * n, n), n))
         total_ref[...] += fold(e * e)
@@ -256,9 +264,9 @@
     x_in.wait()
     fwd_seed(h, acc, t)
 
-    @pl.loop(0, nu // 2)
+    @steps(nu // 2)
     def _(p):
-        slot = lax.rem(p, 2)
+        slot = odd(p)
         for cp in loads(p, slot):
             cp.wait()
 
@@ -316,7 +324,7 @@
     for cp in stores(np_ - 1, (np_ - 1) % 2):
         cp.wait()
     wait_all()
-    nb[0] = jnp.zeros((8, 128), jnp.float32)
+    nb[0] = jnp.zeros(TILE, jnp.float32)
 
     ws_cp.wait()
 
@@ -371,7 +379,7 @@
     def z_store(p, slot):
         return local(zb.at[slot], z_out.at[pl.ds(2 * p, 2)], z_sem.at[slot])
 
-    @pl.loop(0, nu + VG_LAG[5])
+    @steps(nu + VG_LAG[5])
     def _(it):
         @pl.when(it < nu)
         def _():
@@ -398,10 +406,10 @@
             core_arrived(u).wait_recv()
             local(vb.at[u], v_out.at[u], v_sem.at[u]).start()
 
-        @pl.when((u >= 0) & (lax.rem(u, 2) == 1))
+        @pl.when((u >= 0) & (odd(u) == 1))
         def _():
             p = u // 2
-            slot = lax.rem(p, 2)
+            slot = odd(p)
 
             @pl.when(p >= 2)
             def _():
@@ -429,7 +437,7 @@
     out.start()
     sq.start()
 
-    @pl.loop(0, nu)
+    @steps(nu)
     def _(u):
         local(vb.at[u], v_out.at[u], v_sem.at[u]).wait()
         hops(u)[2](*sems(u, 0)).wait_send()
@@ -448,16 +456,16 @@
     slots = cbuf.shape[0]
 
     def core_copy(it):
-        slot = lax.rem(it, 2)
+        slot = odd(it)
         return remote(sbuf.at[slot], cbuf.at[lax.rem(it, slots)], csend_sem.at[slot], core_sem.at[it], peers[0])
 
     def core_stage(j):
         cs = lax.rem(j, slots)
         core_copy(j).wait_recv()
-        cbuf[cs] = cbuf[cs] + obuf[lax.rem(j, 2)]
+        cbuf[cs] = cbuf[cs] + obuf[odd(j)]
         after_core(j)
 
-    @pl.loop(0, nu + max(lag for lag, _ in events))
+    @steps(nu + max(lag for lag, _ in events))
     def _(it):
         @pl.when(it == nf)
         def _():
@@ -468,7 +476,7 @@
 
         @pl.when(it < nu)
         def _():
-            slot = lax.rem(it, 2)
+            slot = odd(it)
             for cp in tiles(it, slot):
                 cp.wait()
 
@@ -489,7 +497,7 @@
 
             @pl.when(it >= slots)
             def _():
-                pl.semaphore_wait(credit, 1)
+                pl.semaphore_wait(credit)
             core_copy(it).start()
             obuf[slot] = dot(tb[core], eb[core])
 
@@ -512,7 +520,7 @@
 def free_slot(j, nu, slots, credit, peer):
     @pl.when(j + slots < nu)
     def _():
-        pl.semaphore_signal(credit, inc=1, device_id=(peer,), device_id_type=MESH)
+        pl.semaphore_signal(credit, device_id=(peer,), device_id_type=MESH)
 
 
 def halving(dm, bits, peers, cbuf, rbuf, send_sem, recv_sem, credit, lags, on_total):
@@ -520,6 +528,7 @@
     nu = nf * nl
     piece = d // 16
     slots = cbuf.shape[0]
+    partner = peers[0]
 
     def rs_sends(it, k):
         ps, _, send, on = route(bits, peers, it, d)
@@ -564,8 +573,8 @@
             else:
                 on_total(unit_of(j, nf, nl), total)
                 ref = cbuf.at[lax.rem(j, slots), pl.ds(0, 15 * piece), :]
-                remote(ref, ref, send_sem.at[j], recv_sem.at[0, j, 3], peers[0]).wait_send()
-                free_slot(j, nu, slots, credit, peers[0])
+                remote(ref, ref, send_sem.at[j], recv_sem.at[0, j, 3], partner).wait_send()
+                free_slot(j, nu, slots, credit, partner)
         return event
     return start, [(lags[k], stage(k)) for k in range(4)]
 
@@ -580,13 +589,16 @@
     at_end = ba == bb
     chunk = d // 8
     XU, XK, EU, EK, MU, MK, YY = range(7)
+    ALL, MIDDLE, CORE = range(3)
+    HALF, MATE, PAIR, LAST, FULL = range(5)
+    partner = peers[0]
 
     def send(j, src, dst, sem, peer):
         remote(cbuf.at[lax.rem(j, slots), src, :], dst, send_sem.at[j], recv_sem.at[sem, j], peer).start()
 
     def add(j, rows, buf, sem):
         mine = cbuf.at[lax.rem(j, slots), rows, :]
-        remote(mine, buf, send_sem.at[j], recv_sem.at[sem, j], peers[0]).wait_recv()
+        remote(mine, buf, send_sem.at[j], recv_sem.at[sem, j], partner).wait_recv()
         mine[...] = mine[...] + buf[...]
 
     def at(j):
@@ -659,35 +671,35 @@
         remote(mine, r4.at[j], send_sem.at[j], recv_sem.at[YY, j], p3).wait_recv()
         on_total(u, mine[...] + r4[j])
         own_copy(j).start()
-        give(j, r["keep"], 0, 0, p3, gs.at[u]).start()
+        give(j, r["keep"], ALL, HALF, p3, gs.at[u]).start()
         ref = cbuf.at[lax.rem(j, slots), pl.ds(0, 15 * piece), :]
         remote(ref, ref, send_sem.at[j], recv_sem.at[YY, j], p3).wait_send()
-        free_slot(j, nu, slots, credit, peers[0])
+        free_slot(j, nu, slots, credit, partner)
 
     def g1(j):
         r, p1, pa, pm, p3 = at(j)
         own_copy(j).wait()
-        give(j, r["send"], 0, 0, p3).wait_recv()
-        give(j, r["own"], 0, 1, pa).start()
+        give(j, r["send"], ALL, HALF, p3).wait_recv()
+        give(j, r["own"], ALL, MATE, pa).start()
 
         @pl.when(jnp.logical_not(at_end))
         def _():
-            give(j, r["own"], 1, 2, pm).start()
-        give(j, r["own"], 0, 3, p1).start()
+            give(j, r["own"], MIDDLE, PAIR, pm).start()
+        give(j, r["own"], ALL, LAST, p1).start()
 
     def g2(j):
         r, p1, pa, pm, _ = at(j)
-        give(j, r["mate"], 0, 1, pa).wait_recv()
+        give(j, r["mate"], ALL, MATE, pa).wait_recv()
 
         @pl.when(jnp.logical_not(at_end))
         def _():
-            give(j, r["mate"], 1, 2, pm).start()
-        give(j, r["mate"], 0, 3, p1).start()
+            give(j, r["mate"], MIDDLE, PAIR, pm).start()
+        give(j, r["mate"], ALL, LAST, p1).start()
 
     def g3(j, r, p1, pa):
-        give(j, r["other_pair"], 1, 2, pa).wait_recv()
-        give(j, r["other_pair"], 0, 3, p1).start()
-        give(j, r["half"], 2, 4, peers[0]).start()
+        give(j, r["other_pair"], MIDDLE, PAIR, pa).wait_recv()
+        give(j, r["other_pair"], ALL, LAST, p1).start()
+        give(j, r["half"], CORE, FULL, partner).start()
 
     def g3_middle(j):
         r, p1, pa, _, _ = at(j)
@@ -695,7 +707,7 @@
         @pl.when(jnp.logical_not(at_end))
         def _():
             g3(j, r, p1, pa)
-            give(j, r["other_pair"], 1, 2, pa).start()
+            give(j, r["other_pair"], MIDDLE, PAIR, pa).start()
 
     def g3_end(j):
         r, p1, pa, _, _ = at(j)
@@ -706,28 +718,28 @@
 
     def g4(j):
         r, p1, _, _, _ = at(j)
-        give(j, r["other_half"], 0, 3, p1).wait_recv()
-        give(j, r["other_half"], 2, 4, peers[0]).start()
+        give(j, r["other_half"], ALL, LAST, p1).wait_recv()
+        give(j, r["other_half"], CORE, FULL, partner).start()
 
     def finish_unit(j):
         ref = w_out.at[unit_of(j, nf, nl), 1 - core]
-        last = remote(ref, ref, ag_send.at[j, 2], ag_recv.at[j, 4], peers[0])
+        last = remote(ref, ref, ag_send.at[j, CORE], ag_recv.at[j, FULL], partner)
         last.wait_recv()
         last.wait_send()
         ref = full(j).at[pl.ds(0, 11 * piece), :]
-        remote(ref, ref, ag_send.at[j, 0], ag_recv.at[j, 3], peers[0]).wait_send()
+        remote(ref, ref, ag_send.at[j, ALL], ag_recv.at[j, LAST], partner).wait_send()
 
         @pl.when(jnp.logical_not(at_end))
         def _():
             ref = full(j).at[pl.ds(0, 8 * piece), :]
-            remote(ref, ref, ag_send.at[j, 1], ag_recv.at[j, 2], peers[0]).wait_send()
+            remote(ref, ref, ag_send.at[j, MIDDLE], ag_recv.at[j, PAIR], partner).wait_send()
 
     steps = (s1, s2, s3, s4, s5, g1, g2, g3_middle, g3_end, g4)
     return start, list(zip(lags, steps)), finish_unit
 
 
 def second_backward(dm, scale, x_hbm, h_hbm, q_hbm, z_hbm, v_hbm, ws_hbm, sq_hbm, w_out, sq_out,
-                    q, tmp, tb, eb, acc, zb, vb, cbuf, obuf, sbuf, r1, r2, r3, r4, gs, r5,
+                    q, tmp, tb, eb, acc, zb, vb, cbuf, obuf, sbuf, r1, r2, r3, r4, r5, gs,
                     load_sem, io_sem, csend_sem, core_sem, send_sem, recv_sem, credit, nb, ag_send, ag_recv, ag_loc, nsend_sem, nrecv_sem):
     t, d, f, nf, nl = dm
     nu = nf * nl
@@ -778,7 +790,7 @@
     sq_cp = local(nb.at[12], sq_out, io_sem.at[3])
     sq_cp.start()
 
-    @pl.loop(0, nu)
+    @steps(nu)
     def _(j):
         finish_unit(j)
     sq_cp.wait()
@@ -821,38 +833,39 @@
     scale = 1.0 / (t * n_dev * d)
     rho = RHO_FRAC * math.sqrt(nl * (d + ff))
     bf, f32 = jnp.bfloat16, jnp.float32
-    V, DMA = pltpu.VMEM, pltpu.SemaphoreType.DMA
+    V, DMA, REG = pltpu.VMEM, pltpu.SemaphoreType.DMA, pltpu.SemaphoreType.REGULAR
     x = x_loc.transpose(1, 0, 2).reshape(t, d)
     y = y_loc.transpose(1, 0, 2).reshape(t, d)
-    z_s, v_s, w_s, a_s = sds((nu, t, f), bf), sds((nu, 2, d, f), bf), sds((nu, piece, f), f32), sds((t, d), bf)
-
-    REG = pltpu.SemaphoreType.REGULAR
+    z_s, v_s, w_s, a_s, n_s = sds((nu, t, f), bf), sds((nu, 2, d, f), bf), sds((nu, piece, f), f32), sds((t, d), bf), sds(TILE, f32)
     slots = min(CORE_SLOTS, nu)
-    n_s = sds((8, 128), f32)
-    reduce_bufs = [V((slots, d, f), f32), V((2, d, f), f32), V((2, d, f), f32),
-                   V((nu, d // 2, f), f32), V((nu, d // 4, f), f32), V((nu, d // 8, f), f32), V((nu, d // 16, f), f32), V((nu, piece, f), f32)]
-    acts = [V((t, d), bf), V((t, d), bf), V((2, d, t), bf), V((2, t, f), bf), V((t, d), f32)]
+    tile2, rows = V((2, d, f), f32), V((nu, piece, f), f32)
+    reduce_bufs = [V((slots, d, f), f32), tile2, tile2, *(V((nu, d >> k, f), f32) for k in range(1, 5))]
+    act, sums, both = V((t, d), bf), V((t, d), f32), V((t, 2 * f), bf)
+    acts = [act, act, V((2, d, t), bf), V((2, t, f), bf), sums]
+    norms, tens = V((13, *TILE), f32), DMA((10,))
+    two, four, per_unit, loads = DMA((2,)), DMA((4,)), DMA((nu,)), DMA((2, 2))
 
     z, v, ws, wc, g, norm = call(
         functools.partial(first_pass, dm, scale), 4, [z_s, v_s, w_s, w_s, w_s, n_s],
-        acts + [V((t, 2 * f), bf), V((2, d, 2 * f), f32), V((2, 2 * f, d), f32), V((2, 2, t, f), bf), V((2, 2, 2, d, f), bf), V((nu, piece, f), f32), V((nu, piece, f), f32)]
-        + reduce_bufs[:-1] + [V((13, 8, 128), f32), DMA((2, 2)), DMA((2,)), DMA((2,)), DMA((4,)), DMA((2,)), DMA((nu,)), DMA((nu,)), DMA((2, nu, 4)), REG, DMA((10,)), DMA((10,))],
+        acts + [both, V((2, d, 2 * f), f32), V((2, 2 * f, d), f32), V((2, 2, t, f), bf), V((2, 2, 2, d, f), bf), rows, rows]
+        + reduce_bufs + [norms, loads, two, two, four, two, per_unit, per_unit, DMA((2, nu, 4)), REG, tens, tens],
         "pass_a", 0)(x, y, w_in, w_out)
 
     z, v, h1, q, sq = call(
         functools.partial(second_forward, dm, scale, rho), 5, [z_s, v_s, a_s, a_s, n_s],
-        [V((t, d), bf), V((t, d), bf), V((t, d), f32), V((t, 2 * f), bf), V((nu, piece, f), f32), V((nu, piece, f), f32), V((nu, 2, d, f), bf), V((2, 2, t, f), bf),
-         V((8, 128), f32), DMA((nu, 2)), DMA((nu, 5)), DMA((2,)), DMA((nu,)), DMA((5,))], "fwd_b", 1)(g, ws, norm, x, y)
+        [act, act, sums, both, rows, rows, V((nu, 2, d, f), bf), V((2, 2, t, f), bf), V(TILE, f32),
+         DMA((nu, 2)), DMA((nu, 5)), two, per_unit, DMA((5,))], "fwd_b", 1)(g, ws, norm, x, y)
 
     w_new, sq = call(
         functools.partial(second_backward, dm, scale), 7, [sds((nu, 2, d, f), f32), n_s],
-        acts + [V((2, t, f), bf), V((2, 2, d, f), bf)] + reduce_bufs + [V((nu, d // 4, f), f32), DMA((2, 2)), DMA((4,)), DMA((2,)), DMA((nu,)), DMA((nu,)), DMA((7, nu)), REG,
-         V((13, 8, 128), f32), DMA((nu, 3)), DMA((nu, 5)), DMA((nu,)), DMA((10,)), DMA((10,))], "bwd_b", 2)(x, h1, q, z, v, wc, sq)
+        acts + [V((2, t, f), bf), V((2, 2, d, f), bf)] + reduce_bufs
+        + [V((nu, d // 4, f), f32), rows, loads, four, two, per_unit, per_unit, DMA((7, nu)), REG,
+           norms, DMA((nu, 3)), DMA((nu, 5)), per_unit, tens, tens], "bwd_b", 2)(x, h1, q, z, v, wc, sq)
 
     new_in, new_out, loss = pl.pallas_call(
         functools.partial(finish, scale, f),
         grid=(nl, nf // 4),
-        in_specs=[pl.BlockSpec((4, 2, d, f), lambda i, j: (i * (nf // 4) + j, 0, 0, 0)), pl.BlockSpec((8, 128), lambda i, j: (0, 0))],
+        in_specs=[pl.BlockSpec((4, 2, d, f), lambda i, j: (i * (nf // 4) + j, 0, 0, 0)), pl.BlockSpec(TILE, lambda i, j: (0, 0))],
         out_specs=[pl.BlockSpec((1, d, 4 * f), lambda i, j: (i, 0, j)), pl.BlockSpec((1, 4 * f, d), lambda i, j: (i, j, 0)),
                    pl.BlockSpec((1, 1), lambda i, j: (0, 0), memory_space=pltpu.SMEM)],
         out_shape=[sds((nl, d, ff), f32), sds((nl, ff, d), f32), sds((1, 1), f32)],

time: 629 us -> 629 us (level)
  no operation moved by 1% of the time
where the time goes in v8:
time: 629 us
  Pallas kernels  628 us (100%)
    pallas_call x1, Pallas kernels, local_step(): call(functools.partial(second_backward, dm, scale), 7, [sds((nu, 2, d, f)...  301 us
    pallas_call x1, Pallas kernels, local_step(): call(functools.partial(first_pass, dm, scale), 4, [z_s, v_s, w_s, w_s, w_...  210 us
    pallas_call x1, Pallas kernels, local_step(): call(functools.partial(second_forward, dm, scale, rho), 5, [z_s, v_s, a_s...  92.1 us
    pallas_call x1, Pallas kernels, local_step(): pl.pallas_call(functools.partial(finish, scale, f), grid=(nl, nf // 4), i...  25.3 us

profile of v8, /device:TPU:0, one launch (start us, length us, event | category | flops | bytes accessed | tf_op | source)
XLA Modules:
  0.0 629.2 jit_solution(7978520581460225414)
XLA Ops:
  0.6 210.2 %pass_a.1 = (bf16[24,1568,256]{2,1,0:T(8,128)(2,1)}, bf16[24,2,768,256]{3,2,1,0:T(8,128)(2,1)}, f32[24,48,256]{2,1,0:T(8,128)}, f32[24,48,256]{2,1,0:T(8,128)}, ...) custom-call(bf16[1568,768]{1,0:T(8,128)(2,1)} %bitcast.7, bf16[1568,768]{1,0:T(8,128)(2,1)} %bitcast.10, f32[2,768,3072]{2,1,0:T(8,128)} %wi_hbm.1, ...), custom_call_target="tpu_custom_call" | custom-call | tf_op jit(solution)/shard_map/pass_a/pallas_call | solution.py:848
  210.8 92.1 %fwd_b.1 = (bf16[24,1568,256]{2,1,0:T(8,128)(2,1)}, bf16[24,2,768,256]{3,2,1,0:T(8,128)(2,1)}, bf16[1568,768]{1,0:T(8,128)(2,1)}, bf16[1568,768]{1,0:T(8,128)(2,1)}, f32[8,128]{1,0:T(8,128)}) custom-call(f32[24,48,256]{2,1,0:T(8,128)} %get-tuple-element.17.gs_hbm, f32[24,48,256]{2,1,0:T(8,128)} %get-tuple-element.18.ws_hbm, ...), custom_call_target="tpu_custom_call" | custom-call | tf_op jit(solution)/shard_map/fwd_b/pallas_call | solution.py:854
  303.0 300.9 %bwd_b.1 = (f32[24,2,768,256]{3,2,1,0:T(8,128)}, f32[8,128]{1,0:T(8,128)}) custom-call(bf16[1568,768]{1,0:T(8,128)(2,1)} %bitcast.9, bf16[1568,768]{1,0:T(8,128)(2,1)} %get-tuple-element.20.h_hbm, bf16[1568,768]{1,0:T(8,128)(2,1)} %get-tuple-element.21.q_hbm, bf16[24,1568,256]{2,1,0:T(8,128)(2,1)} %get-tuple-element.22.z_hbm, ...), custom_call_target="tpu_custom_call" | custom-call | tf_op jit(solution)/shard_map/bwd_b/pallas_call | solution.py:859
  603.9 25.3 %finish.1 = (f32[2,768,3072]{2,1,0:T(8,128)}, f32[2,3072,768]{2,1,0:T(8,128)}, f32[1,1]{1,0:T(1,128)}) custom-call(f32[24,2,768,256]{3,2,1,0:T(8,128)} %get-tuple-element.26.w_ref, f32[8,128]{1,0:T(8,128)} %get-tuple-element.27.sq_ref), custom_call_target="tpu_custom_call" | custom-call | tf_op jit(solution)/shard_map/finish/pallas_call | solution.py:865

commit v9 on v8

--- a/solution.py
+++ b/solution.py
@@ -18,10 +18,11 @@
 GELU_K = 0.044715
 VMEM_CAP = 67043328
 TILE = (8, 128)
+FINISH_TILES = 6
 CORE_SLOTS = 9
-LAG_A = (0, 1, 4, 5, 7)
-LAG_B = (0, 1, 2, 3, 4, 4, 5, 7, 8, 9, 12)
-VG_LAG = (0, 2, 3, 5, 7, 9)
+LAG_A = (0, 1, 3, 5, 7)
+LAG_B = (0, 2, 3, 4, 5, 6, 7, 8, 9, 11, 12)
+VG_LAG = (0, 1, 2, 4, 6, 8)
 
 
 steps = functools.partial(pl.loop, 0)
@@ -862,11 +863,12 @@
         + [V((nu, d // 4, f), f32), rows, loads, four, two, per_unit, per_unit, DMA((7, nu)), REG,
            norms, DMA((nu, 3)), DMA((nu, 5)), per_unit, tens, tens], "bwd_b", 2)(x, h1, q, z, v, wc, sq)
 
+    per_step = min(FINISH_TILES, nf)
     new_in, new_out, loss = pl.pallas_call(
         functools.partial(finish, scale, f),
-        grid=(nl, nf // 4),
-        in_specs=[pl.BlockSpec((4, 2, d, f), lambda i, j: (i * (nf // 4) + j, 0, 0, 0)), pl.BlockSpec(TILE, lambda i, j: (0, 0))],
-        out_specs=[pl.BlockSpec((1, d, 4 * f), lambda i, j: (i, 0, j)), pl.BlockSpec((1, 4 * f, d), lambda i, j: (i, j, 0)),
+        grid=(nl, nf // per_step),
+        in_specs=[pl.BlockSpec((per_step, 2, d, f), lambda i, j: (i * (nf // per_step) + j, 0, 0, 0)), pl.BlockSpec(TILE, lambda i, j: (0, 0))],
+        out_specs=[pl.BlockSpec((1, d, per_step * f), lambda i, j: (i, 0, j)), pl.BlockSpec((1, per_step * f, d), lambda i, j: (i, j, 0)),
                    pl.BlockSpec((1, 1), lambda i, j: (0, 0), memory_space=pltpu.SMEM)],
         out_shape=[sds((nl, d, ff), f32), sds((nl, ff, d), f32), sds((1, 1), f32)],
         compiler_params=pltpu.CompilerParams(vmem_limit_bytes=VMEM_CAP),

time: 629 us -> 622 us (0.989)
  Pallas kernels: 628 us -> 621 us
    pallas_call x1, Pallas kernels: 301 us -> 292 us  [local_step(): call(functools.partial(second_backward, dm, scale), 7, [sds((nu, 2, d, f)...]
where the time goes in v9:
time: 622 us; the launch traced here: 621 us
  Pallas kernels  621 us (100%)
    pallas_call x1, Pallas kernels, local_step(): call(functools.partial(second_backward, dm, scale), 7, [sds((nu, 2, d, f)...  292 us
    pallas_call x1, Pallas kernels, local_step(): call(functools.partial(first_pass, dm, scale), 4, [z_s, v_s, w_s, w_s, w_...  210 us
    pallas_call x1, Pallas kernels, local_step(): call(functools.partial(second_forward, dm, scale, rho), 5, [z_s, v_s, a_s...  94.8 us
    pallas_call x1, Pallas kernels, local_step(): pl.pallas_call(functools.partial(finish, scale, f), grid=(nl, nf // per_s...  23.9 us

profile of v9, /device:TPU:0, one launch (start us, length us, event | category | flops | bytes accessed | tf_op | source)
XLA Modules:
  0.0 621.4 jit_solution(8738451344949932649)
XLA Ops:
  0.6 209.5 %pass_a.1 = (bf16[24,1568,256]{2,1,0:T(8,128)(2,1)}, bf16[24,2,768,256]{3,2,1,0:T(8,128)(2,1)}, f32[24,48,256]{2,1,0:T(8,128)}, f32[24,48,256]{2,1,0:T(8,128)}, ...) custom-call(bf16[1568,768]{1,0:T(8,128)(2,1)} %bitcast.7, bf16[1568,768]{1,0:T(8,128)(2,1)} %bitcast.10, f32[2,768,3072]{2,1,0:T(8,128)} %wi_hbm.1, ...), custom_call_target="tpu_custom_call" | custom-call | tf_op jit(solution)/shard_map/pass_a/pallas_call | solution.py:849
  210.1 94.8 %fwd_b.1 = (bf16[24,1568,256]{2,1,0:T(8,128)(2,1)}, bf16[24,2,768,256]{3,2,1,0:T(8,128)(2,1)}, bf16[1568,768]{1,0:T(8,128)(2,1)}, bf16[1568,768]{1,0:T(8,128)(2,1)}, f32[8,128]{1,0:T(8,128)}) custom-call(f32[24,48,256]{2,1,0:T(8,128)} %get-tuple-element.17.gs_hbm, f32[24,48,256]{2,1,0:T(8,128)} %get-tuple-element.18.ws_hbm, ...), custom_call_target="tpu_custom_call" | custom-call | tf_op jit(solution)/shard_map/fwd_b/pallas_call | solution.py:855
  305.0 292.4 %bwd_b.1 = (f32[24,2,768,256]{3,2,1,0:T(8,128)}, f32[8,128]{1,0:T(8,128)}) custom-call(bf16[1568,768]{1,0:T(8,128)(2,1)} %bitcast.9, bf16[1568,768]{1,0:T(8,128)(2,1)} %get-tuple-element.20.h_hbm, bf16[1568,768]{1,0:T(8,128)(2,1)} %get-tuple-element.21.q_hbm, bf16[24,1568,256]{2,1,0:T(8,128)(2,1)} %get-tuple-element.22.z_hbm, ...), custom_call_target="tpu_custom_call" | custom-call | tf_op jit(solution)/shard_map/bwd_b/pallas_call | solution.py:860
  597.4 23.9 %finish.1 = (f32[2,768,3072]{2,1,0:T(8,128)}, f32[2,3072,768]{2,1,0:T(8,128)}, f32[1,1]{1,0:T(1,128)}) custom-call(f32[24,2,768,256]{3,2,1,0:T(8,128)} %get-tuple-element.26.w_ref, f32[8,128]{1,0:T(8,128)} %get-tuple-element.27.sq_ref), custom_call_target="tpu_custom_call" | custom-call | tf_op jit(solution)/shard_map/finish/pallas_call | solution.py:867

commit v10 on v9

--- a/solution.py
+++ b/solution.py
@@ -21,8 +21,8 @@
 FINISH_TILES = 6
 CORE_SLOTS = 9
 LAG_A = (0, 1, 3, 5, 7)
-LAG_B = (0, 2, 3, 4, 5, 6, 7, 8, 9, 11, 12)
-VG_LAG = (0, 1, 2, 4, 6, 8)
+LAG_B = (0, 2, 3, 4, 5, 6, 8, 9, 10, 12, 14)
+VG_LAG = (0, 2, 4, 7, 9, 11)
 
 
 steps = functools.partial(pl.loop, 0)

time: 622 us -> 610 us (0.981)
  Pallas kernels: 621 us -> 610 us
    pallas_call x1, Pallas kernels: 94.8 us -> 86.2 us  [local_step(): call(functools.partial(second_forward, dm, scale, rho), 5, [z_s, v_s, a_s...]
where the time goes in v10:
time: 610 us
  Pallas kernels  610 us (100%)
    pallas_call x1, Pallas kernels, local_step(): call(functools.partial(second_backward, dm, scale), 7, [sds((nu, 2, d, f)...  290 us
    pallas_call x1, Pallas kernels, local_step(): call(functools.partial(first_pass, dm, scale), 4, [z_s, v_s, w_s, w_s, w_...  210 us
    pallas_call x1, Pallas kernels, local_step(): call(functools.partial(second_forward, dm, scale, rho), 5, [z_s, v_s, a_s...  86.2 us
    pallas_call x1, Pallas kernels, local_step(): pl.pallas_call(functools.partial(finish, scale, f), grid=(nl, nf // per_s...  23.9 us

profile of v10, /device:TPU:0, one launch (start us, length us, event | category | flops | bytes accessed | tf_op | source)
XLA Modules:
  0.0 610.3 jit_solution(13622221817722474973)
XLA Ops:
  0.6 209.5 %pass_a.1 = (bf16[24,1568,256]{2,1,0:T(8,128)(2,1)}, bf16[24,2,768,256]{3,2,1,0:T(8,128)(2,1)}, f32[24,48,256]{2,1,0:T(8,128)}, f32[24,48,256]{2,1,0:T(8,128)}, ...) custom-call(bf16[1568,768]{1,0:T(8,128)(2,1)} %bitcast.7, bf16[1568,768]{1,0:T(8,128)(2,1)} %bitcast.10, f32[2,768,3072]{2,1,0:T(8,128)} %wi_hbm.1, ...), custom_call_target="tpu_custom_call" | custom-call | tf_op jit(solution)/shard_map/pass_a/pallas_call | solution.py:849
  210.1 86.2 %fwd_b.1 = (bf16[24,1568,256]{2,1,0:T(8,128)(2,1)}, bf16[24,2,768,256]{3,2,1,0:T(8,128)(2,1)}, bf16[1568,768]{1,0:T(8,128)(2,1)}, bf16[1568,768]{1,0:T(8,128)(2,1)}, f32[8,128]{1,0:T(8,128)}) custom-call(f32[24,48,256]{2,1,0:T(8,128)} %get-tuple-element.17.gs_hbm, f32[24,48,256]{2,1,0:T(8,128)} %get-tuple-element.18.ws_hbm, ...), custom_call_target="tpu_custom_call" | custom-call | tf_op jit(solution)/shard_map/fwd_b/pallas_call | solution.py:855
  296.3 290.0 %bwd_b.1 = (f32[24,2,768,256]{3,2,1,0:T(8,128)}, f32[8,128]{1,0:T(8,128)}) custom-call(bf16[1568,768]{1,0:T(8,128)(2,1)} %bitcast.9, bf16[1568,768]{1,0:T(8,128)(2,1)} %get-tuple-element.20.h_hbm, bf16[1568,768]{1,0:T(8,128)(2,1)} %get-tuple-element.21.q_hbm, bf16[24,1568,256]{2,1,0:T(8,128)(2,1)} %get-tuple-element.22.z_hbm, ...), custom_call_target="tpu_custom_call" | custom-call | tf_op jit(solution)/shard_map/bwd_b/pallas_call | solution.py:860
  586.4 23.9 %finish.1 = (f32[2,768,3072]{2,1,0:T(8,128)}, f32[2,3072,768]{2,1,0:T(8,128)}, f32[1,1]{1,0:T(1,128)}) custom-call(f32[24,2,768,256]{3,2,1,0:T(8,128)} %get-tuple-element.26.w_ref, f32[8,128]{1,0:T(8,128)} %get-tuple-element.27.sq_ref), custom_call_target="tpu_custom_call" | custom-call | tf_op jit(solution)/shard_map/finish/pallas_call | solution.py:867

commit v11 on v10

--- a/solution.py
+++ b/solution.py
@@ -20,9 +20,9 @@
 TILE = (8, 128)
 FINISH_TILES = 6
 CORE_SLOTS = 9
-LAG_A = (0, 1, 3, 5, 7)
-LAG_B = (0, 2, 3, 4, 5, 6, 8, 9, 10, 12, 14)
-VG_LAG = (0, 2, 4, 7, 9, 11)
+LAG_A = (0, 1, 2, 3, 5)
+LAG_B = (0, 2, 3, 4, 5, 6, 8, 9, 10, 14, 16)
+VG_LAG = (0, 4, 6, 11, 14, 16)
 
 
 steps = functools.partial(pl.loop, 0)

time: 610 us -> 607 us (level)
  no operation moved by 1% of the time
where the time goes in v11:
time: 607 us
  Pallas kernels  606 us (100%)
    pallas_call x1, Pallas kernels, local_step(): call(functools.partial(second_backward, dm, scale), 7, [sds((nu, 2, d, f)...  290 us
    pallas_call x1, Pallas kernels, local_step(): call(functools.partial(first_pass, dm, scale), 4, [z_s, v_s, w_s, w_s, w_...  207 us
    pallas_call x1, Pallas kernels, local_step(): call(functools.partial(second_forward, dm, scale, rho), 5, [z_s, v_s, a_s...  85 us
    pallas_call x1, Pallas kernels, local_step(): pl.pallas_call(functools.partial(finish, scale, f), grid=(nl, nf // per_s...  23.9 us

profile of v11, /device:TPU:0, one launch (start us, length us, event | category | flops | bytes accessed | tf_op | source)
XLA Modules:
  0.0 606.7 jit_solution(2058180622811287516)
XLA Ops:
  0.6 206.9 %pass_a.1 = (bf16[24,1568,256]{2,1,0:T(8,128)(2,1)}, bf16[24,2,768,256]{3,2,1,0:T(8,128)(2,1)}, f32[24,48,256]{2,1,0:T(8,128)}, f32[24,48,256]{2,1,0:T(8,128)}, ...) custom-call(bf16[1568,768]{1,0:T(8,128)(2,1)} %bitcast.7, bf16[1568,768]{1,0:T(8,128)(2,1)} %bitcast.10, f32[2,768,3072]{2,1,0:T(8,128)} %wi_hbm.1, ...), custom_call_target="tpu_custom_call" | custom-call | tf_op jit(solution)/shard_map/pass_a/pallas_call | solution.py:849
  207.6 85.0 %fwd_b.1 = (bf16[24,1568,256]{2,1,0:T(8,128)(2,1)}, bf16[24,2,768,256]{3,2,1,0:T(8,128)(2,1)}, bf16[1568,768]{1,0:T(8,128)(2,1)}, bf16[1568,768]{1,0:T(8,128)(2,1)}, f32[8,128]{1,0:T(8,128)}) custom-call(f32[24,48,256]{2,1,0:T(8,128)} %get-tuple-element.17.gs_hbm, f32[24,48,256]{2,1,0:T(8,128)} %get-tuple-element.18.ws_hbm, ...), custom_call_target="tpu_custom_call" | custom-call | tf_op jit(solution)/shard_map/fwd_b/pallas_call | solution.py:855
  292.6 290.2 %bwd_b.1 = (f32[24,2,768,256]{3,2,1,0:T(8,128)}, f32[8,128]{1,0:T(8,128)}) custom-call(bf16[1568,768]{1,0:T(8,128)(2,1)} %bitcast.9, bf16[1568,768]{1,0:T(8,128)(2,1)} %get-tuple-element.20.h_hbm, bf16[1568,768]{1,0:T(8,128)(2,1)} %get-tuple-element.21.q_hbm, bf16[24,1568,256]{2,1,0:T(8,128)(2,1)} %get-tuple-element.22.z_hbm, ...), custom_call_target="tpu_custom_call" | custom-call | tf_op jit(solution)/shard_map/bwd_b/pallas_call | solution.py:860
  582.8 23.9 %finish.1 = (f32[2,768,3072]{2,1,0:T(8,128)}, f32[2,3072,768]{2,1,0:T(8,128)}, f32[1,1]{1,0:T(1,128)}) custom-call(f32[24,2,768,256]{3,2,1,0:T(8,128)} %get-tuple-element.26.w_ref, f32[8,128]{1,0:T(8,128)} %get-tuple-element.27.sq_ref), custom_call_target="tpu_custom_call" | custom-call | tf_op jit(solution)/shard_map/finish/pallas_call | solution.py:867

commit v12 on v11

--- a/solution.py
+++ b/solution.py
@@ -123,15 +123,20 @@
     return out
 
 
-def exchange_sum(buf, first, peers, send_sem, recv_sem, sem0):
+def exchange(buf, first, peers, send_sem, recv_sem, sem0):
     copies = [remote(buf.at[first], buf.at[first + 1 + i], send_sem.at[sem0 + i], recv_sem.at[sem0 + i], peer) for i, peer in enumerate(peers)]
-    for cp in copies:
-        cp.start()
-    total = buf[first]
-    for i, cp in enumerate(copies):
-        cp.wait()
-        total = total + buf[first + 1 + i]
-    buf[first + len(peers) + 1] = total
+
+    def start():
+        for cp in copies:
+            cp.start()
+
+    def close():
+        total = buf[first]
+        for i, cp in enumerate(copies):
+            cp.wait()
+            total = total + buf[first + 1 + i]
+        buf[first + len(peers) + 1] = total
+    return start, close
 
 
 def gather_hops(bits, peers, unit, d, full, piece_src=None):
@@ -339,8 +344,9 @@
                    csend_sem, core_sem, credit, tiles, x_again.wait, LAG_A[0], start, events)
     g_cp = local(ws, g_out, io_sem.at[0])
     g_cp.start()
-    exchange_sum(nb, 0, near, nsend_sem, nrecv_sem, 0)
-    exchange_sum(nb, 8, far, nsend_sem, nrecv_sem, 7)
+    for start, close in (exchange(nb, 0, near, nsend_sem, nrecv_sem, 0), exchange(nb, 8, far, nsend_sem, nrecv_sem, 7)):
+        start()
+        close()
     n_cp = local(nb.at[12], n_out, io_sem.at[1])
     n_cp.start()
     wc_cp.wait()
@@ -427,11 +433,10 @@
             def _():
                 fwd_close(h, acc, t)
                 fwd_seed(h, acc, t)
-                out = local(h, h_out, io_sem.at[0])
-                out.start()
-                out.wait()
+                local(h, h_out, io_sem.at[0]).start()
 
     ins[3].wait()
+    local(h, h_out, io_sem.at[0]).wait()
     loss_close(h, yb, acc, t, d, nb)
     out = local(h, q_out, io_sem.at[0])
     sq = local(nb, sq_out, io_sem.at[1])
@@ -756,10 +761,7 @@
     h_in = local(h_hbm, tmp, io_sem.at[1])
     ws_in = local(ws_hbm, gs, io_sem.at[2])
     sq_in = local(sq_hbm, nb.at[0], io_sem.at[3])
-    q_in.start()
-    for cp in tiles(0, 0):
-        cp.start()
-    for cp in (h_in, ws_in, sq_in):
+    for cp in (q_in, h_in, *tiles(0, 0), ws_in, sq_in):
         cp.start()
     q_in.wait()
     fwd_seed(q, acc, t)
@@ -775,14 +777,18 @@
     def on_total(u, total):
         gs[u] = gs[u] - LEARN_RATE * (total * scale)
 
+    start_near, close_near = exchange(nb, 0, near, nsend_sem, nrecv_sem, 0)
+    start_far, close_far = exchange(nb, 8, far, nsend_sem, nrecv_sem, 7)
+
+    def start_far_after():
+        close_near()
+        start_far()
+
     def sums(j):
-        @pl.when(j == 1)
-        def _():
-            exchange_sum(nb, 0, near, nsend_sem, nrecv_sem, 0)
-
-        @pl.when(j == 2)
-        def _():
-            exchange_sum(nb, 8, far, nsend_sem, nrecv_sem, 7)
+        for at, step in ((1, start_near), (nf // 2, start_far_after), (nf, close_far)):
+            @pl.when(j == at)
+            def _():
+                step()
 
     start, events, finish_unit = chain(dm, bits, peers, cbuf, (r1, r2, r3, r4, r5), gs, w_out, send_sem, recv_sem, credit,
                                        ag_send, ag_recv, ag_loc, LAG_B[1:], on_total)

time: 607 us -> 593 us (0.977)
  Pallas kernels: 606 us -> 592 us
    pallas_call x1, Pallas kernels: 290 us -> 276 us  [local_step(): call(functools.partial(second_backward, dm, scale), 7, [sds((nu, 2, d, f)...]
where the time goes in v12:
time: 593 us
  Pallas kernels  592 us (100%)
    pallas_call x1, Pallas kernels, local_step(): call(functools.partial(second_backward, dm, scale), 7, [sds((nu, 2, d, f)...  276 us
    pallas_call x1, Pallas kernels, local_step(): call(functools.partial(first_pass, dm, scale), 4, [z_s, v_s, w_s, w_s, w_...  207 us
    pallas_call x1, Pallas kernels, local_step(): call(functools.partial(second_forward, dm, scale, rho), 5, [z_s, v_s, a_s...  85 us
    pallas_call x1, Pallas kernels, local_step(): pl.pallas_call(functools.partial(finish, scale, f), grid=(nl, nf // per_s...  23.9 us

profile of v12, /device:TPU:0, one launch (start us, length us, event | category | flops | bytes accessed | tf_op | source)
XLA Modules:
  0.0 592.7 jit_solution(13067621283383269540)
XLA Ops:
  0.6 206.9 %pass_a.1 = (bf16[24,1568,256]{2,1,0:T(8,128)(2,1)}, bf16[24,2,768,256]{3,2,1,0:T(8,128)(2,1)}, f32[24,48,256]{2,1,0:T(8,128)}, f32[24,48,256]{2,1,0:T(8,128)}, ...) custom-call(bf16[1568,768]{1,0:T(8,128)(2,1)} %bitcast.7, bf16[1568,768]{1,0:T(8,128)(2,1)} %bitcast.10, f32[2,768,3072]{2,1,0:T(8,128)} %wi_hbm.1, ...), custom_call_target="tpu_custom_call" | custom-call | tf_op jit(solution)/shard_map/pass_a/pallas_call | solution.py:855
  207.6 85.0 %fwd_b.1 = (bf16[24,1568,256]{2,1,0:T(8,128)(2,1)}, bf16[24,2,768,256]{3,2,1,0:T(8,128)(2,1)}, bf16[1568,768]{1,0:T(8,128)(2,1)}, bf16[1568,768]{1,0:T(8,128)(2,1)}, f32[8,128]{1,0:T(8,128)}) custom-call(f32[24,48,256]{2,1,0:T(8,128)} %get-tuple-element.17.gs_hbm, f32[24,48,256]{2,1,0:T(8,128)} %get-tuple-element.18.ws_hbm, ...), custom_call_target="tpu_custom_call" | custom-call | tf_op jit(solution)/shard_map/fwd_b/pallas_call | solution.py:861
  292.6 276.2 %bwd_b.1 = (f32[24,2,768,256]{3,2,1,0:T(8,128)}, f32[8,128]{1,0:T(8,128)}) custom-call(bf16[1568,768]{1,0:T(8,128)(2,1)} %bitcast.9, bf16[1568,768]{1,0:T(8,128)(2,1)} %get-tuple-element.20.h_hbm, bf16[1568,768]{1,0:T(8,128)(2,1)} %get-tuple-element.21.q_hbm, bf16[24,1568,256]{2,1,0:T(8,128)(2,1)} %get-tuple-element.22.z_hbm, ...), custom_call_target="tpu_custom_call" | custom-call | tf_op jit(solution)/shard_map/bwd_b/pallas_call | solution.py:866
  568.8 23.9 %finish.1 = (f32[2,768,3072]{2,1,0:T(8,128)}, f32[2,3072,768]{2,1,0:T(8,128)}, f32[1,1]{1,0:T(1,128)}) custom-call(f32[24,2,768,256]{3,2,1,0:T(8,128)} %get-tuple-element.26.w_ref, f32[8,128]{1,0:T(8,128)} %get-tuple-element.27.sq_ref), custom_call_target="tpu_custom_call" | custom-call | tf_op jit(solution)/shard_map/finish/pallas_call | solution.py:873

commit v13 on v12

--- a/solution.py
+++ b/solution.py
@@ -20,8 +20,8 @@
 TILE = (8, 128)
 FINISH_TILES = 6
 CORE_SLOTS = 9
-LAG_A = (0, 1, 2, 3, 5)
-LAG_B = (0, 2, 3, 4, 5, 6, 8, 9, 10, 14, 16)
+LAG_A = (0, 1, 3, 5, 7)
+LAG_B = (0, 2, 4, 5, 6, 7, 9, 10, 11, 14, 16)
 VG_LAG = (0, 4, 6, 11, 14, 16)
 
 
@@ -512,7 +512,7 @@
                 for lo, n in halves(t):
                     acc[lo:lo + n, :] += dot(eb[0, lo:lo + n, :], vb[slot, 0], NT)
 
-        for lag, event in ((core_lag, core_stage), *events):
+        for lag, event in (*reversed(events), (core_lag, core_stage)):
             j = it - lag
 
             @pl.when((j >= 0) & (j < nu))

time: 593 us -> 596 us (level)
  no operation moved by 1% of the time
where the time goes in v13:
time: 596 us
  Pallas kernels  595 us (100%)
    pallas_call x1, Pallas kernels, local_step(): call(functools.partial(second_backward, dm, scale), 7, [sds((nu, 2, d, f)...  277 us
    pallas_call x1, Pallas kernels, local_step(): call(functools.partial(first_pass, dm, scale), 4, [z_s, v_s, w_s, w_s, w_...  209 us
    pallas_call x1, Pallas kernels, local_step(): call(functools.partial(second_forward, dm, scale, rho), 5, [z_s, v_s, a_s...  85.2 us
    pallas_call x1, Pallas kernels, local_step(): pl.pallas_call(functools.partial(finish, scale, f), grid=(nl, nf // per_s...  23.9 us

profile of v13, /device:TPU:0, one launch (start us, length us, event | category | flops | bytes accessed | tf_op | source)
XLA Modules:
  0.0 595.9 jit_solution(13850434295791132736)
XLA Ops:
  0.6 208.8 %pass_a.1 = (bf16[24,1568,256]{2,1,0:T(8,128)(2,1)}, bf16[24,2,768,256]{3,2,1,0:T(8,128)(2,1)}, f32[24,48,256]{2,1,0:T(8,128)}, f32[24,48,256]{2,1,0:T(8,128)}, ...) custom-call(bf16[1568,768]{1,0:T(8,128)(2,1)} %bitcast.7, bf16[1568,768]{1,0:T(8,128)(2,1)} %bitcast.10, f32[2,768,3072]{2,1,0:T(8,128)} %wi_hbm.1, ...), custom_call_target="tpu_custom_call" | custom-call | tf_op jit(solution)/shard_map/pass_a/pallas_call | solution.py:855
  209.4 85.2 %fwd_b.1 = (bf16[24,1568,256]{2,1,0:T(8,128)(2,1)}, bf16[24,2,768,256]{3,2,1,0:T(8,128)(2,1)}, bf16[1568,768]{1,0:T(8,128)(2,1)}, bf16[1568,768]{1,0:T(8,128)(2,1)}, f32[8,128]{1,0:T(8,128)}) custom-call(f32[24,48,256]{2,1,0:T(8,128)} %get-tuple-element.17.gs_hbm, f32[24,48,256]{2,1,0:T(8,128)} %get-tuple-element.18.ws_hbm, ...), custom_call_target="tpu_custom_call" | custom-call | tf_op jit(solution)/shard_map/fwd_b/pallas_call | solution.py:861
  294.6 277.3 %bwd_b.1 = (f32[24,2,768,256]{3,2,1,0:T(8,128)}, f32[8,128]{1,0:T(8,128)}) custom-call(bf16[1568,768]{1,0:T(8,128)(2,1)} %bitcast.9, bf16[1568,768]{1,0:T(8,128)(2,1)} %get-tuple-element.20.h_hbm, bf16[1568,768]{1,0:T(8,128)(2,1)} %get-tuple-element.21.q_hbm, bf16[24,1568,256]{2,1,0:T(8,128)(2,1)} %get-tuple-element.22.z_hbm, ...), custom_call_target="tpu_custom_call" | custom-call | tf_op jit(solution)/shard_map/bwd_b/pallas_call | solution.py:866
  571.9 23.9 %finish.1 = (f32[2,768,3072]{2,1,0:T(8,128)}, f32[2,3072,768]{2,1,0:T(8,128)}, f32[1,1]{1,0:T(1,128)}) custom-call(f32[24,2,768,256]{3,2,1,0:T(8,128)} %get-tuple-element.26.w_ref, f32[8,128]{1,0:T(8,128)} %get-tuple-element.27.sq_ref), custom_call_target="tpu_custom_call" | custom-call | tf_op jit(solution)/shard_map/finish/pallas_call | solution.py:873
